TPU v7x, 128 devices: a whole 4x4x4 slice. The times are simulated.
128 devices in a mesh: seq: 32 (over y_lo, z, x), head: 4 (over y_hi, core).
Axes of the slice: x: 4, y: 4 (y_hi: 2, y_lo: 2; y = y_hi * 2 + y_lo), z: 4, core: 2. Of those that a mesh axis runs over, the one named last changes fastest.
Arguments:
- queries: bfloat16 [4096, 3072], P('seq', 'head'), may hold values from -8 to 8
- latents: bfloat16 [4096, 576], P('seq'), may hold values from -8 to 8
- key_up: bfloat16 [512, 2048], P(None, 'head'), may hold values from -0.25 to 0.25
- value_up: bfloat16 [512, 2048], P(None, 'head'), may hold values from -0.25 to 0.25
- out_grad: bfloat16 [4096, 2048], P('seq', 'head'), may hold values from -48 to 48
- positions: int32 [4096], P('seq'), may hold values from 0 to 4095, as said below
Outputs:
- query_grad: bfloat16 [4096, 3072], P('seq', 'head')
- latent_grad: float32 [4096, 576], P('seq')
- key_up_grad: float32 [512, 2048], P(None, 'head')
- value_up_grad: float32 [512, 2048], P(None, 'head')
Inputs may be any that keep to these rules, and one draw needn't show every extreme that they name: Every position from 0 to 4095 occurs once; positions come in stripes of 128 consecutive positions in ascending order, each stripe whole within the rows of one device.
All inputs are finite; a program needn't handle non-finite values.
Results may differ from a plain program's by a relative error of at most 0.0084.
Values may be sent and summed in bfloat16 or wider, within the bound.
No kernel may reach another device: no remote copies, remote signals or barrier semaphores. Data moves between devices by JAX's collectives and lax.ppermute only.
A program may use at most 64 MiB of HBM per device.

v0:
```python
import functools
import math

import jax
import jax.numpy as jnp
from jax import lax
from jax.experimental import pallas as pl
from jax.experimental.pallas import tpu as pltpu
from jax.sharding import PartitionSpec as P


BF = jnp.bfloat16
F32 = jnp.float32
D_LAT = 512
D_ROPE = 64
D_NOPE = 128
ROWS = 128
SCALE = 1.0 / math.sqrt(D_NOPE + D_ROPE)
SCALE2 = SCALE * math.log2(math.e)
NEG = -1e30
QP = 336
LP = 592
NQ = 2048
NK = 1024
TQ = 256


def place(y, z, x):
    return (y % 2) * 16 + (z % 4) * 4 + x % 4


def along(value, dy=0, dz=0, dx=0):
    pairs = [
        (place(y, z, x), place(y + dy, z + dz, x + dx))
        for y in range(2)
        for z in range(4)
        for x in range(4)
    ]
    return lax.ppermute(value, "seq", pairs)


def by_core(value, dx):
    pairs = []
    for y in range(2):
        for z in range(4):
            for x in range(4):
                for h in range(4):
                    step = dx if h % 2 == 0 else -dx
                    pairs.append((place(y, z, x) * 4 + h, place(y, z, x + step) * 4 + h))
    return lax.ppermute(value, ("seq", "head"), pairs)


def to_core(value):
    return lax.ppermute(value, "head", [(0, 1), (1, 0), (2, 3), (3, 2)])


YZ_GROUPS = [[4 * k + i for k in range(8)] for i in range(4)]
VM, SM, HB = pltpu.VMEM, pltpu.SMEM, pltpu.HBM


def call(kernel, outs, args, scratch=(), flops=0, grant=6):
    args = [arg if isinstance(arg, tuple) else (arg, VM) for arg in args]
    args = [(pltpu.with_memory_space_constraint(a, HB) if m is HB else a, m) for a, m in args]
    return pl.pallas_call(
        kernel,
        out_shape=[HB(o[0], o[1]) if o[2:] == (HB,) else jax.ShapeDtypeStruct(o[0], o[1]) for o in outs],
        in_specs=[pl.BlockSpec(memory_space=space) for _, space in args],
        out_specs=[pl.BlockSpec(memory_space=o[2] if len(o) > 2 else VM) for o in outs],
        scratch_shapes=list(scratch),
        cost_estimate=pl.CostEstimate(flops=max(flops, 1), bytes_accessed=1 << 20, transcendentals=0),
        compiler_params=pltpu.CompilerParams(vmem_limit_bytes=grant << 20),
    )(*[array for array, _ in args])


def dense_rope(block):
    return jnp.concatenate([block[0:64], block[64:128]], axis=1)


def wide_rope(block):
    return jnp.concatenate([block[:, 0:64], block[:, 64:128]], axis=0)


def pack(pos_hbm, x, q_hbm, g_hbm, lat_hbm, own, to1, to2, to3, lat, q, g, heads, pos, sems):
    copies = [
        pltpu.make_async_copy(q_hbm, q, sems.at[0]),
        pltpu.make_async_copy(g_hbm, g, sems.at[1]),
        pltpu.make_async_copy(lat_hbm, lat.at[0:576], sems.at[2]),
        pltpu.make_async_copy(pos_hbm, pos, sems.at[3]),
    ]
    for copy in copies:
        copy.start()
    copies.pop().wait()
    tag = jnp.full((16, 128), (pos[0] >> 7).astype(F32), F32).astype(BF)
    lat[576:592] = tag
    for copy in copies:
        copy.wait()
    for h in range(4):
        heads[h, 0:128] = q[:, 192 * h : 192 * h + 128]
        heads[h, 128:256] = g[:, 128 * h : 128 * h + 128]
        heads[h, 256:320] = dense_rope(q[:, 192 * h + 128 : 192 * h + 192])
        heads[h, 320:336] = tag
    for r, out in enumerate((own, to1, to2, to3)):
        out[...] = heads[(x[0] + r) & 3]


def masked_scores(raw, qtags, ktags, late):
    rows = []
    for kb in range(NK // 128):
        cols = []
        for qb in range(TQ // 128):
            part = raw[128 * kb : 128 * kb + 128, 128 * qb : 128 * qb + 128]
            seen = late <= (qtags[qb] - ktags[kb]) * 128.0
            cols.append(jnp.where(seen, part * SCALE2, NEG))
        rows.append(jnp.concatenate(cols, axis=1))
    return jnp.concatenate(rows, axis=0)


def lateness():
    shape = (128, 128)
    return (lax.broadcasted_iota(jnp.int32, shape, 0) - lax.broadcasted_iota(jnp.int32, shape, 1)).astype(F32)


NT = (((1,), (1,)), ((), ()))
NN = (((1,), (0,)), ((), ()))


def mm(a, b, dims):
    return lax.dot_general(a, b, dims, preferred_element_type=F32)


def take_queries(blocks, qp, do, qtag):
    zeros = jnp.zeros((128, 64), BF)
    for n, block in enumerate(blocks):
        at = 128 * n
        qp[at : at + 128, 0:128] = block[0:128]
        qp[at : at + 128, 128:256] = jnp.concatenate([wide_rope(block[256:320]), zeros], axis=1)
        do[at : at + 128] = block[128:256]
        qtag[0:8, at : at + 128] = block[320:336].astype(F32)[0:8]


def statistics(rows, qp, do, qtag, kp, v, ktag, stats, first):
    late = lateness()
    ktags = [ktag[8 * n : 8 * n + 1] for n in range(8)]

    def turn(i, carry):
        at = pl.multiple_of(i * TQ, TQ)
        to = pl.multiple_of(first + i * TQ, TQ)
        raw = mm(kp[...], qp[pl.ds(at, TQ)], NT)
        qt = qtag[0:1, pl.ds(at, TQ)]
        s = masked_scores(raw, [qt[:, 0:128], qt[:, 128:256]], ktags, late)
        top = jnp.max(s, axis=0, keepdims=True)
        p = jnp.exp2(s - top)
        dp = mm(v[...], do[pl.ds(at, TQ)], NT)
        stats[0:1, pl.ds(to, TQ)] = top
        stats[1:2, pl.ds(to, TQ)] = jnp.sum(p, axis=0, keepdims=True)
        stats[2:3, pl.ds(to, TQ)] = jnp.sum(p * dp, axis=0, keepdims=True)
        return carry

    lax.fori_loop(0, rows // TQ, turn, 0)


def copied(pairs, sems):
    copies = [pltpu.make_async_copy(src, dst, sems.at[n]) for n, (src, dst) in enumerate(pairs)]
    for copy in copies:
        copy.start()
    return copies


def forward_near(
    core, q0, qa, qb, pair, lp, lpe, lh, lhe, ku, vu,
    qp_hbm, do_hbm, compt_hbm, kpt_hbm, qtag_hbm, kp_hbm, v_hbm, ktag_hbm, kp, v, ktag, stats,
    qp, do, compt, kpt, qtag, sems, late_sems,
):
    take_queries([ref[i] for ref in (q0, qb, qa) for i in range(4)], qp, do, qtag)
    first = core[0] == 0
    for n in range(8):
        if n < 2:
            block = pair[n]
        elif n in (4, 5):
            mine, other = (lh, lhe) if n == 4 else (lhe, lh)
            block = jnp.where(first, mine[...], other[...])
        else:
            mine, other = (lpe, lp) if n < 4 else (lp, lpe)
            block = jnp.where(first, mine[n % 2], other[n % 2])
        at = 128 * n
        compt[:, at : at + 128] = block[0:512]
        kpt[128:192, at : at + 128] = block[512:576]
        ktag[8 * n : 8 * n + 8] = block[576:592].astype(F32)[0:8]
    kpt[192:256] = jnp.zeros((64, NK), BF)
    kpt[0:128] = mm(ku[...].T, compt[...], NN).astype(BF)
    pairs = [(qp, qp_hbm), (do, do_hbm), (compt, compt_hbm), (kpt, kpt_hbm), (qtag, qtag_hbm), (ktag, ktag_hbm)]
    copies = copied(pairs, sems)
    v[...] = mm(vu[...].T, compt[...], NN).astype(BF).T
    kp[...] = kpt[...].T
    copies += copied([(kp, kp_hbm), (v, v_hbm)], late_sems)
    stats[...] = jnp.zeros_like(stats)
    statistics(1536, qp, do, qtag, kp, v, ktag, stats, 0)
    for copy in copies:
        copy.wait()


def forward_far(qz, kp, v, ktag, near, qp_hbm, do_hbm, qtag_hbm, stats, qp, do, qtag, own, sems):
    take_queries([qz[i] for i in range(4)], qp, do, qtag)
    copies = copied([(qp, qp_hbm), (do, do_hbm), (qtag, qtag_hbm)], sems)
    own[...] = jnp.zeros((8, 512), F32)
    statistics(512, qp, do, qtag, kp, v, ktag, own, 0)
    for p in range(3):
        stats[4 * p : 4 * p + 4] = near[0:4, 512 * p : 512 * p + 512]
    stats[12:16] = own[0:4]
    for copy in copies:
        copy.wait()


START = {0: 0, 1: 512, 3: 1024, 2: 1536}


def backward(*refs):
    there, (s0, s1, s2, s3), zpay, xpay, up = refs[:11], refs[11:15], refs[15:19], refs[19:23], refs[23]
    (dk, dv, low), here, sems = refs[24:27], refs[27:38], refs[38]
    kp, ktag, qp, qtag, v, do, kpt, qp2, qtag2, do2, compt = here
    copies = copied(list(zip(there, here)), sems)
    copies[1].wait()
    late = lateness()
    ktags = [ktag[8 * n : 8 * n + 1] for n in range(8)]
    stats = [s0, s1, s2, s3]
    for r in range(4):
        rows = []
        for d in range(4):
            at = START[(r - d) % 4] // 128
            rows.append([stats[d][at + n : at + n + 1] for n in range(3)])
        top = functools.reduce(jnp.maximum, [t[0] for t in rows])
        total = sum(t[1] * jnp.exp2(t[0] - top) for t in rows)
        weighted = sum(t[2] * jnp.exp2(t[0] - top) for t in rows)
        at = START[r]
        low[0:1, at : at + 512] = top + jnp.log2(total)
        low[1:2, at : at + 512] = weighted / total
    dk[...] = jnp.zeros_like(dk)
    dv[...] = jnp.zeros_like(dv)
    for n in (0, 2, 3, 4, 5, 6):
        copies[n].wait()
    for r in (0, 1, 3, 2):
        if r == 2:
            for copy in copies[7:10]:
                copy.wait()
        for i in range(2):
            to = START[r] + i * TQ
            if r == 2:
                q, g, qt = qp2[i * TQ : i * TQ + TQ], do2[i * TQ : i * TQ + TQ], qtag2[0:1, i * TQ : i * TQ + TQ]
            else:
                q, g, qt = qp[to : to + TQ], do[to : to + TQ], qtag[0:1, to : to + TQ]
            raw = mm(kp[...], q, NT)
            s = masked_scores(raw, [qt[:, 0:128], qt[:, 128:256]], ktags, late)
            p = jnp.exp2(s - low[0:1, to : to + TQ])
            dp = mm(v[...], g, NT)
            ds = (p * (dp - low[1:2, to : to + TQ])).astype(BF)
            dk[...] += mm(ds, q, NN)
            dv[...] += mm(p.astype(BF), g, NN)
            dq = (mm(kpt[...], ds, NN).T * SCALE).astype(BF)
            for b in range(2):
                m = 2 * i + b
                zpay[r][128 * m : 128 * m + 128] = dq[128 * b : 128 * b + 128, 0:128]
                zpay[r][512 + 64 * m : 576 + 64 * m] = dense_rope(dq[128 * b : 128 * b + 128, 128:192])
    dk16 = (dk[...] * SCALE).astype(BF)
    dv16 = dv[...].astype(BF)
    drope = dk16[:, 128:256].T
    for n in range(8):
        r, m = n // 2, n % 2
        xpay[r][128 * m : 128 * m + 128] = dk16[128 * n : 128 * n + 128, 0:128]
        xpay[r][256 + 128 * m : 384 + 128 * m] = dv16[128 * n : 128 * n + 128]
        xpay[r][512 + 64 * m : 576 + 64 * m] = drope[0:64, 128 * n : 128 * n + 128]
    copies[10].wait()
    both = mm(compt[...], jnp.concatenate([dk16[:, 0:128], dv16], axis=1), NN).astype(BF)
    for y in range(2):
        for z in range(4):
            at = 128 * z + 64 * y
            up[4 * y + z, 0:64] = both[at : at + 64, 0:128]
            up[4 * y + z, 64:128] = both[at : at + 64, 128:256]


def sum_queries(z0, z1, z2, z3, q0, q1, q2, q3):
    def total(rows):
        return sum(a[rows].astype(F32) for a in (z0, z1, z2, z3)).astype(BF)

    for r, back in enumerate((q0, q1, q2, q3)):
        back[0:128] = total(slice(128 * r, 128 * r + 128))
        back[128:192] = total(slice(512 + 64 * r, 576 + 64 * r))


def fold(x, x0, x1, x2, x3, ku, vu, pay, lat):
    acc = jnp.zeros((512, 256), F32)
    rope = jnp.zeros((128, 128), F32)
    for r, p in enumerate((x0, x1, x2, x3)):
        h = pl.multiple_of(lax.rem(x[0] + 4 - r, 4) * 128, 128)
        acc += mm(ku[:, pl.ds(h, 128)], p[0:256], NT)
        acc += mm(vu[:, pl.ds(h, 128)], p[256:512], NT)
        rope += p[512:640].astype(F32)
    lat[0:512] = acc[:, 0:128]
    lat[512:576] = rope[0:64]
    pay[0:512] = acc[:, 128:256].astype(BF)
    pay[512:576] = rope[64:128].astype(BF)


def spread(parts, every):
    mine = sum(parts[n].astype(F32) for n in range(8)).astype(BF)
    for n in range(32):
        every[n] = mine


def unpack_query_grad(x, q0, q1, q2, q3, out, heads):
    for r, ref in enumerate((q0, q1, q2, q3)):
        heads[(x[0] + r) & 3] = ref[...]
    for h in range(4):
        out[:, 192 * h : 192 * h + 128] = heads[h, 0:128]
        out[:, 192 * h + 128 : 192 * h + 192] = wide_rope(heads[h, 128:192])


def unpack_up(a, key, value):
    for y in range(2):
        for z in range(4):
            for x in range(4):
                part = a[place(y, z, x)].astype(F32)
                at = 128 * z + 64 * y
                key[at : at + 64, 128 * x : 128 * x + 128] = part[0:64]
                value[at : at + 64, 128 * x : 128 * x + 128] = part[64:128]


def shards(queries, latents, key_up, value_up, out_grad, positions):
    here = lax.axis_index("seq").astype(jnp.int32)
    x = here & 3
    part = ((QP, 128), BF)
    own, to1, to2, to3, lat = call(
        pack,
        [part, part, part, part, ((LP, 128), BF)],
        [(positions, HB), (x[None], SM), (queries, HB), (out_grad, HB), (latents.T, HB)],
        scratch=[
            pltpu.VMEM((ROWS, 768), BF), pltpu.VMEM((ROWS, 512), BF), pltpu.VMEM((4, QP, 128), BF),
            pltpu.SMEM((ROWS,), jnp.int32), pltpu.SemaphoreType.DMA((4,)),
        ],
    )
    core = lax.axis_index("head").astype(jnp.int32) & 1
    lat_y = along(lat, dy=1)
    q_1 = along(to1, dx=1)
    q_3 = along(to3, dx=-1)
    q_2 = along(to2, dx=2)
    pair = jnp.stack([lat, lat_y])
    q0 = jnp.stack([own, q_1, q_2, q_3])
    lp = by_core(pair, 1)
    lh = by_core(lax.dynamic_index_in_dim(pair, core, 0, keepdims=False), 2)
    qa = along(q0, dz=1)
    qb = along(q0, dz=-1)
    lpe = to_core(lp)
    lhe = to_core(lh)
    qz = along(q0, dz=2)
    ku = lax.dynamic_slice(key_up, (0, x * 128), (D_LAT, 128))
    vu = lax.dynamic_slice(value_up, (0, x * 128), (D_LAT, 128))

    flops = 2 * NQ * NK * 512
    near = [
        ((1536, 256), BF), ((1536, 128), BF), ((512, NK), BF), ((256, NK), BF), ((8, 1536), F32),
        ((NK, 256), BF), ((NK, 128), BF), ((64, 128), F32),
    ]
    qp, do, compt, kpt, qtag, kp, v, ktag, kp_here, v_here, ktag_here, stats = call(
        forward_near,
        [(*o, HB) for o in near] + near[5:8] + [((8, 1536), F32)],
        [(core[None], SM), q0, qa, qb, pair, lp, lpe, lh, lhe, ku, vu],
        scratch=[pltpu.VMEM(*o) for o in near[:5]] + [pltpu.SemaphoreType.DMA((6,)), pltpu.SemaphoreType.DMA((2,))],
        flops=flops * 3 // 4, grant=20,
    )
    far = [((512, 256), BF), ((512, 128), BF), ((8, 512), F32)]
    qp2, do2, qtag2, stats = call(
        forward_far,
        [(*o, HB) for o in far] + [((16, 512), F32)],
        [qz, kp_here, v_here, ktag_here, stats],
        scratch=[pltpu.VMEM(*o) for o in far] + [pltpu.VMEM((8, 512), F32), pltpu.SemaphoreType.DMA((3,))],
        flops=flops // 4, grant=12,
    )
    s3 = along(stats, dz=1)
    s1 = along(stats, dz=-1)
    s2 = along(stats, dz=2)

    there = [kp, ktag, qp, qtag, v, do, kpt, qp2, qtag2, do2, compt]
    pays = call(
        backward,
        [((768, 128), BF)] * 4 + [((640, 128), BF)] * 4 + [((8, 128, 128), BF)],
        [(a, HB) for a in there] + [stats, s1, s2, s3],
        scratch=[
            pltpu.VMEM((NK, 256), F32), pltpu.VMEM((NK, 128), F32), pltpu.VMEM((8, NQ), F32),
            *[pltpu.VMEM(a.shape, a.dtype) for a in there], pltpu.SemaphoreType.DMA((11,)),
        ],
        flops=3 * flops, grant=24,
    )
    zpay, xpay, up = pays[:4], pays[4:8], pays[8]
    x1 = along(xpay[1], dx=1)
    x3 = along(xpay[3], dx=3)
    x2 = along(xpay[2], dx=2)
    ups = lax.all_to_all(up, "seq", 0, 0, tiled=True, axis_index_groups=YZ_GROUPS)
    z1 = along(zpay[1], dz=1)
    z3 = along(zpay[3], dz=3)
    z2 = along(zpay[2], dz=2)
    pay, mine = call(
        fold, [((576, 128), BF), ((576, 128), F32)],
        [(x[None], SM), xpay[0], x1, x2, x3, key_up, value_up],
        flops=2 * 256 * 512 * 1024, grant=10,
    )
    got = along(pay, dy=1)
    (every,) = call(spread, [((32, 128, 128), BF)], [ups])
    whole = lax.all_to_all(every, "seq", 0, 0, tiled=True)
    b0, b1, b2, b3 = call(sum_queries, [((192, 128), BF)] * 4, [zpay[0], z1, z2, z3])
    c1 = along(b1, dx=-1)
    c3 = along(b3, dx=-3)
    c2 = along(b2, dx=-2)
    lat16 = lax.reduce_precision(mine + got.astype(F32), 8, 7).astype(BF)
    near16 = to_core(lat16)
    two = lax.reduce_precision(lat16.astype(F32) + near16.astype(F32), 8, 7).astype(BF)
    far16 = lax.ppermute(two, "head", [(0, 2), (1, 3), (2, 0), (3, 1)])
    latent_grad = (two.astype(F32) + far16.astype(F32)).T
    (query_grad,) = call(
        unpack_query_grad, [((ROWS, 768), BF)], [(x[None], SM), b0, c1, c2, c3],
        scratch=[pltpu.VMEM((4, 192, 128), BF)],
    )
    key_up_grad, value_up_grad = call(unpack_up, [((512, 512), F32), ((512, 512), F32)], [whole])
    return (query_grad, latent_grad, key_up_grad, value_up_grad)


def solution(mesh):
    in_specs = (
        P("seq", "head"),
        P("seq", None),
        P(None, "head"),
        P(None, "head"),
        P("seq", "head"),
        P("seq"),
    )
    out_specs = (P("seq", "head"), P("seq", None), P(None, "head"), P(None, "head"))
    return jax.shard_map(shards, mesh=mesh, in_specs=in_specs, out_specs=out_specs, check_vma=False)
```

profile of v0, /device:TPU:0, one launch (start us, length us, event | category | flops | bytes accessed | tf_op | source)
XLA Modules:
  0.0 108.9 jit_solution(2547024531771383382)
XLA Ops:
  0.6 1.3 %shard_map.93 = (bf16[336,128]{1,0:T(8,128)(2,1)S(1)}, bf16[336,128]{1,0:T(8,128)(2,1)S(1)}, bf16[336,128]{1,0:T(8,128)(2,1)S(1)}, bf16[336,128]{1,0:T(8,128)(2,1)S(1)}, bf16[592,128]{1,0:T(8,128)(2,1)S(1)}) custom-call(s32[128]{0:T(128)} %pos_hbm.1, s32[1]{0:T(128)} %bitcast.x, bf16[128,768]{1,0:T(8,128)(2,1)} %q_hbm.1, bf16[128,512]{1,0:T(8,128)(2,1)} %g_hbm.1, ...), custom_call_target="tpu_custom_call" | custom-call | flops 1 | bytes 1048576 | tf_op jit(solution)/shard_map/pallas_call | solution.py:64
  1.9 1.8 %collective-permute-start.5 = (bf16[592,128]{1,0:T(8,128)(2,1)S(1)}, bf16[592,128]{1,0:T(8,128)(2,1)S(1)}, u32[]{:S(2)}, u32[]{:S(2)}) collective-permute-start(bf16[592,128]{1,0:T(8,128)(2,1)S(1)} %get-tuple-element.46), channel_id=1, source_target_pairs={{0,64},{4,68},{8,72},{12,76},{16,80},{20,84},{24,88},{28,92},{32,9... | collective-permute-start | bytes 454664 | tf_op jit(solution)/shard_map/ppermute | solution.py:39
  3.7 1.5 %collective-permute-start = (bf16[336,128]{1,0:T(8,128)(2,1)S(1)}, bf16[336,128]{1,0:T(8,128)(2,1)S(1)}, u32[]{:S(2)}, u32[]{:S(2)}) collective-permute-start(bf16[336,128]{1,0:T(8,128)(2,1)S(1)} %get-tuple-element.43), channel_id=1, source_target_pairs={{0,4},{4,8},{8,12},{12,0},{16,20},{20,24},{24,28},{28,16},{32,36},... | collective-permute-start | bytes 258056 | tf_op jit(solution)/shard_map/ppermute | solution.py:39
  5.2 2.7 %collective-permute-start.1 = (bf16[336,128]{1,0:T(8,128)(2,1)S(1)}, bf16[336,128]{1,0:T(8,128)(2,1)S(1)}, u32[]{:S(2)}, u32[]{:S(2)}) collective-permute-start(bf16[336,128]{1,0:T(8,128)(2,1)S(1)} %get-tuple-element.44), channel_id=1, source_target_pairs={{0,8},{4,12},{8,0},{12,4},{16,24},{20,28},{24,16},{28,20},{32,40},... | collective-permute-start | bytes 258056 | tf_op jit(solution)/shard_map/ppermute | solution.py:39
  7.9 1.4 %collective-permute-start.2 = (bf16[336,128]{1,0:T(8,128)(2,1)S(1)}, bf16[336,128]{1,0:T(8,128)(2,1)S(1)}, u32[]{:S(2)}, u32[]{:S(2)}) collective-permute-start(bf16[336,128]{1,0:T(8,128)(2,1)S(1)} %get-tuple-element.45), channel_id=1, source_target_pairs={{0,12},{4,0},{8,4},{12,8},{16,28},{20,16},{24,20},{28,24},{32,44},... | collective-permute-start | bytes 258056 | tf_op jit(solution)/shard_map/ppermute | solution.py:39
  9.4 0.7 collective-permute-start.6
  10.3 1.4 %collective-permute-done.1 = bf16[336,128]{1,0:T(8,128)(2,1)S(1)} collective-permute-done((bf16[336,128]{1,0:T(8,128)(2,1)S(1)}, bf16[336,128]{1,0:T(8,128)(2,1)S(1)}, u32[]{:S(2)}, u32[]{:S(2)}) %collective-permute-start.1) | collective-permute-done | bytes 86048 | tf_op jit(solution)/shard_map/ppermute | solution.py:39
  11.7 1.6 %collective-permute-done.2 = bf16[336,128]{1,0:T(8,128)(2,1)S(1)} collective-permute-done((bf16[336,128]{1,0:T(8,128)(2,1)S(1)}, bf16[336,128]{1,0:T(8,128)(2,1)S(1)}, u32[]{:S(2)}, u32[]{:S(2)}) %collective-permute-start.2) | collective-permute-done | bytes 86048 | tf_op jit(solution)/shard_map/ppermute | solution.py:39
  13.3 2.0 %collective-permute-start.3 = (bf16[4,336,128]{2,1,0:T(8,128)(2,1)S(1)}, bf16[4,336,128]{2,1,0:T(8,128)(2,1)S(1)}, u32[]{:S(2)}, u32[]{:S(2)}) collective-permute-start(bf16[4,336,128]{2,1,0:T(8,128)(2,1)S(1)} %pad_maximum_fusion.q0), channel_id=1, source_target_pairs={{0,16},{4,20},{8,24},{12,28},{16,32},{20,36},{24,40},{28,44},{32,4... | collective-permute-start | bytes 1032200 | tf_op jit(solution)/shard_map/ppermute | solution.py:39
  15.3 2.2 %collective-permute-start.4 = (bf16[4,336,128]{2,1,0:T(8,128)(2,1)S(1)}, bf16[4,336,128]{2,1,0:T(8,128)(2,1)S(1)}, u32[]{:S(2)}, u32[]{:S(2)}) collective-permute-start(bf16[4,336,128]{2,1,0:T(8,128)(2,1)S(1)} %pad_maximum_fusion.q0), channel_id=1, source_target_pairs={{0,48},{4,52},{8,56},{12,60},{16,0},{20,4},{24,8},{28,12},{32,16},... | collective-permute-start | bytes 1032200 | tf_op jit(solution)/shard_map/ppermute | solution.py:39
  17.6 2.8 %collective-permute-start.8 = (bf16[592,128]{1,0:T(8,128)(2,1)S(1)}, bf16[592,128]{1,0:T(8,128)(2,1)S(1)}, u32[]{:S(2)}, u32[]{:S(2)}) collective-permute-start(bf16[592,128]{1,0:T(8,128)(2,1)S(1)} %fusion.1), channel_id=1, source_target_pairs={{0,8},{1,9},{2,10},{3,11},{4,12},{5,13},{6,14},{7,15},{8,0},{9,1},... | collective-permute-start | bytes 454664 | tf_op jit(solution)/shard_map/ppermute | solution.py:50
  20.4 2.6 %collective-permute-start.10 = (bf16[4,336,128]{2,1,0:T(8,128)(2,1)S(1)}, bf16[4,336,128]{2,1,0:T(8,128)(2,1)S(1)}, u32[]{:S(2)}, u32[]{:S(2)}) collective-permute-start(bf16[4,336,128]{2,1,0:T(8,128)(2,1)S(1)} %pad_maximum_fusion.q0), channel_id=1, source_target_pairs={{0,32},{4,36},{8,40},{12,44},{16,48},{20,52},{24,56},{28,60},{32,0... | collective-permute-start | bytes 1032200 | tf_op jit(solution)/shard_map/ppermute | solution.py:39
  23.0 1.4 %collective-permute-done.8.lh = bf16[592,128]{1,0:T(8,128)(2,1)S(1)} collective-permute-done((bf16[592,128]{1,0:T(8,128)(2,1)S(1)}, bf16[592,128]{1,0:T(8,128)(2,1)S(1)}, u32[]{:S(2)}, u32[]{:S(2)}) %collective-permute-start.8) | collective-permute-done | bytes 151584 | tf_op jit(solution)/shard_map/ppermute | solution.py:50
  24.5 1.3 %collective-permute-done.9.lhe = bf16[592,128]{1,0:T(8,128)(2,1)S(1)} collective-permute-done((bf16[592,128]{1,0:T(8,128)(2,1)S(1)}, bf16[592,128]{1,0:T(8,128)(2,1)S(1)}, u32[]{:S(2)}, u32[]{:S(2)}) %collective-permute-start.9) | collective-permute-done | bytes 151584 | tf_op jit(solution)/shard_map/ppermute | solution.py:54
  25.8 6.2 %shard_map.94 = (bf16[1536,256]{1,0:T(8,128)(2,1)}, bf16[1536,128]{1,0:T(8,128)(2,1)}, bf16[512,1024]{1,0:T(8,128)(2,1)}, bf16[256,1024]{1,0:T(8,128)(2,1)}, f32...) custom-call(s32[1]{0:T(128)} %bitcast.1.core, ...), custom_call_target="tpu_custom_call" | custom-call | flops 1610612736 | bytes 1048576 | tf_op jit(solution)/shard_map/pallas_call | solution.py:64
  31.9 0.4 collective-permute-done.10.qz
  32.4 1.5 %shard_map.95 = (bf16[512,256]{1,0:T(8,128)(2,1)}, bf16[512,128]{1,0:T(8,128)(2,1)}, f32[8,512]{1,0:T(8,128)}, f32[16,512]{1,0:T(8,128)S(1)}) custom-call(bf16[4,336,128]{2,1,0:T(8,128)(2,1)S(1)} %collective-permute-done.10.qz, bf16[1024,256]{1,0:T(8,128)(2,1)S(1)} %get-tuple-element.54.kp, bf16[1024,128]{1,0:T(8,128)(2,1)S(1)} %get-tuple-element.55.v, ...), custom_call_target="tpu_custom_call" | custom-call | flops 536870912 | bytes 1048576 | tf_op jit(solution)/shard_map/pallas_call | solution.py:64
  33.9 2.8 %collective-permute-start.11 = (f32[16,512]{1,0:T(8,128)S(1)}, f32[16,512]{1,0:T(8,128)S(1)}, u32[]{:S(2)}, u32[]{:S(2)}) collective-permute-start(f32[16,512]{1,0:T(8,128)S(1)} %get-tuple-element.62.refs_11_), channel_id=1, source_target_pairs={{0,48},{4,52},{8,56},{12,60},{16,0},{20,4},{24,8},{28,12},{32,16},... | collective-permute-start | bytes 98312 | tf_op jit(solution)/shard_map/ppermute | solution.py:39
  36.7 0.3 collective-permute-start.12
  37.0 1.0 collective-permute-start.13
  38.0 0.3 collective-permute-done.11.refs_12_
  38.3 3.9 %collective-permute-done.12.refs_13_ = f32[16,512]{1,0:T(8,128)S(1)} collective-permute-done((f32[16,512]{1,0:T(8,128)S(1)}, f32[16,512]{1,0:T(8,128)S(1)}, u32[]{:S(2)}, u32[]{:S(2)}) %collective-permute-start.12) | collective-permute-done | bytes 32800 | tf_op jit(solution)/shard_map/ppermute | solution.py:39
  42.2 0.3 collective-permute-done.13.refs_14_
  42.5 9.7 %shard_map.96 = (bf16[768,128]{1,0:T(8,128)(2,1)S(1)}, bf16[768,128]{1,0:T(8,128)(2,1)S(1)}, bf16[768,128]{1,0:T(8,128)(2,1)S(1)}, bf16[768,128]{1,0:T(8,128)(2,...) custom-call(bf16[1024,256]{1,0:T(8,128)(2,1)} %get-tuple-element.47., ...), custom_call_target="tpu_custom_call" | custom-call | flops 6442450944 | bytes 1048576 | tf_op jit(solution)/shard_map/pallas_call | solution.py:64
  52.3 8.8 %collective-permute-start.21 = (bf16[640,128]{1,0:T(8,128)(2,1)S(1)}, bf16[640,128]{1,0:T(8,128)(2,1)S(1)}, u32[]{:S(2)}, u32[]{:S(2)}) collective-permute-start(bf16[640,128]{1,0:T(8,128)(2,1)S(1)} %get-tuple-element.73), channel_id=1, source_target_pairs={{0,8},{4,12},{8,0},{12,4},{16,24},{20,28},{24,16},{28,20},{32,40},... | collective-permute-start | bytes 491528 | tf_op jit(solution)/shard_map/ppermute | solution.py:39
  61.1 0.7 collective-permute-start.22
  61.8 3.4 %all-to-all-start = ((bf16[8,128,128]{2,1,0:T(8,128)(2,1)}), bf16[8,128,128]{2,1,0:T(8,128)(2,1)S(1)}, u32[]{:S(2)}, u32[]{:S(2)}) async-start(bf16[8,128,128]{2,1,0:T(8,128)(2,1)} %get-tuple-element.77), calls=%async_computation | async-start | bytes 524288 | tf_op jit(solution)/shard_map/all_to_all | solution.py:396
  65.3 0.9 collective-permute-done.21.x2
  66.2 0.3 collective-permute-done.22.x3
  66.4 0.7 shard_map.99
  67.2 0.9 collective-permute-start.23
  68.0 4.4 %all-to-all-done.parts = bf16[8,128,128]{2,1,0:T(8,128)(2,1)S(1)} async-done(((bf16[8,128,128]{2,1,0:T(8,128)(2,1)}), bf16[8,128,128]{2,1,0:T(8,128)(2,1)S(1)}, u32[]{:S(2)}, u32[]{:S(2)}) %all-to-all-start) | async-done | bytes 262176 | tf_op jit(solution)/shard_map/all_to_all | solution.py:396
  72.4 1.1 %shard_map.100 = bf16[32,128,128]{2,1,0:T(8,128)(2,1)} custom-call(bf16[8,128,128]{2,1,0:T(8,128)(2,1)S(1)} %all-to-all-done.parts), custom_call_target="tpu_custom_call" | custom-call | flops 1 | bytes 1048576 | tf_op jit(solution)/shard_map/pallas_call | solution.py:64
  73.5 4.2 %all-to-all-start.1 = ((bf16[32,128,128]{2,1,0:T(8,128)(2,1)}), bf16[32,128,128]{2,1,0:T(8,128)(2,1)S(1)}, u32[]{:S(2)}, u32[]{:S(2)}) async-start(bf16[32,128,128]{2,1,0:T(8,128)(2,1)} %shard_map.100), calls=%async_computation.1 | async-start | bytes 2097152 | tf_op jit(solution)/shard_map/all_to_all | solution.py:407
  77.9 1.9 %collective-permute-start.14 = (bf16[768,128]{1,0:T(8,128)(2,1)S(1)}, bf16[768,128]{1,0:T(8,128)(2,1)S(1)}, u32[]{:S(2)}, u32[]{:S(2)}) collective-permute-start(bf16[768,128]{1,0:T(8,128)(2,1)S(1)} %get-tuple-element.64), channel_id=1, source_target_pairs={{0,16},{4,20},{8,24},{12,28},{16,32},{20,36},{24,40},{28,44},{32,4... | collective-permute-start | bytes 589832 | tf_op jit(solution)/shard_map/ppermute | solution.py:39
  79.7 2.7 %collective-permute-start.15 = (bf16[768,128]{1,0:T(8,128)(2,1)S(1)}, bf16[768,128]{1,0:T(8,128)(2,1)S(1)}, u32[]{:S(2)}, u32[]{:S(2)}) collective-permute-start(bf16[768,128]{1,0:T(8,128)(2,1)S(1)} %get-tuple-element.65), channel_id=1, source_target_pairs={{0,32},{4,36},{8,40},{12,44},{16,48},{20,52},{24,56},{28,60},{32,0... | collective-permute-start | bytes 589832 | tf_op jit(solution)/shard_map/ppermute | solution.py:39
  82.4 1.5 %collective-permute-start.16 = (bf16[768,128]{1,0:T(8,128)(2,1)S(1)}, bf16[768,128]{1,0:T(8,128)(2,1)S(1)}, u32[]{:S(2)}, u32[]{:S(2)}) collective-permute-start(bf16[768,128]{1,0:T(8,128)(2,1)S(1)} %get-tuple-element.66), channel_id=1, source_target_pairs={{0,48},{4,52},{8,56},{12,60},{16,0},{20,4},{24,8},{28,12},{32,16},... | collective-permute-start | bytes 589832 | tf_op jit(solution)/shard_map/ppermute | solution.py:39
  83.9 3.2 %collective-permute-start.25 = (bf16[576,128]{1,0:T(8,128)(2,1)S(1)}, bf16[576,128]{1,0:T(8,128)(2,1)S(1)}, u32[]{:S(2)}, u32[]{:S(2)}) collective-permute-start(bf16[576,128]{1,0:T(8,128)(2,1)S(1)} %reduce-precision_convert_fusion), channel_id=1, source_target_pairs={{0,2},{1,3},{2,0},{3,1},{4,6},{5,7},{6,4},{7,5},{8,10},{9,11},{10,... | collective-permute-start | bytes 442376 | tf_op jit(solution)/shard_map/ppermute | solution.py:415
  87.1 5.0 %collective-permute-done.14.z1 = bf16[768,128]{1,0:T(8,128)(2,1)S(1)} collective-permute-done((bf16[768,128]{1,0:T(8,128)(2,1)S(1)}, bf16[768,128]{1,0:T(8,128)(2,1)S(1)}, u32[]{:S(2)}, u32[]{:S(2)}) %collective-permute-start.14) | collective-permute-done | bytes 196640 | tf_op jit(solution)/shard_map/ppermute | solution.py:39
  92.1 4.6 %collective-permute-done.15.z2 = bf16[768,128]{1,0:T(8,128)(2,1)S(1)} collective-permute-done((bf16[768,128]{1,0:T(8,128)(2,1)S(1)}, bf16[768,128]{1,0:T(8,128)(2,1)S(1)}, u32[]{:S(2)}, u32[]{:S(2)}) %collective-permute-start.15) | collective-permute-done | bytes 196640 | tf_op jit(solution)/shard_map/ppermute | solution.py:39
  96.9 2.7 %collective-permute-start.17 = (bf16[192,128]{1,0:T(8,128)(2,1)S(1)}, bf16[192,128]{1,0:T(8,128)(2,1)S(1)}, u32[]{:S(2)}, u32[]{:S(2)}) collective-permute-start(bf16[192,128]{1,0:T(8,128)(2,1)S(1)} %get-tuple-element.68), channel_id=1, source_target_pairs={{0,12},{4,0},{8,4},{12,8},{16,28},{20,16},{24,20},{28,24},{32,44},... | collective-permute-start | bytes 147464 | tf_op jit(solution)/shard_map/ppermute | solution.py:39
  99.6 0.9 collective-permute-start.18
  100.5 0.8 collective-permute-start.19
  101.5 3.7 %collective-permute-done.18.q2 = bf16[192,128]{1,0:T(8,128)(2,1)S(1)} collective-permute-done((bf16[192,128]{1,0:T(8,128)(2,1)S(1)}, bf16[192,128]{1,0:T(8,128)(2,1)S(1)}, u32[]{:S(2)}, u32[]{:S(2)}) %collective-permute-start.18) | collective-permute-done | bytes 49184 | tf_op jit(solution)/shard_map/ppermute | solution.py:39
  105.1 0.6 collective-permute-done.19.q3
  105.8 0.9 shard_map.98
  106.7 0.7 add_bitcast_fusion
  107.4 1.5 %shard_map.101 = (f32[512,512]{1,0:T(8,128)}, f32[512,512]{1,0:T(8,128)}) custom-call(bf16[32,128,128]{2,1,0:T(8,128)(2,1)S(1)} %all-to-all-done.1.a), custom_call_target="tpu_custom_call" | custom-call | flops 1 | bytes 1048576 | tf_op jit(solution)/shard_map/pallas_call | solution.py:64
  (28 shorter events, 1.1 us)
Async XLA Ops:
  1.9 7.4 %collective-permute-start.5 = (bf16[592,128]{1,0:T(8,128)(2,1)S(1)}, bf16[592,128]{1,0:T(8,128)(2,1)S(1)}, u32[]{:S(2)}, u32[]{:S(2)}) collective-permute-start(bf16[592,128]{1,0:T(8,128)(2,1)S(1)} %get-tuple-element.46), channel_id=1, source_target_pairs={{0,64},{4,68},{8,72},{12,76},{16,80},{20,84},{24,88},{28,92},{32,9... | collective-permute-start | bytes 454664 | tf_op jit(solution)/shard_map/ppermute | solution.py:39
  3.7 6.6 %collective-permute-start = (bf16[336,128]{1,0:T(8,128)(2,1)S(1)}, bf16[336,128]{1,0:T(8,128)(2,1)S(1)}, u32[]{:S(2)}, u32[]{:S(2)}) collective-permute-start(bf16[336,128]{1,0:T(8,128)(2,1)S(1)} %get-tuple-element.43), channel_id=1, source_target_pairs={{0,4},{4,8},{8,12},{12,0},{16,20},{20,24},{24,28},{28,16},{32,36},... | collective-permute-start | bytes 258056 | tf_op jit(solution)/shard_map/ppermute | solution.py:39
  5.2 6.5 %collective-permute-start.1 = (bf16[336,128]{1,0:T(8,128)(2,1)S(1)}, bf16[336,128]{1,0:T(8,128)(2,1)S(1)}, u32[]{:S(2)}, u32[]{:S(2)}) collective-permute-start(bf16[336,128]{1,0:T(8,128)(2,1)S(1)} %get-tuple-element.44), channel_id=1, source_target_pairs={{0,8},{4,12},{8,0},{12,4},{16,24},{20,28},{24,16},{28,20},{32,40},... | collective-permute-start | bytes 258056 | tf_op jit(solution)/shard_map/ppermute | solution.py:39
  7.9 5.4 %collective-permute-start.2 = (bf16[336,128]{1,0:T(8,128)(2,1)S(1)}, bf16[336,128]{1,0:T(8,128)(2,1)S(1)}, u32[]{:S(2)}, u32[]{:S(2)}) collective-permute-start(bf16[336,128]{1,0:T(8,128)(2,1)S(1)} %get-tuple-element.45), channel_id=1, source_target_pairs={{0,12},{4,0},{8,4},{12,8},{16,28},{20,16},{24,20},{28,24},{32,44},... | collective-permute-start | bytes 258056 | tf_op jit(solution)/shard_map/ppermute | solution.py:39
  9.4 11.0 %collective-permute-start.6 = (bf16[2,592,128]{2,1,0:T(8,128)(2,1)S(1)}, bf16[2,592,128]{2,1,0:T(8,128)(2,1)S(1)}, u32[]{:S(2)}, u32[]{:S(2)}) collective-permute-start(bf16[2,592,128]{2,1,0:T(8,128)(2,1)S(1)} %pad_maximum_fusion.1.pair), channel_id=1, source_target_pairs={{0,4},{1,13},{2,6},{3,15},{4,8},{5,1},{6,10},{7,3},{8,12},{9,5},{1... | collective-permute-start | bytes 909320 | tf_op jit(solution)/shard_map/ppermute | solution.py:50
  13.3 11.1 %copy-start = (bf16[512,512]{1,0:T(8,128)(2,1)S(1)}, bf16[512,512]{1,0:T(8,128)(2,1)}, u32[]{:S(2)}) copy-start(bf16[512,512]{1,0:T(8,128)(2,1)} %vu.1) | copy-start | bytes 1572868
  13.3 11.1 %copy-start.1 = (bf16[512,512]{1,0:T(8,128)(2,1)S(1)}, bf16[512,512]{1,0:T(8,128)(2,1)}, u32[]{:S(2)}) copy-start(bf16[512,512]{1,0:T(8,128)(2,1)} %ku.1) | copy-start | bytes 1572868
  13.3 11.1 %collective-permute-start.3 = (bf16[4,336,128]{2,1,0:T(8,128)(2,1)S(1)}, bf16[4,336,128]{2,1,0:T(8,128)(2,1)S(1)}, u32[]{:S(2)}, u32[]{:S(2)}) collective-permute-start(bf16[4,336,128]{2,1,0:T(8,128)(2,1)S(1)} %pad_maximum_fusion.q0), channel_id=1, source_target_pairs={{0,16},{4,20},{8,24},{12,28},{16,32},{20,36},{24,40},{28,44},{32,4... | collective-permute-start | bytes 1032200 | tf_op jit(solution)/shard_map/ppermute | solution.py:39
  15.3 9.1 %collective-permute-start.4 = (bf16[4,336,128]{2,1,0:T(8,128)(2,1)S(1)}, bf16[4,336,128]{2,1,0:T(8,128)(2,1)S(1)}, u32[]{:S(2)}, u32[]{:S(2)}) collective-permute-start(bf16[4,336,128]{2,1,0:T(8,128)(2,1)S(1)} %pad_maximum_fusion.q0), channel_id=1, source_target_pairs={{0,48},{4,52},{8,56},{12,60},{16,0},{20,4},{24,8},{28,12},{32,16},... | collective-permute-start | bytes 1032200 | tf_op jit(solution)/shard_map/ppermute | solution.py:39
  17.6 6.8 %collective-permute-start.8 = (bf16[592,128]{1,0:T(8,128)(2,1)S(1)}, bf16[592,128]{1,0:T(8,128)(2,1)S(1)}, u32[]{:S(2)}, u32[]{:S(2)}) collective-permute-start(bf16[592,128]{1,0:T(8,128)(2,1)S(1)} %fusion.1), channel_id=1, source_target_pairs={{0,8},{1,9},{2,10},{3,11},{4,12},{5,13},{6,14},{7,15},{8,0},{9,1},... | collective-permute-start | bytes 454664 | tf_op jit(solution)/shard_map/ppermute | solution.py:50
  20.4 5.4 %collective-permute-start.7 = (bf16[2,592,128]{2,1,0:T(8,128)(2,1)S(1)}, bf16[2,592,128]{2,1,0:T(8,128)(2,1)}, u32[]{:S(2)}, u32[]{:S(2)}) collective-permute-start(bf16[2,592,128]{2,1,0:T(8,128)(2,1)S(1)} %collective-permute-done.6.lp), channel_id=1, source_target_pairs={{0,1},{1,0},{2,3},{3,2},{4,5},{5,4},{6,7},{7,6},{8,9},{9,8},{10,11... | collective-permute-start | bytes 909320 | tf_op jit(solution)/shard_map/ppermute | solution.py:54
  20.4 12.0 %collective-permute-start.10 = (bf16[4,336,128]{2,1,0:T(8,128)(2,1)S(1)}, bf16[4,336,128]{2,1,0:T(8,128)(2,1)S(1)}, u32[]{:S(2)}, u32[]{:S(2)}) collective-permute-start(bf16[4,336,128]{2,1,0:T(8,128)(2,1)S(1)} %pad_maximum_fusion.q0), channel_id=1, source_target_pairs={{0,32},{4,36},{8,40},{12,44},{16,48},{20,52},{24,56},{28,60},{32,0... | collective-permute-start | bytes 1032200 | tf_op jit(solution)/shard_map/ppermute | solution.py:39
  24.4 1.4 %collective-permute-start.9 = (bf16[592,128]{1,0:T(8,128)(2,1)S(1)}, bf16[592,128]{1,0:T(8,128)(2,1)S(1)}, u32[]{:S(2)}, u32[]{:S(2)}) collective-permute-start(bf16[592,128]{1,0:T(8,128)(2,1)S(1)} %collective-permute-done.8.lh), channel_id=1, source_target_pairs={{0,1},{1,0},{2,3},{3,2},{4,5},{5,4},{6,7},{7,6},{8,9},{9,8},{10,11... | collective-permute-start | bytes 454664 | tf_op jit(solution)/shard_map/ppermute | solution.py:54
  33.9 4.4 %collective-permute-start.11 = (f32[16,512]{1,0:T(8,128)S(1)}, f32[16,512]{1,0:T(8,128)S(1)}, u32[]{:S(2)}, u32[]{:S(2)}) collective-permute-start(f32[16,512]{1,0:T(8,128)S(1)} %get-tuple-element.62.refs_11_), channel_id=1, source_target_pairs={{0,48},{4,52},{8,56},{12,60},{16,0},{20,4},{24,8},{28,12},{32,16},... | collective-permute-start | bytes 98312 | tf_op jit(solution)/shard_map/ppermute | solution.py:39
  36.7 5.5 %collective-permute-start.12 = (f32[16,512]{1,0:T(8,128)S(1)}, f32[16,512]{1,0:T(8,128)S(1)}, u32[]{:S(2)}, u32[]{:S(2)}) collective-permute-start(f32[16,512]{1,0:T(8,128)S(1)} %get-tuple-element.62.refs_11_), channel_id=1, source_target_pairs={{0,32},{4,36},{8,40},{12,44},{16,48},{20,52},{24,56},{28,60},{32,0... | collective-permute-start | bytes 98312 | tf_op jit(solution)/shard_map/ppermute | solution.py:39
  37.0 5.5 %collective-permute-start.13 = (f32[16,512]{1,0:T(8,128)S(1)}, f32[16,512]{1,0:T(8,128)S(1)}, u32[]{:S(2)}, u32[]{:S(2)}) collective-permute-start(f32[16,512]{1,0:T(8,128)S(1)} %get-tuple-element.62.refs_11_), channel_id=1, source_target_pairs={{0,16},{4,20},{8,24},{12,28},{16,32},{20,36},{24,40},{28,44},{32,4... | collective-permute-start | bytes 98312 | tf_op jit(solution)/shard_map/ppermute | solution.py:39
  52.2 13.0 %collective-permute-start.20 = (bf16[640,128]{1,0:T(8,128)(2,1)S(1)}, bf16[640,128]{1,0:T(8,128)(2,1)S(1)}, u32[]{:S(2)}, u32[]{:S(2)}) collective-permute-start(bf16[640,128]{1,0:T(8,128)(2,1)S(1)} %get-tuple-element.72), channel_id=1, source_target_pairs={{0,4},{4,8},{8,12},{12,0},{16,20},{20,24},{24,28},{28,16},{32,36},... | collective-permute-start | bytes 491528 | tf_op jit(solution)/shard_map/ppermute | solution.py:39
  52.3 13.8 %collective-permute-start.21 = (bf16[640,128]{1,0:T(8,128)(2,1)S(1)}, bf16[640,128]{1,0:T(8,128)(2,1)S(1)}, u32[]{:S(2)}, u32[]{:S(2)}) collective-permute-start(bf16[640,128]{1,0:T(8,128)(2,1)S(1)} %get-tuple-element.73), channel_id=1, source_target_pairs={{0,8},{4,12},{8,0},{12,4},{16,24},{20,28},{24,16},{28,20},{32,40},... | collective-permute-start | bytes 491528 | tf_op jit(solution)/shard_map/ppermute | solution.py:39
  61.1 5.3 %collective-permute-start.22 = (bf16[640,128]{1,0:T(8,128)(2,1)S(1)}, bf16[640,128]{1,0:T(8,128)(2,1)S(1)}, u32[]{:S(2)}, u32[]{:S(2)}) collective-permute-start(bf16[640,128]{1,0:T(8,128)(2,1)S(1)} %get-tuple-element.74), channel_id=1, source_target_pairs={{0,12},{4,0},{8,4},{12,8},{16,28},{20,16},{24,20},{28,24},{32,44},... | collective-permute-start | bytes 491528 | tf_op jit(solution)/shard_map/ppermute | solution.py:39
  61.8 10.6 %all-to-all-start = ((bf16[8,128,128]{2,1,0:T(8,128)(2,1)}), bf16[8,128,128]{2,1,0:T(8,128)(2,1)S(1)}, u32[]{:S(2)}, u32[]{:S(2)}) async-start(bf16[8,128,128]{2,1,0:T(8,128)(2,1)} %get-tuple-element.77), calls=%async_computation | async-start | bytes 524288 | tf_op jit(solution)/shard_map/all_to_all | solution.py:396
  67.2 10.6 %collective-permute-start.23 = (bf16[576,128]{1,0:T(8,128)(2,1)S(1)}, bf16[576,128]{1,0:T(8,128)(2,1)S(1)}, u32[]{:S(2)}, u32[]{:S(2)}) collective-permute-start(bf16[576,128]{1,0:T(8,128)(2,1)S(1)} %get-tuple-element.76), channel_id=1, source_target_pairs={{0,64},{4,68},{8,72},{12,76},{16,80},{20,84},{24,88},{28,92},{32,9... | collective-permute-start | bytes 442376 | tf_op jit(solution)/shard_map/ppermute | solution.py:39
  73.5 33.9 %all-to-all-start.1 = ((bf16[32,128,128]{2,1,0:T(8,128)(2,1)}), bf16[32,128,128]{2,1,0:T(8,128)(2,1)S(1)}, u32[]{:S(2)}, u32[]{:S(2)}) async-start(bf16[32,128,128]{2,1,0:T(8,128)(2,1)} %shard_map.100), calls=%async_computation.1 | async-start | bytes 2097152 | tf_op jit(solution)/shard_map/all_to_all | solution.py:407
  77.8 6.1 %collective-permute-start.24 = (bf16[576,128]{1,0:T(8,128)(2,1)S(1)}, bf16[576,128]{1,0:T(8,128)(2,1)S(1)}, u32[]{:S(2)}, u32[]{:S(2)}) collective-permute-start(bf16[576,128]{1,0:T(8,128)(2,1)S(1)} %reduce-precision_convert_fusion.1), channel_id=1, source_target_pairs={{0,1},{1,0},{2,3},{3,2},{4,5},{5,4},{6,7},{7,6},{8,9},{9,8},{10,11... | collective-permute-start | bytes 442376 | tf_op jit(solution)/shard_map/ppermute | solution.py:54
  77.9 14.2 %collective-permute-start.14 = (bf16[768,128]{1,0:T(8,128)(2,1)S(1)}, bf16[768,128]{1,0:T(8,128)(2,1)S(1)}, u32[]{:S(2)}, u32[]{:S(2)}) collective-permute-start(bf16[768,128]{1,0:T(8,128)(2,1)S(1)} %get-tuple-element.64), channel_id=1, source_target_pairs={{0,16},{4,20},{8,24},{12,28},{16,32},{20,36},{24,40},{28,44},{32,4... | collective-permute-start | bytes 589832 | tf_op jit(solution)/shard_map/ppermute | solution.py:39
  79.7 17.0 %collective-permute-start.15 = (bf16[768,128]{1,0:T(8,128)(2,1)S(1)}, bf16[768,128]{1,0:T(8,128)(2,1)S(1)}, u32[]{:S(2)}, u32[]{:S(2)}) collective-permute-start(bf16[768,128]{1,0:T(8,128)(2,1)S(1)} %get-tuple-element.65), channel_id=1, source_target_pairs={{0,32},{4,36},{8,40},{12,44},{16,48},{20,52},{24,56},{28,60},{32,0... | collective-permute-start | bytes 589832 | tf_op jit(solution)/shard_map/ppermute | solution.py:39
  82.4 14.3 %collective-permute-start.16 = (bf16[768,128]{1,0:T(8,128)(2,1)S(1)}, bf16[768,128]{1,0:T(8,128)(2,1)S(1)}, u32[]{:S(2)}, u32[]{:S(2)}) collective-permute-start(bf16[768,128]{1,0:T(8,128)(2,1)S(1)} %get-tuple-element.66), channel_id=1, source_target_pairs={{0,48},{4,52},{8,56},{12,60},{16,0},{20,4},{24,8},{28,12},{32,16},... | collective-permute-start | bytes 589832 | tf_op jit(solution)/shard_map/ppermute | solution.py:39
  83.9 22.7 %collective-permute-start.25 = (bf16[576,128]{1,0:T(8,128)(2,1)S(1)}, bf16[576,128]{1,0:T(8,128)(2,1)S(1)}, u32[]{:S(2)}, u32[]{:S(2)}) collective-permute-start(bf16[576,128]{1,0:T(8,128)(2,1)S(1)} %reduce-precision_convert_fusion), channel_id=1, source_target_pairs={{0,2},{1,3},{2,0},{3,1},{4,6},{5,7},{6,4},{7,5},{8,10},{9,11},{10,... | collective-permute-start | bytes 442376 | tf_op jit(solution)/shard_map/ppermute | solution.py:415
  96.9 4.6 %collective-permute-start.17 = (bf16[192,128]{1,0:T(8,128)(2,1)S(1)}, bf16[192,128]{1,0:T(8,128)(2,1)S(1)}, u32[]{:S(2)}, u32[]{:S(2)}) collective-permute-start(bf16[192,128]{1,0:T(8,128)(2,1)S(1)} %get-tuple-element.68), channel_id=1, source_target_pairs={{0,12},{4,0},{8,4},{12,8},{16,28},{20,16},{24,20},{28,24},{32,44},... | collective-permute-start | bytes 147464 | tf_op jit(solution)/shard_map/ppermute | solution.py:39
  99.6 5.6 %collective-permute-start.18 = (bf16[192,128]{1,0:T(8,128)(2,1)S(1)}, bf16[192,128]{1,0:T(8,128)(2,1)S(1)}, u32[]{:S(2)}, u32[]{:S(2)}) collective-permute-start(bf16[192,128]{1,0:T(8,128)(2,1)S(1)} %get-tuple-element.69), channel_id=1, source_target_pairs={{0,8},{4,12},{8,0},{12,4},{16,24},{20,28},{24,16},{28,20},{32,40},... | collective-permute-start | bytes 147464 | tf_op jit(solution)/shard_map/ppermute | solution.py:39
  100.5 5.3 %collective-permute-start.19 = (bf16[192,128]{1,0:T(8,128)(2,1)S(1)}, bf16[192,128]{1,0:T(8,128)(2,1)S(1)}, u32[]{:S(2)}, u32[]{:S(2)}) collective-permute-start(bf16[192,128]{1,0:T(8,128)(2,1)S(1)} %get-tuple-element.70), channel_id=1, source_target_pairs={{0,4},{4,8},{8,12},{12,0},{16,20},{20,24},{24,28},{28,16},{32,36},... | collective-permute-start | bytes 147464 | tf_op jit(solution)/shard_map/ppermute | solution.py:39
where the time goes:
time: 109 us
  starting transfers between devices  53.4 us (49%)
  waiting for transfers between devices  30.7 us (28%)
  Pallas kernels  23 us (21%)
    ppermute x20, starting transfers between devices, along(): return lax.ppermute(value, 'seq', pairs)  39.1 us
    ppermute x20, waiting for transfers between devices, along(): return lax.ppermute(value, 'seq', pairs)  23.5 us
    pallas_call x9, Pallas kernels, call(): pl.pallas_call(kernel, out_shape=[HB(o[0], o[1]) if o[2:] == (HB,) else j...  23 us
    all_to_all x1, waiting for transfers between devices, shards(): lax.all_to_all(up, 'seq', 0, 0, tiled=True, axis_index_groups=YZ_GROUPS)  4.42 us
    all_to_all x1, starting transfers between devices, shards(): whole = lax.all_to_all(every, 'seq', 0, 0, tiled=True)  4.17 us
    ppermute x2, starting transfers between devices, by_core(): return lax.ppermute(value, ('seq', 'head'), pairs)  3.45 us
    all_to_all x1, starting transfers between devices, shards(): lax.all_to_all(up, 'seq', 0, 0, tiled=True, axis_index_groups=YZ_GROUPS)  3.41 us
    ppermute x1, starting transfers between devices, shards(): far16 = lax.ppermute(two, 'head', [(0, 2), (1, 3), (2, 0), (3, 1)])  3.16 us
  transfers between devices with their start and end apart: 28, of which 17 were waited for; matrix products, arithmetic and copies ran while one was open for 1% of the time, Pallas kernels for 8%

commit v1 on v0

--- a/solution.py
+++ b/solution.py
@@ -141,6 +141,7 @@
 def statistics(rows, qp, do, qtag, kp, v, ktag, stats, first):
     late = lateness()
     ktags = [ktag[8 * n : 8 * n + 1] for n in range(8)]
+    stats[...] = jnp.zeros_like(stats)
 
     def turn(i, carry):
         at = pl.multiple_of(i * TQ, TQ)
@@ -166,12 +167,12 @@
     return copies
 
 
-def forward_near(
-    core, q0, qa, qb, pair, lp, lpe, lh, lhe, ku, vu,
-    qp_hbm, do_hbm, compt_hbm, kpt_hbm, qtag_hbm, kp_hbm, v_hbm, ktag_hbm, kp, v, ktag, stats,
-    qp, do, compt, kpt, qtag, sems, late_sems,
+def forward_own(
+    core, q0, q1, pair, lp, lpe, lh, lhe, ku, vu,
+    qp_hbm, do_hbm, qtag_hbm, compt_hbm, kpt_hbm, kp_hbm, v_hbm, ktag_hbm, kp, v, ktag, stats,
+    qp, do, qtag, compt, kpt, sems, late_sems,
 ):
-    take_queries([ref[i] for ref in (q0, qb, qa) for i in range(4)], qp, do, qtag)
+    take_queries([ref[i] for ref in (q0, q1) for i in range(2)], qp, do, qtag)
     first = core[0] == 0
     for n in range(8):
         if n < 2:
@@ -188,41 +189,45 @@
         ktag[8 * n : 8 * n + 8] = block[576:592].astype(F32)[0:8]
     kpt[192:256] = jnp.zeros((64, NK), BF)
     kpt[0:128] = mm(ku[...].T, compt[...], NN).astype(BF)
-    pairs = [(qp, qp_hbm), (do, do_hbm), (compt, compt_hbm), (kpt, kpt_hbm), (qtag, qtag_hbm), (ktag, ktag_hbm)]
+    pairs = [(qp, qp_hbm), (do, do_hbm), (qtag, qtag_hbm), (compt, compt_hbm), (kpt, kpt_hbm), (ktag, ktag_hbm)]
     copies = copied(pairs, sems)
     v[...] = mm(vu[...].T, compt[...], NN).astype(BF).T
     kp[...] = kpt[...].T
     copies += copied([(kp, kp_hbm), (v, v_hbm)], late_sems)
-    stats[...] = jnp.zeros_like(stats)
-    statistics(1536, qp, do, qtag, kp, v, ktag, stats, 0)
+    statistics(512, qp, do, qtag, kp, v, ktag, stats, 0)
     for copy in copies:
         copy.wait()
 
 
-def forward_far(qz, kp, v, ktag, near, qp_hbm, do_hbm, qtag_hbm, stats, qp, do, qtag, own, sems):
-    take_queries([qz[i] for i in range(4)], qp, do, qtag)
+def forward_near(a0, a1, b0, b1, kp, v, ktag, qp_hbm, do_hbm, qtag_hbm, stats, qp, do, qtag, sems):
+    take_queries([ref[i] for ref in (b0, b1, a0, a1) for i in range(2)], qp, do, qtag)
     copies = copied([(qp, qp_hbm), (do, do_hbm), (qtag, qtag_hbm)], sems)
-    own[...] = jnp.zeros((8, 512), F32)
-    statistics(512, qp, do, qtag, kp, v, ktag, own, 0)
-    for p in range(3):
-        stats[4 * p : 4 * p + 4] = near[0:4, 512 * p : 512 * p + 512]
-    stats[12:16] = own[0:4]
+    statistics(1024, qp, do, qtag, kp, v, ktag, stats, 0)
     for copy in copies:
         copy.wait()
 
 
+def forward_far(qc, qd, kp, v, ktag, own, near, qp_hbm, do_hbm, qtag_hbm, stats, qp, do, qtag, far, sems):
+    take_queries([ref[i] for ref in (qc, qd) for i in range(2)], qp, do, qtag)
+    copies = copied([(qp, qp_hbm), (do, do_hbm), (qtag, qtag_hbm)], sems)
+    statistics(512, qp, do, qtag, kp, v, ktag, far, 0)
+    stats[0:4] = own[0:4]
+    stats[4:8] = near[0:4, 0:512]
+    stats[8:12] = near[0:4, 512:1024]
+    stats[12:16] = far[0:4]
+    for copy in copies:
+        copy.wait()
+
+
 START = {0: 0, 1: 512, 3: 1024, 2: 1536}
 
 
 def backward(*refs):
-    there, (s0, s1, s2, s3), zpay, xpay, up = refs[:11], refs[11:15], refs[15:19], refs[19:23], refs[23]
-    (dk, dv, low), here, sems = refs[24:27], refs[27:38], refs[38]
-    kp, ktag, qp, qtag, v, do, kpt, qp2, qtag2, do2, compt = here
+    there, stats, zpay, xpay, up = refs[:14], refs[14:18], refs[18:22], refs[22:26], refs[26]
+    (dk, dv, low), here, sems = refs[27:30], refs[30:44], refs[44]
+    kp, qp0, v, do0, ktag, qtag0, kpt, qp1, do1, qtag1, qp2, do2, qtag2, compt = here
     copies = copied(list(zip(there, here)), sems)
-    copies[1].wait()
     late = lateness()
-    ktags = [ktag[8 * n : 8 * n + 1] for n in range(8)]
-    stats = [s0, s1, s2, s3]
     for r in range(4):
         rows = []
         for d in range(4):
@@ -236,18 +241,21 @@
         low[1:2, at : at + 512] = weighted / total
     dk[...] = jnp.zeros_like(dk)
     dv[...] = jnp.zeros_like(dv)
-    for n in (0, 2, 3, 4, 5, 6):
-        copies[n].wait()
+    for copy in copies[:7]:
+        copy.wait()
+    ktags = [ktag[8 * n : 8 * n + 1] for n in range(8)]
     for r in (0, 1, 3, 2):
-        if r == 2:
+        if r == 1:
             for copy in copies[7:10]:
                 copy.wait()
+        if r == 2:
+            for copy in copies[10:13]:
+                copy.wait()
+        qp, do, qtag = {0: (qp0, do0, qtag0), 2: (qp2, do2, qtag2)}.get(r, (qp1, do1, qtag1))
         for i in range(2):
             to = START[r] + i * TQ
-            if r == 2:
-                q, g, qt = qp2[i * TQ : i * TQ + TQ], do2[i * TQ : i * TQ + TQ], qtag2[0:1, i * TQ : i * TQ + TQ]
-            else:
-                q, g, qt = qp[to : to + TQ], do[to : to + TQ], qtag[0:1, to : to + TQ]
+            at = i * TQ + (512 if r == 3 else 0)
+            q, g, qt = qp[at : at + TQ], do[at : at + TQ], qtag[0:1, at : at + TQ]
             raw = mm(kp[...], q, NT)
             s = masked_scores(raw, [qt[:, 0:128], qt[:, 128:256]], ktags, late)
             p = jnp.exp2(s - low[0:1, to : to + TQ])
@@ -268,7 +276,7 @@
         xpay[r][128 * m : 128 * m + 128] = dk16[128 * n : 128 * n + 128, 0:128]
         xpay[r][256 + 128 * m : 384 + 128 * m] = dv16[128 * n : 128 * n + 128]
         xpay[r][512 + 64 * m : 576 + 64 * m] = drope[0:64, 128 * n : 128 * n + 128]
-    copies[10].wait()
+    copies[13].wait()
     both = mm(compt[...], jnp.concatenate([dk16[:, 0:128], dv16], axis=1), NN).astype(BF)
     for y in range(2):
         for z in range(4):
@@ -343,49 +351,67 @@
     q_3 = along(to3, dx=-1)
     q_2 = along(to2, dx=2)
     pair = jnp.stack([lat, lat_y])
-    q0 = jnp.stack([own, q_1, q_2, q_3])
+    q0 = jnp.stack([own, q_1])
+    q1 = jnp.stack([q_2, q_3])
     lp = by_core(pair, 1)
     lh = by_core(lax.dynamic_index_in_dim(pair, core, 0, keepdims=False), 2)
-    qa = along(q0, dz=1)
-    qb = along(q0, dz=-1)
+    qa0 = along(q0, dz=1)
+    qb0 = along(q0, dz=-1)
+    qa1 = along(q1, dz=1)
+    qb1 = along(q1, dz=-1)
+    qc = along(qa0, dz=1)
+    qd = along(qb1, dz=-1)
     lpe = to_core(lp)
     lhe = to_core(lh)
-    qz = along(q0, dz=2)
     ku = lax.dynamic_slice(key_up, (0, x * 128), (D_LAT, 128))
     vu = lax.dynamic_slice(value_up, (0, x * 128), (D_LAT, 128))
 
     flops = 2 * NQ * NK * 512
-    near = [
-        ((1536, 256), BF), ((1536, 128), BF), ((512, NK), BF), ((256, NK), BF), ((8, 1536), F32),
-        ((NK, 256), BF), ((NK, 128), BF), ((64, 128), F32),
-    ]
-    qp, do, compt, kpt, qtag, kp, v, ktag, kp_here, v_here, ktag_here, stats = call(
+
+    def rows(n):
+        return [((n, 256), BF), ((n, 128), BF), ((8, n), F32)]
+
+    def at_hbm(shapes):
+        return [(*o, HB) for o in shapes]
+
+    def at_vmem(shapes):
+        return [pltpu.VMEM(*o) for o in shapes]
+
+    wide = [((512, NK), BF), ((256, NK), BF)]
+    keyed = [((NK, 256), BF), ((NK, 128), BF), ((64, 128), F32)]
+    qp0, do0, qtag0, compt, kpt, kp, v, ktag, *here, own_stats = call(
+        forward_own,
+        at_hbm(rows(512) + wide + keyed) + keyed + [((8, 512), F32)],
+        [(core[None], SM), q0, q1, pair, lp, lpe, lh, lhe, ku, vu],
+        scratch=at_vmem(rows(512) + wide) + [pltpu.SemaphoreType.DMA((6,)), pltpu.SemaphoreType.DMA((2,))],
+        flops=flops // 4, grant=20,
+    )
+    qp1, do1, qtag1, near_stats = call(
         forward_near,
-        [(*o, HB) for o in near] + near[5:8] + [((8, 1536), F32)],
-        [(core[None], SM), q0, qa, qb, pair, lp, lpe, lh, lhe, ku, vu],
-        scratch=[pltpu.VMEM(*o) for o in near[:5]] + [pltpu.SemaphoreType.DMA((6,)), pltpu.SemaphoreType.DMA((2,))],
-        flops=flops * 3 // 4, grant=20,
-    )
-    far = [((512, 256), BF), ((512, 128), BF), ((8, 512), F32)]
+        at_hbm(rows(1024)) + [((8, 1024), F32)],
+        [qa0, qa1, qb0, qb1, *here],
+        scratch=at_vmem(rows(1024)) + [pltpu.SemaphoreType.DMA((3,))],
+        flops=flops // 2, grant=14,
+    )
     qp2, do2, qtag2, stats = call(
         forward_far,
-        [(*o, HB) for o in far] + [((16, 512), F32)],
-        [qz, kp_here, v_here, ktag_here, stats],
-        scratch=[pltpu.VMEM(*o) for o in far] + [pltpu.VMEM((8, 512), F32), pltpu.SemaphoreType.DMA((3,))],
+        at_hbm(rows(512)) + [((16, 512), F32)],
+        [qc, qd, *here, own_stats, near_stats],
+        scratch=at_vmem(rows(512)) + [pltpu.VMEM((8, 512), F32), pltpu.SemaphoreType.DMA((3,))],
         flops=flops // 4, grant=12,
     )
+    s1 = along(stats, dz=-1)
     s3 = along(stats, dz=1)
-    s1 = along(stats, dz=-1)
     s2 = along(stats, dz=2)
 
-    there = [kp, ktag, qp, qtag, v, do, kpt, qp2, qtag2, do2, compt]
+    there = [kp, qp0, v, do0, ktag, qtag0, kpt, qp1, do1, qtag1, qp2, do2, qtag2, compt]
     pays = call(
         backward,
         [((768, 128), BF)] * 4 + [((640, 128), BF)] * 4 + [((8, 128, 128), BF)],
         [(a, HB) for a in there] + [stats, s1, s2, s3],
         scratch=[
             pltpu.VMEM((NK, 256), F32), pltpu.VMEM((NK, 128), F32), pltpu.VMEM((8, NQ), F32),
-            *[pltpu.VMEM(a.shape, a.dtype) for a in there], pltpu.SemaphoreType.DMA((11,)),
+            *[pltpu.VMEM(a.shape, a.dtype) for a in there], pltpu.SemaphoreType.DMA((14,)),
         ],
         flops=3 * flops, grant=24,
     )

time: 109 us -> 113 us (1.037)
  waiting for transfers between devices: 30.7 us -> 39.4 us
  starting transfers between devices: 53.4 us -> 49.3 us
    ppermute x20 -> x23, waiting for transfers between devices: 23.5 us -> 36.3 us  [along(): return lax.ppermute(value, 'seq', pairs)]
    ppermute x20 -> x23, starting transfers between devices: 39.1 us -> 33.7 us  [along(): return lax.ppermute(value, 'seq', pairs)]
    ppermute x2, waiting for transfers between devices: 1.42 us -> 0.01 us  [by_core(): return lax.ppermute(value, ('seq', 'head'), pairs)]
    all_to_all x1, waiting for transfers between devices: 4.42 us -> 3.07 us  [shards(): lax.all_to_all(up, 'seq', 0, 0, tiled=True, axis_index_groups=YZ_GROUPS)]
    ppermute x3, waiting for transfers between devices: 1.3 us -> 0.01 us  [to_core(): return lax.ppermute(value, 'head', [(0, 1), (1, 0), (2, 3), (3, 2)])]
    all_to_all x1, starting transfers between devices: 4.17 us -> 5.35 us  [shards(): whole = lax.all_to_all(every, 'seq', 0, 0, tiled=True)]
    pallas_call x9 -> x10, Pallas kernels: 23 us -> 22.4 us  [call(): pl.pallas_call(kernel, out_shape=[HB(o[0], o[1]) if o[2:] == (HB,) else j...]
  transfers between devices with their start and end apart: 28 -> 31, of which waited for: 17 -> 14; matrix products, arithmetic and copies ran while one was open for 1% -> 1% of each run, Pallas kernels for 8% -> 7%
where the time goes in v1:
time: 113 us
  starting transfers between devices  49.3 us (44%)
  waiting for transfers between devices  39.4 us (35%)
  Pallas kernels  22.4 us (20%)
    ppermute x23, waiting for transfers between devices, along(): return lax.ppermute(value, 'seq', pairs)  36.3 us
    ppermute x23, starting transfers between devices, along(): return lax.ppermute(value, 'seq', pairs)  33.7 us
    pallas_call x10, Pallas kernels, call(): pl.pallas_call(kernel, out_shape=[HB(o[0], o[1]) if o[2:] == (HB,) else j...  22.4 us
    all_to_all x1, starting transfers between devices, shards(): whole = lax.all_to_all(every, 'seq', 0, 0, tiled=True)  5.35 us
    all_to_all x1, starting transfers between devices, shards(): lax.all_to_all(up, 'seq', 0, 0, tiled=True, axis_index_groups=YZ_GROUPS)  3.97 us
    all_to_all x1, waiting for transfers between devices, shards(): lax.all_to_all(up, 'seq', 0, 0, tiled=True, axis_index_groups=YZ_GROUPS)  3.07 us
    ppermute x1, starting transfers between devices, shards(): far16 = lax.ppermute(two, 'head', [(0, 2), (1, 3), (2, 0), (3, 1)])  2.99 us
    ppermute x2, starting transfers between devices, by_core(): return lax.ppermute(value, ('seq', 'head'), pairs)  2.67 us
  transfers between devices with their start and end apart: 31, of which 14 were waited for; matrix products, arithmetic and copies ran while one was open for 1% of the time, Pallas kernels for 7%

profile of v1, /device:TPU:0, one launch (start us, length us, event | category | flops | bytes accessed | tf_op | source)
XLA Modules:
  0.0 112.9 jit_solution(12507434568598277801)
XLA Ops:
  0.6 1.3 %shard_map.93 = (bf16[336,128]{1,0:T(8,128)(2,1)S(1)}, bf16[336,128]{1,0:T(8,128)(2,1)S(1)}, bf16[336,128]{1,0:T(8,128)(2,1)S(1)}, bf16[336,128]{1,0:T(8,128)(2,1)S(1)}, bf16[592,128]{1,0:T(8,128)(2,1)S(1)}) custom-call(s32[128]{0:T(128)} %pos_hbm.1, s32[1]{0:T(128)} %bitcast.x, bf16[128,768]{1,0:T(8,128)(2,1)} %q_hbm.1, bf16[128,512]{1,0:T(8,128)(2,1)} %g_hbm.1, ...), custom_call_target="tpu_custom_call" | custom-call | flops 1 | bytes 1048576 | tf_op jit(solution)/shard_map/pallas_call | solution.py:64
  1.9 1.8 %collective-permute-start.3 = (bf16[592,128]{1,0:T(8,128)(2,1)S(1)}, bf16[592,128]{1,0:T(8,128)(2,1)S(1)}, u32[]{:S(2)}, u32[]{:S(2)}) collective-permute-start(bf16[592,128]{1,0:T(8,128)(2,1)S(1)} %get-tuple-element.50), channel_id=1, source_target_pairs={{0,64},{4,68},{8,72},{12,76},{16,80},{20,84},{24,88},{28,92},{32,9... | collective-permute-start | bytes 454664 | tf_op jit(solution)/shard_map/ppermute | solution.py:39
  3.7 3.9 %collective-permute-done.3 = bf16[592,128]{1,0:T(8,128)(2,1)S(1)} collective-permute-done((bf16[592,128]{1,0:T(8,128)(2,1)S(1)}, bf16[592,128]{1,0:T(8,128)(2,1)S(1)}, u32[]{:S(2)}, u32[]{:S(2)}) %collective-permute-start.3) | collective-permute-done | bytes 151584 | tf_op jit(solution)/shard_map/ppermute | solution.py:39
  7.6 1.7 %collective-permute-start.4 = (bf16[2,592,128]{2,1,0:T(8,128)(2,1)S(1)}, bf16[2,592,128]{2,1,0:T(8,128)(2,1)S(1)}, u32[]{:S(2)}, u32[]{:S(2)}) collective-permute-start(bf16[2,592,128]{2,1,0:T(8,128)(2,1)S(1)} %pad_maximum_fusion.pair), channel_id=1, source_target_pairs={{0,4},{1,13},{2,6},{3,15},{4,8},{5,1},{6,10},{7,3},{8,12},{9,5},{1... | collective-permute-start | bytes 909320 | tf_op jit(solution)/shard_map/ppermute | solution.py:50
  9.4 2.7 %collective-permute-start.1 = (bf16[336,128]{1,0:T(8,128)(2,1)S(1)}, bf16[336,128]{1,0:T(8,128)(2,1)S(1)}, u32[]{:S(2)}, u32[]{:S(2)}) collective-permute-start(bf16[336,128]{1,0:T(8,128)(2,1)S(1)} %get-tuple-element.48), channel_id=1, source_target_pairs={{0,8},{4,12},{8,0},{12,4},{16,24},{20,28},{24,16},{28,20},{32,40},... | collective-permute-start | bytes 258056 | tf_op jit(solution)/shard_map/ppermute | solution.py:39
  12.1 1.4 %collective-permute-start.2 = (bf16[336,128]{1,0:T(8,128)(2,1)S(1)}, bf16[336,128]{1,0:T(8,128)(2,1)S(1)}, u32[]{:S(2)}, u32[]{:S(2)}) collective-permute-start(bf16[336,128]{1,0:T(8,128)(2,1)S(1)} %get-tuple-element.49), channel_id=1, source_target_pairs={{0,12},{4,0},{8,4},{12,8},{16,28},{20,16},{24,20},{28,24},{32,44},... | collective-permute-start | bytes 258056 | tf_op jit(solution)/shard_map/ppermute | solution.py:39
  13.5 0.6 collective-permute-start
  14.2 0.9 collective-permute-start.6
  15.1 5.9 %collective-permute-done.1 = bf16[336,128]{1,0:T(8,128)(2,1)S(1)} collective-permute-done((bf16[336,128]{1,0:T(8,128)(2,1)S(1)}, bf16[336,128]{1,0:T(8,128)(2,1)S(1)}, u32[]{:S(2)}, u32[]{:S(2)}) %collective-permute-start.1) | collective-permute-done | bytes 86048 | tf_op jit(solution)/shard_map/ppermute | solution.py:39
  21.1 4.2 %collective-permute-start.11 = (bf16[2,336,128]{2,1,0:T(8,128)(2,1)S(1)}, bf16[2,336,128]{2,1,0:T(8,128)(2,1)S(1)}, u32[]{:S(2)}, u32[]{:S(2)}) collective-permute-start(bf16[2,336,128]{2,1,0:T(8,128)(2,1)S(1)} %pad_maximum_fusion.2.q1), channel_id=1, source_target_pairs={{0,48},{4,52},{8,56},{12,60},{16,0},{20,4},{24,8},{28,12},{32,16},... | collective-permute-start | bytes 516104 | tf_op jit(solution)/shard_map/ppermute | solution.py:39
  25.4 0.6 collective-permute-start.7
  26.0 2.2 %collective-permute-done.11.b1 = bf16[2,336,128]{2,1,0:T(8,128)(2,1)S(1)} collective-permute-done((bf16[2,336,128]{2,1,0:T(8,128)(2,1)S(1)}, bf16[2,336,128]{2,1,0:T(8,128)(2,1)S(1)}, u32[]{:S(2)}, u32[]{:S(2)}) %collective-permute-start.11) | collective-permute-done | bytes 172064 | tf_op jit(solution)/shard_map/ppermute | solution.py:39
  28.2 3.7 %collective-permute-start.10 = (bf16[2,336,128]{2,1,0:T(8,128)(2,1)S(1)}, bf16[2,336,128]{2,1,0:T(8,128)(2,1)S(1)}, u32[]{:S(2)}, u32[]{:S(2)}) collective-permute-start(bf16[2,336,128]{2,1,0:T(8,128)(2,1)S(1)} %pad_maximum_fusion.1.q0), channel_id=1, source_target_pairs={{0,48},{4,52},{8,56},{12,60},{16,0},{20,4},{24,8},{28,12},{32,16},... | collective-permute-start | bytes 516104 | tf_op jit(solution)/shard_map/ppermute | solution.py:39
  31.9 1.9 %collective-permute-done.8.a0 = bf16[2,336,128]{2,1,0:T(8,128)(2,1)S(1)} collective-permute-done((bf16[2,336,128]{2,1,0:T(8,128)(2,1)S(1)}, bf16[2,336,128]{2,1,0:T(8,128)(2,1)S(1)}, u32[]{:S(2)}, u32[]{:S(2)}) %collective-permute-start.8) | collective-permute-done | bytes 172064 | tf_op jit(solution)/shard_map/ppermute | solution.py:39
  33.9 2.0 %collective-permute-start.12 = (bf16[2,336,128]{2,1,0:T(8,128)(2,1)S(1)}, bf16[2,336,128]{2,1,0:T(8,128)(2,1)S(1)}, u32[]{:S(2)}, u32[]{:S(2)}) collective-permute-start(bf16[2,336,128]{2,1,0:T(8,128)(2,1)S(1)} %collective-permute-done.8.a0), channel_id=1, source_target_pairs={{0,16},{4,20},{8,24},{12,28},{16,32},{20,36},{24,40},{28,44},{32,4... | collective-permute-start | bytes 516104 | tf_op jit(solution)/shard_map/ppermute | solution.py:39
  35.9 2.4 %shard_map.94 = (bf16[512,256]{1,0:T(8,128)(2,1)}, bf16[512,128]{1,0:T(8,128)(2,1)}, f32[8,512]{1,0:T(8,128)}, bf16[512,1024]{1,0:T(8,128)(2,1)}, bf16[256,1024]...) custom-call(s32[1]{0:T(128)} %bitcast.1.core, ...), custom_call_target="tpu_custom_call" | custom-call | flops 536870912 | bytes 1048576 | tf_op jit(solution)/shard_map/pallas_call | solution.py:64
  38.3 3.0 %shard_map.95 = (bf16[1024,256]{1,0:T(8,128)(2,1)}, bf16[1024,128]{1,0:T(8,128)(2,1)}, f32[8,1024]{1,0:T(8,128)}, f32[8,1024]{1,0:T(8,128)S(1)}) custom-call(bf16[2,336,128]{2,1,0:T(8,128)(2,1)S(1)} %collective-permute-done.8.a0, bf16[2,336,128]{2,1,0:T(8,128)(2,1)S(1)} %collective-permute-done.9.a1, bf16[2,336,128]{2,1,0:T(8,128)(2,1)S(1)} %collective-permute-done.10.b0, ...), custom_call_target="tpu_custom_call" | custom-call | flops 1073741824 | bytes 1048576 | tf_op jit(solution)/shard_map/pallas_call | solution.py:64
  41.3 1.5 %shard_map.96 = (bf16[512,256]{1,0:T(8,128)(2,1)}, bf16[512,128]{1,0:T(8,128)(2,1)}, f32[8,512]{1,0:T(8,128)}, f32[16,512]{1,0:T(8,128)S(1)}) custom-call(bf16[2,336,128]{2,1,0:T(8,128)(2,1)S(1)} %collective-permute-done.12.qc, bf16[2,336,128]{2,1,0:T(8,128)(2,1)S(1)} %collective-permute-done.13.qd, bf16[1024,256]{1,0:T(8,128)(2,1)S(1)} %get-tuple-element.58.kp, ...), custom_call_target="tpu_custom_call" | custom-call | flops 536870912 | bytes 1048576 | tf_op jit(solution)/shard_map/pallas_call | solution.py:64
  42.9 1.7 %collective-permute-start.14 = (f32[16,512]{1,0:T(8,128)S(1)}, f32[16,512]{1,0:T(8,128)S(1)}, u32[]{:S(2)}, u32[]{:S(2)}) collective-permute-start(f32[16,512]{1,0:T(8,128)S(1)} %get-tuple-element.70.refs_14_), channel_id=1, source_target_pairs={{0,48},{4,52},{8,56},{12,60},{16,0},{20,4},{24,8},{28,12},{32,16},... | collective-permute-start | bytes 98312 | tf_op jit(solution)/shard_map/ppermute | solution.py:39
  44.6 0.5 collective-permute-start.15
  45.1 0.4 collective-permute-start.16
  45.5 1.4 %collective-permute-done.14.refs_15_ = f32[16,512]{1,0:T(8,128)S(1)} collective-permute-done((f32[16,512]{1,0:T(8,128)S(1)}, f32[16,512]{1,0:T(8,128)S(1)}, u32[]{:S(2)}, u32[]{:S(2)}) %collective-permute-start.14) | collective-permute-done | bytes 32800 | tf_op jit(solution)/shard_map/ppermute | solution.py:39
  46.9 3.1 %collective-permute-done.15.refs_16_ = f32[16,512]{1,0:T(8,128)S(1)} collective-permute-done((f32[16,512]{1,0:T(8,128)S(1)}, f32[16,512]{1,0:T(8,128)S(1)}, u32[]{:S(2)}, u32[]{:S(2)}) %collective-permute-start.15) | collective-permute-done | bytes 32800 | tf_op jit(solution)/shard_map/ppermute | solution.py:39
  50.0 0.3 collective-permute-done.16.refs_17_
  50.3 9.9 %shard_map.97 = (bf16[768,128]{1,0:T(8,128)(2,1)S(1)}, bf16[768,128]{1,0:T(8,128)(2,1)S(1)}, bf16[768,128]{1,0:T(8,128)(2,1)S(1)}, bf16[768,128]{1,0:T(8,128)(2,...) custom-call(bf16[1024,256]{1,0:T(8,128)(2,1)} %get-tuple-element.51., ...), custom_call_target="tpu_custom_call" | custom-call | flops 6442450944 | bytes 1048576 | tf_op jit(solution)/shard_map/pallas_call | solution.py:64
  60.3 3.1 %collective-permute-start.24 = (bf16[640,128]{1,0:T(8,128)(2,1)S(1)}, bf16[640,128]{1,0:T(8,128)(2,1)S(1)}, u32[]{:S(2)}, u32[]{:S(2)}) collective-permute-start(bf16[640,128]{1,0:T(8,128)(2,1)S(1)} %get-tuple-element.81), channel_id=1, source_target_pairs={{0,8},{4,12},{8,0},{12,4},{16,24},{20,28},{24,16},{28,20},{32,40},... | collective-permute-start | bytes 491528 | tf_op jit(solution)/shard_map/ppermute | solution.py:39
  63.7 4.0 %all-to-all-start = ((bf16[8,128,128]{2,1,0:T(8,128)(2,1)}), bf16[8,128,128]{2,1,0:T(8,128)(2,1)S(1)}, u32[]{:S(2)}, u32[]{:S(2)}) async-start(bf16[8,128,128]{2,1,0:T(8,128)(2,1)} %get-tuple-element.85), calls=%async_computation | async-start | bytes 524288 | tf_op jit(solution)/shard_map/all_to_all | solution.py:422
  67.7 0.9 collective-permute-done.23.x1
  68.6 0.9 collective-permute-done.25.x3
  69.5 0.7 shard_map.100
  70.2 1.7 %collective-permute-start.26 = (bf16[576,128]{1,0:T(8,128)(2,1)S(1)}, bf16[576,128]{1,0:T(8,128)(2,1)S(1)}, u32[]{:S(2)}, u32[]{:S(2)}) collective-permute-start(bf16[576,128]{1,0:T(8,128)(2,1)S(1)} %get-tuple-element.84), channel_id=1, source_target_pairs={{0,64},{4,68},{8,72},{12,76},{16,80},{20,84},{24,88},{28,92},{32,9... | collective-permute-start | bytes 442376 | tf_op jit(solution)/shard_map/ppermute | solution.py:39
  71.8 3.1 %all-to-all-done.parts = bf16[8,128,128]{2,1,0:T(8,128)(2,1)S(1)} async-done(((bf16[8,128,128]{2,1,0:T(8,128)(2,1)}), bf16[8,128,128]{2,1,0:T(8,128)(2,1)S(1)}, u32[]{:S(2)}, u32[]{:S(2)}) %all-to-all-start) | async-done | bytes 262176 | tf_op jit(solution)/shard_map/all_to_all | solution.py:422
  74.9 1.1 shard_map.101
  76.0 5.4 %all-to-all-start.1 = ((bf16[32,128,128]{2,1,0:T(8,128)(2,1)}), bf16[32,128,128]{2,1,0:T(8,128)(2,1)S(1)}, u32[]{:S(2)}, u32[]{:S(2)}) async-start(bf16[32,128,128]{2,1,0:T(8,128)(2,1)} %shard_map.101), calls=%async_computation.1 | async-start | bytes 2097152 | tf_op jit(solution)/shard_map/all_to_all | solution.py:433
  81.5 1.9 %collective-permute-start.17 = (bf16[768,128]{1,0:T(8,128)(2,1)S(1)}, bf16[768,128]{1,0:T(8,128)(2,1)S(1)}, u32[]{:S(2)}, u32[]{:S(2)}) collective-permute-start(bf16[768,128]{1,0:T(8,128)(2,1)S(1)} %get-tuple-element.72), channel_id=1, source_target_pairs={{0,16},{4,20},{8,24},{12,28},{16,32},{20,36},{24,40},{28,44},{32,4... | collective-permute-start | bytes 589832 | tf_op jit(solution)/shard_map/ppermute | solution.py:39
  83.4 2.7 %collective-permute-start.18 = (bf16[768,128]{1,0:T(8,128)(2,1)S(1)}, bf16[768,128]{1,0:T(8,128)(2,1)S(1)}, u32[]{:S(2)}, u32[]{:S(2)}) collective-permute-start(bf16[768,128]{1,0:T(8,128)(2,1)S(1)} %get-tuple-element.73), channel_id=1, source_target_pairs={{0,32},{4,36},{8,40},{12,44},{16,48},{20,52},{24,56},{28,60},{32,0... | collective-permute-start | bytes 589832 | tf_op jit(solution)/shard_map/ppermute | solution.py:39
  86.1 1.5 %collective-permute-start.19 = (bf16[768,128]{1,0:T(8,128)(2,1)S(1)}, bf16[768,128]{1,0:T(8,128)(2,1)S(1)}, u32[]{:S(2)}, u32[]{:S(2)}) collective-permute-start(bf16[768,128]{1,0:T(8,128)(2,1)S(1)} %get-tuple-element.74), channel_id=1, source_target_pairs={{0,48},{4,52},{8,56},{12,60},{16,0},{20,4},{24,8},{28,12},{32,16},... | collective-permute-start | bytes 589832 | tf_op jit(solution)/shard_map/ppermute | solution.py:39
  87.6 3.0 %collective-permute-start.28 = (bf16[576,128]{1,0:T(8,128)(2,1)S(1)}, bf16[576,128]{1,0:T(8,128)(2,1)S(1)}, u32[]{:S(2)}, u32[]{:S(2)}) collective-permute-start(bf16[576,128]{1,0:T(8,128)(2,1)S(1)} %reduce-precision_convert_fusion), channel_id=1, source_target_pairs={{0,2},{1,3},{2,0},{3,1},{4,6},{5,7},{6,4},{7,5},{8,10},{9,11},{10,... | collective-permute-start | bytes 442376 | tf_op jit(solution)/shard_map/ppermute | solution.py:441
  90.6 11.1 %collective-permute-done.17.z1 = bf16[768,128]{1,0:T(8,128)(2,1)S(1)} collective-permute-done((bf16[768,128]{1,0:T(8,128)(2,1)S(1)}, bf16[768,128]{1,0:T(8,128)(2,1)S(1)}, u32[]{:S(2)}, u32[]{:S(2)}) %collective-permute-start.17) | collective-permute-done | bytes 196640 | tf_op jit(solution)/shard_map/ppermute | solution.py:39
  101.8 1.6 %collective-permute-start.20 = (bf16[192,128]{1,0:T(8,128)(2,1)S(1)}, bf16[192,128]{1,0:T(8,128)(2,1)S(1)}, u32[]{:S(2)}, u32[]{:S(2)}) collective-permute-start(bf16[192,128]{1,0:T(8,128)(2,1)S(1)} %get-tuple-element.76), channel_id=1, source_target_pairs={{0,12},{4,0},{8,4},{12,8},{16,28},{20,16},{24,20},{28,24},{32,44},... | collective-permute-start | bytes 147464 | tf_op jit(solution)/shard_map/ppermute | solution.py:39
  103.4 1.0 collective-permute-start.21
  104.4 0.8 collective-permute-start.22
  105.2 1.0 collective-permute-done.20.q1
  106.2 2.8 %collective-permute-done.21.q2 = bf16[192,128]{1,0:T(8,128)(2,1)S(1)} collective-permute-done((bf16[192,128]{1,0:T(8,128)(2,1)S(1)}, bf16[192,128]{1,0:T(8,128)(2,1)S(1)}, u32[]{:S(2)}, u32[]{:S(2)}) %collective-permute-start.21) | collective-permute-done | bytes 49184 | tf_op jit(solution)/shard_map/ppermute | solution.py:39
  109.0 0.7 collective-permute-done.22.q3
  109.7 0.9 shard_map.99
  110.6 0.7 add_bitcast_fusion
  111.3 1.5 %shard_map.102 = (f32[512,512]{1,0:T(8,128)}, f32[512,512]{1,0:T(8,128)}) custom-call(bf16[32,128,128]{2,1,0:T(8,128)(2,1)S(1)} %all-to-all-done.1.a), custom_call_target="tpu_custom_call" | custom-call | flops 1 | bytes 1048576 | tf_op jit(solution)/shard_map/pallas_call | solution.py:64
  (36 shorter events, 1.0 us)
Async XLA Ops:
  1.9 5.7 %collective-permute-start.3 = (bf16[592,128]{1,0:T(8,128)(2,1)S(1)}, bf16[592,128]{1,0:T(8,128)(2,1)S(1)}, u32[]{:S(2)}, u32[]{:S(2)}) collective-permute-start(bf16[592,128]{1,0:T(8,128)(2,1)S(1)} %get-tuple-element.50), channel_id=1, source_target_pairs={{0,64},{4,68},{8,72},{12,76},{16,80},{20,84},{24,88},{28,92},{32,9... | collective-permute-start | bytes 454664 | tf_op jit(solution)/shard_map/ppermute | solution.py:39
  7.6 17.7 %collective-permute-start.4 = (bf16[2,592,128]{2,1,0:T(8,128)(2,1)S(1)}, bf16[2,592,128]{2,1,0:T(8,128)(2,1)S(1)}, u32[]{:S(2)}, u32[]{:S(2)}) collective-permute-start(bf16[2,592,128]{2,1,0:T(8,128)(2,1)S(1)} %pad_maximum_fusion.pair), channel_id=1, source_target_pairs={{0,4},{1,13},{2,6},{3,15},{4,8},{5,1},{6,10},{7,3},{8,12},{9,5},{1... | collective-permute-start | bytes 909320 | tf_op jit(solution)/shard_map/ppermute | solution.py:50
  9.4 11.7 %collective-permute-start.1 = (bf16[336,128]{1,0:T(8,128)(2,1)S(1)}, bf16[336,128]{1,0:T(8,128)(2,1)S(1)}, u32[]{:S(2)}, u32[]{:S(2)}) collective-permute-start(bf16[336,128]{1,0:T(8,128)(2,1)S(1)} %get-tuple-element.48), channel_id=1, source_target_pairs={{0,8},{4,12},{8,0},{12,4},{16,24},{20,28},{24,16},{28,20},{32,40},... | collective-permute-start | bytes 258056 | tf_op jit(solution)/shard_map/ppermute | solution.py:39
  12.1 9.0 %collective-permute-start.2 = (bf16[336,128]{1,0:T(8,128)(2,1)S(1)}, bf16[336,128]{1,0:T(8,128)(2,1)S(1)}, u32[]{:S(2)}, u32[]{:S(2)}) collective-permute-start(bf16[336,128]{1,0:T(8,128)(2,1)S(1)} %get-tuple-element.49), channel_id=1, source_target_pairs={{0,12},{4,0},{8,4},{12,8},{16,28},{20,16},{24,20},{28,24},{32,44},... | collective-permute-start | bytes 258056 | tf_op jit(solution)/shard_map/ppermute | solution.py:39
  13.5 11.8 %collective-permute-start = (bf16[336,128]{1,0:T(8,128)(2,1)S(1)}, bf16[336,128]{1,0:T(8,128)(2,1)S(1)}, u32[]{:S(2)}, u32[]{:S(2)}) collective-permute-start(bf16[336,128]{1,0:T(8,128)(2,1)S(1)} %get-tuple-element.47), channel_id=1, source_target_pairs={{0,4},{4,8},{8,12},{12,0},{16,20},{20,24},{24,28},{28,16},{32,36},... | collective-permute-start | bytes 258056 | tf_op jit(solution)/shard_map/ppermute | solution.py:39
  14.1 21.8 %copy-start = (bf16[512,512]{1,0:T(8,128)(2,1)S(1)}, bf16[512,512]{1,0:T(8,128)(2,1)}, u32[]{:S(2)}) copy-start(bf16[512,512]{1,0:T(8,128)(2,1)} %vu.1) | copy-start | bytes 1572868
  14.1 21.8 %copy-start.1 = (bf16[512,512]{1,0:T(8,128)(2,1)S(1)}, bf16[512,512]{1,0:T(8,128)(2,1)}, u32[]{:S(2)}) copy-start(bf16[512,512]{1,0:T(8,128)(2,1)} %ku.1) | copy-start | bytes 1572868
  14.2 11.2 %collective-permute-start.6 = (bf16[592,128]{1,0:T(8,128)(2,1)S(1)}, bf16[592,128]{1,0:T(8,128)(2,1)S(1)}, u32[]{:S(2)}, u32[]{:S(2)}) collective-permute-start(bf16[592,128]{1,0:T(8,128)(2,1)S(1)} %fusion.1), channel_id=1, source_target_pairs={{0,8},{1,9},{2,10},{3,11},{4,12},{5,13},{6,14},{7,15},{8,0},{9,1},... | collective-permute-start | bytes 454664 | tf_op jit(solution)/shard_map/ppermute | solution.py:50
  21.1 7.1 %collective-permute-start.11 = (bf16[2,336,128]{2,1,0:T(8,128)(2,1)S(1)}, bf16[2,336,128]{2,1,0:T(8,128)(2,1)S(1)}, u32[]{:S(2)}, u32[]{:S(2)}) collective-permute-start(bf16[2,336,128]{2,1,0:T(8,128)(2,1)S(1)} %pad_maximum_fusion.2.q1), channel_id=1, source_target_pairs={{0,48},{4,52},{8,56},{12,60},{16,0},{20,4},{24,8},{28,12},{32,16},... | collective-permute-start | bytes 516104 | tf_op jit(solution)/shard_map/ppermute | solution.py:39
  25.3 10.6 %collective-permute-start.5 = (bf16[2,592,128]{2,1,0:T(8,128)(2,1)S(1)}, bf16[2,592,128]{2,1,0:T(8,128)(2,1)S(1)}, u32[]{:S(2)}, u32[]{:S(2)}) collective-permute-start(bf16[2,592,128]{2,1,0:T(8,128)(2,1)S(1)} %collective-permute-done.4.lp), channel_id=1, source_target_pairs={{0,1},{1,0},{2,3},{3,2},{4,5},{5,4},{6,7},{7,6},{8,9},{9,8},{10,11... | collective-permute-start | bytes 909320 | tf_op jit(solution)/shard_map/ppermute | solution.py:54
  25.3 8.5 %collective-permute-start.8 = (bf16[2,336,128]{2,1,0:T(8,128)(2,1)S(1)}, bf16[2,336,128]{2,1,0:T(8,128)(2,1)S(1)}, u32[]{:S(2)}, u32[]{:S(2)}) collective-permute-start(bf16[2,336,128]{2,1,0:T(8,128)(2,1)S(1)} %pad_maximum_fusion.1.q0), channel_id=1, source_target_pairs={{0,16},{4,20},{8,24},{12,28},{16,32},{20,36},{24,40},{28,44},{32,4... | collective-permute-start | bytes 516104 | tf_op jit(solution)/shard_map/ppermute | solution.py:39
  25.4 8.4 %collective-permute-start.7 = (bf16[592,128]{1,0:T(8,128)(2,1)S(1)}, bf16[592,128]{1,0:T(8,128)(2,1)S(1)}, u32[]{:S(2)}, u32[]{:S(2)}) collective-permute-start(bf16[592,128]{1,0:T(8,128)(2,1)S(1)} %collective-permute-done.6.lh), channel_id=1, source_target_pairs={{0,1},{1,0},{2,3},{3,2},{4,5},{5,4},{6,7},{7,6},{8,9},{9,8},{10,11... | collective-permute-start | bytes 454664 | tf_op jit(solution)/shard_map/ppermute | solution.py:54
  26.0 12.3 %collective-permute-start.9 = (bf16[2,336,128]{2,1,0:T(8,128)(2,1)S(1)}, bf16[2,336,128]{2,1,0:T(8,128)(2,1)S(1)}, u32[]{:S(2)}, u32[]{:S(2)}) collective-permute-start(bf16[2,336,128]{2,1,0:T(8,128)(2,1)S(1)} %pad_maximum_fusion.2.q1), channel_id=1, source_target_pairs={{0,16},{4,20},{8,24},{12,28},{16,32},{20,36},{24,40},{28,44},{32,4... | collective-permute-start | bytes 516104 | tf_op jit(solution)/shard_map/ppermute | solution.py:39
  28.2 10.1 %collective-permute-start.10 = (bf16[2,336,128]{2,1,0:T(8,128)(2,1)S(1)}, bf16[2,336,128]{2,1,0:T(8,128)(2,1)S(1)}, u32[]{:S(2)}, u32[]{:S(2)}) collective-permute-start(bf16[2,336,128]{2,1,0:T(8,128)(2,1)S(1)} %pad_maximum_fusion.1.q0), channel_id=1, source_target_pairs={{0,48},{4,52},{8,56},{12,60},{16,0},{20,4},{24,8},{28,12},{32,16},... | collective-permute-start | bytes 516104 | tf_op jit(solution)/shard_map/ppermute | solution.py:39
  33.9 7.5 %collective-permute-start.13 = (bf16[2,336,128]{2,1,0:T(8,128)(2,1)S(1)}, bf16[2,336,128]{2,1,0:T(8,128)(2,1)S(1)}, u32[]{:S(2)}, u32[]{:S(2)}) collective-permute-start(bf16[2,336,128]{2,1,0:T(8,128)(2,1)S(1)} %collective-permute-done.11.b1), channel_id=1, source_target_pairs={{0,48},{4,52},{8,56},{12,60},{16,0},{20,4},{24,8},{28,12},{32,16},... | collective-permute-start | bytes 516104 | tf_op jit(solution)/shard_map/ppermute | solution.py:39
  33.9 7.5 %collective-permute-start.12 = (bf16[2,336,128]{2,1,0:T(8,128)(2,1)S(1)}, bf16[2,336,128]{2,1,0:T(8,128)(2,1)S(1)}, u32[]{:S(2)}, u32[]{:S(2)}) collective-permute-start(bf16[2,336,128]{2,1,0:T(8,128)(2,1)S(1)} %collective-permute-done.8.a0), channel_id=1, source_target_pairs={{0,16},{4,20},{8,24},{12,28},{16,32},{20,36},{24,40},{28,44},{32,4... | collective-permute-start | bytes 516104 | tf_op jit(solution)/shard_map/ppermute | solution.py:39
  42.9 4.0 %collective-permute-start.14 = (f32[16,512]{1,0:T(8,128)S(1)}, f32[16,512]{1,0:T(8,128)S(1)}, u32[]{:S(2)}, u32[]{:S(2)}) collective-permute-start(f32[16,512]{1,0:T(8,128)S(1)} %get-tuple-element.70.refs_14_), channel_id=1, source_target_pairs={{0,48},{4,52},{8,56},{12,60},{16,0},{20,4},{24,8},{28,12},{32,16},... | collective-permute-start | bytes 98312 | tf_op jit(solution)/shard_map/ppermute | solution.py:39
  44.6 5.4 %collective-permute-start.15 = (f32[16,512]{1,0:T(8,128)S(1)}, f32[16,512]{1,0:T(8,128)S(1)}, u32[]{:S(2)}, u32[]{:S(2)}) collective-permute-start(f32[16,512]{1,0:T(8,128)S(1)} %get-tuple-element.70.refs_14_), channel_id=1, source_target_pairs={{0,32},{4,36},{8,40},{12,44},{16,48},{20,52},{24,56},{28,60},{32,0... | collective-permute-start | bytes 98312 | tf_op jit(solution)/shard_map/ppermute | solution.py:39
  45.1 5.3 %collective-permute-start.16 = (f32[16,512]{1,0:T(8,128)S(1)}, f32[16,512]{1,0:T(8,128)S(1)}, u32[]{:S(2)}, u32[]{:S(2)}) collective-permute-start(f32[16,512]{1,0:T(8,128)S(1)} %get-tuple-element.70.refs_14_), channel_id=1, source_target_pairs={{0,16},{4,20},{8,24},{12,28},{16,32},{20,36},{24,40},{28,44},{32,4... | collective-permute-start | bytes 98312 | tf_op jit(solution)/shard_map/ppermute | solution.py:39
  60.2 8.4 %collective-permute-start.23 = (bf16[640,128]{1,0:T(8,128)(2,1)S(1)}, bf16[640,128]{1,0:T(8,128)(2,1)S(1)}, u32[]{:S(2)}, u32[]{:S(2)}) collective-permute-start(bf16[640,128]{1,0:T(8,128)(2,1)S(1)} %get-tuple-element.80), channel_id=1, source_target_pairs={{0,4},{4,8},{8,12},{12,0},{16,20},{20,24},{24,28},{28,16},{32,36},... | collective-permute-start | bytes 491528 | tf_op jit(solution)/shard_map/ppermute | solution.py:39
  60.3 8.3 %collective-permute-start.24 = (bf16[640,128]{1,0:T(8,128)(2,1)S(1)}, bf16[640,128]{1,0:T(8,128)(2,1)S(1)}, u32[]{:S(2)}, u32[]{:S(2)}) collective-permute-start(bf16[640,128]{1,0:T(8,128)(2,1)S(1)} %get-tuple-element.81), channel_id=1, source_target_pairs={{0,8},{4,12},{8,0},{12,4},{16,24},{20,28},{24,16},{28,20},{32,40},... | collective-permute-start | bytes 491528 | tf_op jit(solution)/shard_map/ppermute | solution.py:39
  63.4 6.1 %collective-permute-start.25 = (bf16[640,128]{1,0:T(8,128)(2,1)S(1)}, bf16[640,128]{1,0:T(8,128)(2,1)S(1)}, u32[]{:S(2)}, u32[]{:S(2)}) collective-permute-start(bf16[640,128]{1,0:T(8,128)(2,1)S(1)} %get-tuple-element.82), channel_id=1, source_target_pairs={{0,12},{4,0},{8,4},{12,8},{16,28},{20,16},{24,20},{28,24},{32,44},... | collective-permute-start | bytes 491528 | tf_op jit(solution)/shard_map/ppermute | solution.py:39
  63.7 11.2 %all-to-all-start = ((bf16[8,128,128]{2,1,0:T(8,128)(2,1)}), bf16[8,128,128]{2,1,0:T(8,128)(2,1)S(1)}, u32[]{:S(2)}, u32[]{:S(2)}) async-start(bf16[8,128,128]{2,1,0:T(8,128)(2,1)} %get-tuple-element.85), calls=%async_computation | async-start | bytes 524288 | tf_op jit(solution)/shard_map/all_to_all | solution.py:422
  70.2 11.2 %collective-permute-start.26 = (bf16[576,128]{1,0:T(8,128)(2,1)S(1)}, bf16[576,128]{1,0:T(8,128)(2,1)S(1)}, u32[]{:S(2)}, u32[]{:S(2)}) collective-permute-start(bf16[576,128]{1,0:T(8,128)(2,1)S(1)} %get-tuple-element.84), channel_id=1, source_target_pairs={{0,64},{4,68},{8,72},{12,76},{16,80},{20,84},{24,88},{28,92},{32,9... | collective-permute-start | bytes 442376 | tf_op jit(solution)/shard_map/ppermute | solution.py:39
  76.0 35.3 %all-to-all-start.1 = ((bf16[32,128,128]{2,1,0:T(8,128)(2,1)}), bf16[32,128,128]{2,1,0:T(8,128)(2,1)S(1)}, u32[]{:S(2)}, u32[]{:S(2)}) async-start(bf16[32,128,128]{2,1,0:T(8,128)(2,1)} %shard_map.101), calls=%async_computation.1 | async-start | bytes 2097152 | tf_op jit(solution)/shard_map/all_to_all | solution.py:433
  81.4 6.1 %collective-permute-start.27 = (bf16[576,128]{1,0:T(8,128)(2,1)S(1)}, bf16[576,128]{1,0:T(8,128)(2,1)S(1)}, u32[]{:S(2)}, u32[]{:S(2)}) collective-permute-start(bf16[576,128]{1,0:T(8,128)(2,1)S(1)} %reduce-precision_convert_fusion.1), channel_id=1, source_target_pairs={{0,1},{1,0},{2,3},{3,2},{4,5},{5,4},{6,7},{7,6},{8,9},{9,8},{10,11... | collective-permute-start | bytes 442376 | tf_op jit(solution)/shard_map/ppermute | solution.py:54
  81.5 20.1 %collective-permute-start.17 = (bf16[768,128]{1,0:T(8,128)(2,1)S(1)}, bf16[768,128]{1,0:T(8,128)(2,1)S(1)}, u32[]{:S(2)}, u32[]{:S(2)}) collective-permute-start(bf16[768,128]{1,0:T(8,128)(2,1)S(1)} %get-tuple-element.72), channel_id=1, source_target_pairs={{0,16},{4,20},{8,24},{12,28},{16,32},{20,36},{24,40},{28,44},{32,4... | collective-permute-start | bytes 589832 | tf_op jit(solution)/shard_map/ppermute | solution.py:39
  83.4 18.3 %collective-permute-start.18 = (bf16[768,128]{1,0:T(8,128)(2,1)S(1)}, bf16[768,128]{1,0:T(8,128)(2,1)S(1)}, u32[]{:S(2)}, u32[]{:S(2)}) collective-permute-start(bf16[768,128]{1,0:T(8,128)(2,1)S(1)} %get-tuple-element.73), channel_id=1, source_target_pairs={{0,32},{4,36},{8,40},{12,44},{16,48},{20,52},{24,56},{28,60},{32,0... | collective-permute-start | bytes 589832 | tf_op jit(solution)/shard_map/ppermute | solution.py:39
  86.1 15.6 %collective-permute-start.19 = (bf16[768,128]{1,0:T(8,128)(2,1)S(1)}, bf16[768,128]{1,0:T(8,128)(2,1)S(1)}, u32[]{:S(2)}, u32[]{:S(2)}) collective-permute-start(bf16[768,128]{1,0:T(8,128)(2,1)S(1)} %get-tuple-element.74), channel_id=1, source_target_pairs={{0,48},{4,52},{8,56},{12,60},{16,0},{20,4},{24,8},{28,12},{32,16},... | collective-permute-start | bytes 589832 | tf_op jit(solution)/shard_map/ppermute | solution.py:39
  87.6 23.0 %collective-permute-start.28 = (bf16[576,128]{1,0:T(8,128)(2,1)S(1)}, bf16[576,128]{1,0:T(8,128)(2,1)S(1)}, u32[]{:S(2)}, u32[]{:S(2)}) collective-permute-start(bf16[576,128]{1,0:T(8,128)(2,1)S(1)} %reduce-precision_convert_fusion), channel_id=1, source_target_pairs={{0,2},{1,3},{2,0},{3,1},{4,6},{5,7},{6,4},{7,5},{8,10},{9,11},{10,... | collective-permute-start | bytes 442376 | tf_op jit(solution)/shard_map/ppermute | solution.py:441
  101.8 4.4 %collective-permute-start.20 = (bf16[192,128]{1,0:T(8,128)(2,1)S(1)}, bf16[192,128]{1,0:T(8,128)(2,1)S(1)}, u32[]{:S(2)}, u32[]{:S(2)}) collective-permute-start(bf16[192,128]{1,0:T(8,128)(2,1)S(1)} %get-tuple-element.76), channel_id=1, source_target_pairs={{0,12},{4,0},{8,4},{12,8},{16,28},{20,16},{24,20},{28,24},{32,44},... | collective-permute-start | bytes 147464 | tf_op jit(solution)/shard_map/ppermute | solution.py:39
  103.4 5.6 %collective-permute-start.21 = (bf16[192,128]{1,0:T(8,128)(2,1)S(1)}, bf16[192,128]{1,0:T(8,128)(2,1)S(1)}, u32[]{:S(2)}, u32[]{:S(2)}) collective-permute-start(bf16[192,128]{1,0:T(8,128)(2,1)S(1)} %get-tuple-element.77), channel_id=1, source_target_pairs={{0,8},{4,12},{8,0},{12,4},{16,24},{20,28},{24,16},{28,20},{32,40},... | collective-permute-start | bytes 147464 | tf_op jit(solution)/shard_map/ppermute | solution.py:39
  104.4 5.3 %collective-permute-start.22 = (bf16[192,128]{1,0:T(8,128)(2,1)S(1)}, bf16[192,128]{1,0:T(8,128)(2,1)S(1)}, u32[]{:S(2)}, u32[]{:S(2)}) collective-permute-start(bf16[192,128]{1,0:T(8,128)(2,1)S(1)} %get-tuple-element.78), channel_id=1, source_target_pairs={{0,4},{4,8},{8,12},{12,0},{16,20},{20,24},{24,28},{28,16},{32,36},... | collective-permute-start | bytes 147464 | tf_op jit(solution)/shard_map/ppermute | solution.py:39

commit v2 on v1

--- a/solution.py
+++ b/solution.py
@@ -160,8 +160,8 @@
     lax.fori_loop(0, rows // TQ, turn, 0)
 
 
-def copied(pairs, sems):
-    copies = [pltpu.make_async_copy(src, dst, sems.at[n]) for n, (src, dst) in enumerate(pairs)]
+def copied(pairs, sems, first=0):
+    copies = [pltpu.make_async_copy(src, dst, sems.at[first + n]) for n, (src, dst) in enumerate(pairs)]
     for copy in copies:
         copy.start()
     return copies
@@ -226,7 +226,8 @@
     there, stats, zpay, xpay, up = refs[:14], refs[14:18], refs[18:22], refs[22:26], refs[26]
     (dk, dv, low), here, sems = refs[27:30], refs[30:44], refs[44]
     kp, qp0, v, do0, ktag, qtag0, kpt, qp1, do1, qtag1, qp2, do2, qtag2, compt = here
-    copies = copied(list(zip(there, here)), sems)
+    pairs = list(zip(there, here))
+    copies = copied(pairs[:6], sems)
     late = lateness()
     for r in range(4):
         rows = []
@@ -241,8 +242,9 @@
         low[1:2, at : at + 512] = weighted / total
     dk[...] = jnp.zeros_like(dk)
     dv[...] = jnp.zeros_like(dv)
-    for copy in copies[:7]:
+    for copy in copies:
         copy.wait()
+    copies += copied(pairs[6:], sems, 6)
     ktags = [ktag[8 * n : 8 * n + 1] for n in range(8)]
     for r in (0, 1, 3, 2):
         if r == 1:
@@ -263,6 +265,8 @@
             ds = (p * (dp - low[1:2, to : to + TQ])).astype(BF)
             dk[...] += mm(ds, q, NN)
             dv[...] += mm(p.astype(BF), g, NN)
+            if to == 0:
+                copies[6].wait()
             dq = (mm(kpt[...], ds, NN).T * SCALE).astype(BF)
             for b in range(2):
                 m = 2 * i + b

time: 113 us -> 113 us (level)
  no operation moved by 1% of the time
where the time goes in v2:
time: 113 us
  starting transfers between devices  49.3 us (44%)
  waiting for transfers between devices  39.4 us (35%)
  Pallas kernels  22.4 us (20%)
    ppermute x23, waiting for transfers between devices, along(): return lax.ppermute(value, 'seq', pairs)  36.3 us
    ppermute x23, starting transfers between devices, along(): return lax.ppermute(value, 'seq', pairs)  33.7 us
    pallas_call x10, Pallas kernels, call(): pl.pallas_call(kernel, out_shape=[HB(o[0], o[1]) if o[2:] == (HB,) else j...  22.4 us
    all_to_all x1, starting transfers between devices, shards(): whole = lax.all_to_all(every, 'seq', 0, 0, tiled=True)  5.35 us
    all_to_all x1, starting transfers between devices, shards(): lax.all_to_all(up, 'seq', 0, 0, tiled=True, axis_index_groups=YZ_GROUPS)  3.97 us
    all_to_all x1, waiting for transfers between devices, shards(): lax.all_to_all(up, 'seq', 0, 0, tiled=True, axis_index_groups=YZ_GROUPS)  3.07 us
    ppermute x1, starting transfers between devices, shards(): far16 = lax.ppermute(two, 'head', [(0, 2), (1, 3), (2, 0), (3, 1)])  2.99 us
    ppermute x2, starting transfers between devices, by_core(): return lax.ppermute(value, ('seq', 'head'), pairs)  2.67 us
  transfers between devices with their start and end apart: 31, of which 14 were waited for; matrix products, arithmetic and copies ran while one was open for 1% of the time, Pallas kernels for 7%

profile of v2, /device:TPU:0, one launch (start us, length us, event | category | flops | bytes accessed | tf_op | source)
XLA Modules:
  0.0 112.9 jit_solution(12845569967061219438)
XLA Ops:
  0.6 1.3 %shard_map.93 = (bf16[336,128]{1,0:T(8,128)(2,1)S(1)}, bf16[336,128]{1,0:T(8,128)(2,1)S(1)}, bf16[336,128]{1,0:T(8,128)(2,1)S(1)}, bf16[336,128]{1,0:T(8,128)(2,1)S(1)}, bf16[592,128]{1,0:T(8,128)(2,1)S(1)}) custom-call(s32[128]{0:T(128)} %pos_hbm.1, s32[1]{0:T(128)} %bitcast.x, bf16[128,768]{1,0:T(8,128)(2,1)} %q_hbm.1, bf16[128,512]{1,0:T(8,128)(2,1)} %g_hbm.1, ...), custom_call_target="tpu_custom_call" | custom-call | flops 1 | bytes 1048576 | tf_op jit(solution)/shard_map/pallas_call | solution.py:64
  1.9 1.8 %collective-permute-start.3 = (bf16[592,128]{1,0:T(8,128)(2,1)S(1)}, bf16[592,128]{1,0:T(8,128)(2,1)S(1)}, u32[]{:S(2)}, u32[]{:S(2)}) collective-permute-start(bf16[592,128]{1,0:T(8,128)(2,1)S(1)} %get-tuple-element.50), channel_id=1, source_target_pairs={{0,64},{4,68},{8,72},{12,76},{16,80},{20,84},{24,88},{28,92},{32,9... | collective-permute-start | bytes 454664 | tf_op jit(solution)/shard_map/ppermute | solution.py:39
  3.7 3.9 %collective-permute-done.3 = bf16[592,128]{1,0:T(8,128)(2,1)S(1)} collective-permute-done((bf16[592,128]{1,0:T(8,128)(2,1)S(1)}, bf16[592,128]{1,0:T(8,128)(2,1)S(1)}, u32[]{:S(2)}, u32[]{:S(2)}) %collective-permute-start.3) | collective-permute-done | bytes 151584 | tf_op jit(solution)/shard_map/ppermute | solution.py:39
  7.6 1.7 %collective-permute-start.4 = (bf16[2,592,128]{2,1,0:T(8,128)(2,1)S(1)}, bf16[2,592,128]{2,1,0:T(8,128)(2,1)S(1)}, u32[]{:S(2)}, u32[]{:S(2)}) collective-permute-start(bf16[2,592,128]{2,1,0:T(8,128)(2,1)S(1)} %pad_maximum_fusion.pair), channel_id=1, source_target_pairs={{0,4},{1,13},{2,6},{3,15},{4,8},{5,1},{6,10},{7,3},{8,12},{9,5},{1... | collective-permute-start | bytes 909320 | tf_op jit(solution)/shard_map/ppermute | solution.py:50
  9.4 2.7 %collective-permute-start.1 = (bf16[336,128]{1,0:T(8,128)(2,1)S(1)}, bf16[336,128]{1,0:T(8,128)(2,1)S(1)}, u32[]{:S(2)}, u32[]{:S(2)}) collective-permute-start(bf16[336,128]{1,0:T(8,128)(2,1)S(1)} %get-tuple-element.48), channel_id=1, source_target_pairs={{0,8},{4,12},{8,0},{12,4},{16,24},{20,28},{24,16},{28,20},{32,40},... | collective-permute-start | bytes 258056 | tf_op jit(solution)/shard_map/ppermute | solution.py:39
  12.1 1.4 %collective-permute-start.2 = (bf16[336,128]{1,0:T(8,128)(2,1)S(1)}, bf16[336,128]{1,0:T(8,128)(2,1)S(1)}, u32[]{:S(2)}, u32[]{:S(2)}) collective-permute-start(bf16[336,128]{1,0:T(8,128)(2,1)S(1)} %get-tuple-element.49), channel_id=1, source_target_pairs={{0,12},{4,0},{8,4},{12,8},{16,28},{20,16},{24,20},{28,24},{32,44},... | collective-permute-start | bytes 258056 | tf_op jit(solution)/shard_map/ppermute | solution.py:39
  13.5 0.6 collective-permute-start
  14.2 0.9 collective-permute-start.6
  15.1 5.9 %collective-permute-done.1 = bf16[336,128]{1,0:T(8,128)(2,1)S(1)} collective-permute-done((bf16[336,128]{1,0:T(8,128)(2,1)S(1)}, bf16[336,128]{1,0:T(8,128)(2,1)S(1)}, u32[]{:S(2)}, u32[]{:S(2)}) %collective-permute-start.1) | collective-permute-done | bytes 86048 | tf_op jit(solution)/shard_map/ppermute | solution.py:39
  21.1 4.2 %collective-permute-start.11 = (bf16[2,336,128]{2,1,0:T(8,128)(2,1)S(1)}, bf16[2,336,128]{2,1,0:T(8,128)(2,1)S(1)}, u32[]{:S(2)}, u32[]{:S(2)}) collective-permute-start(bf16[2,336,128]{2,1,0:T(8,128)(2,1)S(1)} %pad_maximum_fusion.2.q1), channel_id=1, source_target_pairs={{0,48},{4,52},{8,56},{12,60},{16,0},{20,4},{24,8},{28,12},{32,16},... | collective-permute-start | bytes 516104 | tf_op jit(solution)/shard_map/ppermute | solution.py:39
  25.4 0.6 collective-permute-start.7
  26.0 2.2 %collective-permute-done.11.b1 = bf16[2,336,128]{2,1,0:T(8,128)(2,1)S(1)} collective-permute-done((bf16[2,336,128]{2,1,0:T(8,128)(2,1)S(1)}, bf16[2,336,128]{2,1,0:T(8,128)(2,1)S(1)}, u32[]{:S(2)}, u32[]{:S(2)}) %collective-permute-start.11) | collective-permute-done | bytes 172064 | tf_op jit(solution)/shard_map/ppermute | solution.py:39
  28.2 3.7 %collective-permute-start.10 = (bf16[2,336,128]{2,1,0:T(8,128)(2,1)S(1)}, bf16[2,336,128]{2,1,0:T(8,128)(2,1)S(1)}, u32[]{:S(2)}, u32[]{:S(2)}) collective-permute-start(bf16[2,336,128]{2,1,0:T(8,128)(2,1)S(1)} %pad_maximum_fusion.1.q0), channel_id=1, source_target_pairs={{0,48},{4,52},{8,56},{12,60},{16,0},{20,4},{24,8},{28,12},{32,16},... | collective-permute-start | bytes 516104 | tf_op jit(solution)/shard_map/ppermute | solution.py:39
  31.9 1.9 %collective-permute-done.8.a0 = bf16[2,336,128]{2,1,0:T(8,128)(2,1)S(1)} collective-permute-done((bf16[2,336,128]{2,1,0:T(8,128)(2,1)S(1)}, bf16[2,336,128]{2,1,0:T(8,128)(2,1)S(1)}, u32[]{:S(2)}, u32[]{:S(2)}) %collective-permute-start.8) | collective-permute-done | bytes 172064 | tf_op jit(solution)/shard_map/ppermute | solution.py:39
  33.9 2.0 %collective-permute-start.12 = (bf16[2,336,128]{2,1,0:T(8,128)(2,1)S(1)}, bf16[2,336,128]{2,1,0:T(8,128)(2,1)S(1)}, u32[]{:S(2)}, u32[]{:S(2)}) collective-permute-start(bf16[2,336,128]{2,1,0:T(8,128)(2,1)S(1)} %collective-permute-done.8.a0), channel_id=1, source_target_pairs={{0,16},{4,20},{8,24},{12,28},{16,32},{20,36},{24,40},{28,44},{32,4... | collective-permute-start | bytes 516104 | tf_op jit(solution)/shard_map/ppermute | solution.py:39
  35.9 2.4 %shard_map.94 = (bf16[512,256]{1,0:T(8,128)(2,1)}, bf16[512,128]{1,0:T(8,128)(2,1)}, f32[8,512]{1,0:T(8,128)}, bf16[512,1024]{1,0:T(8,128)(2,1)}, bf16[256,1024]...) custom-call(s32[1]{0:T(128)} %bitcast.1.core, ...), custom_call_target="tpu_custom_call" | custom-call | flops 536870912 | bytes 1048576 | tf_op jit(solution)/shard_map/pallas_call | solution.py:64
  38.3 3.0 %shard_map.95 = (bf16[1024,256]{1,0:T(8,128)(2,1)}, bf16[1024,128]{1,0:T(8,128)(2,1)}, f32[8,1024]{1,0:T(8,128)}, f32[8,1024]{1,0:T(8,128)S(1)}) custom-call(bf16[2,336,128]{2,1,0:T(8,128)(2,1)S(1)} %collective-permute-done.8.a0, bf16[2,336,128]{2,1,0:T(8,128)(2,1)S(1)} %collective-permute-done.9.a1, bf16[2,336,128]{2,1,0:T(8,128)(2,1)S(1)} %collective-permute-done.10.b0, ...), custom_call_target="tpu_custom_call" | custom-call | flops 1073741824 | bytes 1048576 | tf_op jit(solution)/shard_map/pallas_call | solution.py:64
  41.3 1.5 %shard_map.96 = (bf16[512,256]{1,0:T(8,128)(2,1)}, bf16[512,128]{1,0:T(8,128)(2,1)}, f32[8,512]{1,0:T(8,128)}, f32[16,512]{1,0:T(8,128)S(1)}) custom-call(bf16[2,336,128]{2,1,0:T(8,128)(2,1)S(1)} %collective-permute-done.12.qc, bf16[2,336,128]{2,1,0:T(8,128)(2,1)S(1)} %collective-permute-done.13.qd, bf16[1024,256]{1,0:T(8,128)(2,1)S(1)} %get-tuple-element.58.kp, ...), custom_call_target="tpu_custom_call" | custom-call | flops 536870912 | bytes 1048576 | tf_op jit(solution)/shard_map/pallas_call | solution.py:64
  42.9 1.7 %collective-permute-start.14 = (f32[16,512]{1,0:T(8,128)S(1)}, f32[16,512]{1,0:T(8,128)S(1)}, u32[]{:S(2)}, u32[]{:S(2)}) collective-permute-start(f32[16,512]{1,0:T(8,128)S(1)} %get-tuple-element.70.refs_14_), channel_id=1, source_target_pairs={{0,48},{4,52},{8,56},{12,60},{16,0},{20,4},{24,8},{28,12},{32,16},... | collective-permute-start | bytes 98312 | tf_op jit(solution)/shard_map/ppermute | solution.py:39
  44.6 0.5 collective-permute-start.15
  45.1 0.4 collective-permute-start.16
  45.5 1.4 %collective-permute-done.14.refs_15_ = f32[16,512]{1,0:T(8,128)S(1)} collective-permute-done((f32[16,512]{1,0:T(8,128)S(1)}, f32[16,512]{1,0:T(8,128)S(1)}, u32[]{:S(2)}, u32[]{:S(2)}) %collective-permute-start.14) | collective-permute-done | bytes 32800 | tf_op jit(solution)/shard_map/ppermute | solution.py:39
  46.9 3.1 %collective-permute-done.15.refs_16_ = f32[16,512]{1,0:T(8,128)S(1)} collective-permute-done((f32[16,512]{1,0:T(8,128)S(1)}, f32[16,512]{1,0:T(8,128)S(1)}, u32[]{:S(2)}, u32[]{:S(2)}) %collective-permute-start.15) | collective-permute-done | bytes 32800 | tf_op jit(solution)/shard_map/ppermute | solution.py:39
  50.0 0.3 collective-permute-done.16.refs_17_
  50.3 9.9 %shard_map.97 = (bf16[768,128]{1,0:T(8,128)(2,1)S(1)}, bf16[768,128]{1,0:T(8,128)(2,1)S(1)}, bf16[768,128]{1,0:T(8,128)(2,1)S(1)}, bf16[768,128]{1,0:T(8,128)(2,...) custom-call(bf16[1024,256]{1,0:T(8,128)(2,1)} %get-tuple-element.51., ...), custom_call_target="tpu_custom_call" | custom-call | flops 6442450944 | bytes 1048576 | tf_op jit(solution)/shard_map/pallas_call | solution.py:64
  60.3 3.1 %collective-permute-start.24 = (bf16[640,128]{1,0:T(8,128)(2,1)S(1)}, bf16[640,128]{1,0:T(8,128)(2,1)S(1)}, u32[]{:S(2)}, u32[]{:S(2)}) collective-permute-start(bf16[640,128]{1,0:T(8,128)(2,1)S(1)} %get-tuple-element.81), channel_id=1, source_target_pairs={{0,8},{4,12},{8,0},{12,4},{16,24},{20,28},{24,16},{28,20},{32,40},... | collective-permute-start | bytes 491528 | tf_op jit(solution)/shard_map/ppermute | solution.py:39
  63.7 4.0 %all-to-all-start = ((bf16[8,128,128]{2,1,0:T(8,128)(2,1)}), bf16[8,128,128]{2,1,0:T(8,128)(2,1)S(1)}, u32[]{:S(2)}, u32[]{:S(2)}) async-start(bf16[8,128,128]{2,1,0:T(8,128)(2,1)} %get-tuple-element.85), calls=%async_computation | async-start | bytes 524288 | tf_op jit(solution)/shard_map/all_to_all | solution.py:426
  67.7 0.9 collective-permute-done.23.x1
  68.6 0.9 collective-permute-done.25.x3
  69.5 0.7 shard_map.100
  70.2 1.7 %collective-permute-start.26 = (bf16[576,128]{1,0:T(8,128)(2,1)S(1)}, bf16[576,128]{1,0:T(8,128)(2,1)S(1)}, u32[]{:S(2)}, u32[]{:S(2)}) collective-permute-start(bf16[576,128]{1,0:T(8,128)(2,1)S(1)} %get-tuple-element.84), channel_id=1, source_target_pairs={{0,64},{4,68},{8,72},{12,76},{16,80},{20,84},{24,88},{28,92},{32,9... | collective-permute-start | bytes 442376 | tf_op jit(solution)/shard_map/ppermute | solution.py:39
  71.9 3.1 %all-to-all-done.parts = bf16[8,128,128]{2,1,0:T(8,128)(2,1)S(1)} async-done(((bf16[8,128,128]{2,1,0:T(8,128)(2,1)}), bf16[8,128,128]{2,1,0:T(8,128)(2,1)S(1)}, u32[]{:S(2)}, u32[]{:S(2)}) %all-to-all-start) | async-done | bytes 262176 | tf_op jit(solution)/shard_map/all_to_all | solution.py:426
  74.9 1.1 shard_map.101
  76.0 5.4 %all-to-all-start.1 = ((bf16[32,128,128]{2,1,0:T(8,128)(2,1)}), bf16[32,128,128]{2,1,0:T(8,128)(2,1)S(1)}, u32[]{:S(2)}, u32[]{:S(2)}) async-start(bf16[32,128,128]{2,1,0:T(8,128)(2,1)} %shard_map.101), calls=%async_computation.1 | async-start | bytes 2097152 | tf_op jit(solution)/shard_map/all_to_all | solution.py:437
  81.5 1.9 %collective-permute-start.17 = (bf16[768,128]{1,0:T(8,128)(2,1)S(1)}, bf16[768,128]{1,0:T(8,128)(2,1)S(1)}, u32[]{:S(2)}, u32[]{:S(2)}) collective-permute-start(bf16[768,128]{1,0:T(8,128)(2,1)S(1)} %get-tuple-element.72), channel_id=1, source_target_pairs={{0,16},{4,20},{8,24},{12,28},{16,32},{20,36},{24,40},{28,44},{32,4... | collective-permute-start | bytes 589832 | tf_op jit(solution)/shard_map/ppermute | solution.py:39
  83.4 2.7 %collective-permute-start.18 = (bf16[768,128]{1,0:T(8,128)(2,1)S(1)}, bf16[768,128]{1,0:T(8,128)(2,1)S(1)}, u32[]{:S(2)}, u32[]{:S(2)}) collective-permute-start(bf16[768,128]{1,0:T(8,128)(2,1)S(1)} %get-tuple-element.73), channel_id=1, source_target_pairs={{0,32},{4,36},{8,40},{12,44},{16,48},{20,52},{24,56},{28,60},{32,0... | collective-permute-start | bytes 589832 | tf_op jit(solution)/shard_map/ppermute | solution.py:39
  86.1 1.5 %collective-permute-start.19 = (bf16[768,128]{1,0:T(8,128)(2,1)S(1)}, bf16[768,128]{1,0:T(8,128)(2,1)S(1)}, u32[]{:S(2)}, u32[]{:S(2)}) collective-permute-start(bf16[768,128]{1,0:T(8,128)(2,1)S(1)} %get-tuple-element.74), channel_id=1, source_target_pairs={{0,48},{4,52},{8,56},{12,60},{16,0},{20,4},{24,8},{28,12},{32,16},... | collective-permute-start | bytes 589832 | tf_op jit(solution)/shard_map/ppermute | solution.py:39
  87.6 3.0 %collective-permute-start.28 = (bf16[576,128]{1,0:T(8,128)(2,1)S(1)}, bf16[576,128]{1,0:T(8,128)(2,1)S(1)}, u32[]{:S(2)}, u32[]{:S(2)}) collective-permute-start(bf16[576,128]{1,0:T(8,128)(2,1)S(1)} %reduce-precision_convert_fusion), channel_id=1, source_target_pairs={{0,2},{1,3},{2,0},{3,1},{4,6},{5,7},{6,4},{7,5},{8,10},{9,11},{10,... | collective-permute-start | bytes 442376 | tf_op jit(solution)/shard_map/ppermute | solution.py:445
  90.6 11.1 %collective-permute-done.17.z1 = bf16[768,128]{1,0:T(8,128)(2,1)S(1)} collective-permute-done((bf16[768,128]{1,0:T(8,128)(2,1)S(1)}, bf16[768,128]{1,0:T(8,128)(2,1)S(1)}, u32[]{:S(2)}, u32[]{:S(2)}) %collective-permute-start.17) | collective-permute-done | bytes 196640 | tf_op jit(solution)/shard_map/ppermute | solution.py:39
  101.8 1.6 %collective-permute-start.20 = (bf16[192,128]{1,0:T(8,128)(2,1)S(1)}, bf16[192,128]{1,0:T(8,128)(2,1)S(1)}, u32[]{:S(2)}, u32[]{:S(2)}) collective-permute-start(bf16[192,128]{1,0:T(8,128)(2,1)S(1)} %get-tuple-element.76), channel_id=1, source_target_pairs={{0,12},{4,0},{8,4},{12,8},{16,28},{20,16},{24,20},{28,24},{32,44},... | collective-permute-start | bytes 147464 | tf_op jit(solution)/shard_map/ppermute | solution.py:39
  103.4 1.0 collective-permute-start.21
  104.4 0.8 collective-permute-start.22
  105.2 1.0 collective-permute-done.20.q1
  106.2 2.8 %collective-permute-done.21.q2 = bf16[192,128]{1,0:T(8,128)(2,1)S(1)} collective-permute-done((bf16[192,128]{1,0:T(8,128)(2,1)S(1)}, bf16[192,128]{1,0:T(8,128)(2,1)S(1)}, u32[]{:S(2)}, u32[]{:S(2)}) %collective-permute-start.21) | collective-permute-done | bytes 49184 | tf_op jit(solution)/shard_map/ppermute | solution.py:39
  109.0 0.7 collective-permute-done.22.q3
  109.7 0.9 shard_map.99
  110.6 0.7 add_bitcast_fusion
  111.4 1.5 %shard_map.102 = (f32[512,512]{1,0:T(8,128)}, f32[512,512]{1,0:T(8,128)}) custom-call(bf16[32,128,128]{2,1,0:T(8,128)(2,1)S(1)} %all-to-all-done.1.a), custom_call_target="tpu_custom_call" | custom-call | flops 1 | bytes 1048576 | tf_op jit(solution)/shard_map/pallas_call | solution.py:64
  (36 shorter events, 1.0 us)
Async XLA Ops:
  1.9 5.7 %collective-permute-start.3 = (bf16[592,128]{1,0:T(8,128)(2,1)S(1)}, bf16[592,128]{1,0:T(8,128)(2,1)S(1)}, u32[]{:S(2)}, u32[]{:S(2)}) collective-permute-start(bf16[592,128]{1,0:T(8,128)(2,1)S(1)} %get-tuple-element.50), channel_id=1, source_target_pairs={{0,64},{4,68},{8,72},{12,76},{16,80},{20,84},{24,88},{28,92},{32,9... | collective-permute-start | bytes 454664 | tf_op jit(solution)/shard_map/ppermute | solution.py:39
  7.6 17.7 %collective-permute-start.4 = (bf16[2,592,128]{2,1,0:T(8,128)(2,1)S(1)}, bf16[2,592,128]{2,1,0:T(8,128)(2,1)S(1)}, u32[]{:S(2)}, u32[]{:S(2)}) collective-permute-start(bf16[2,592,128]{2,1,0:T(8,128)(2,1)S(1)} %pad_maximum_fusion.pair), channel_id=1, source_target_pairs={{0,4},{1,13},{2,6},{3,15},{4,8},{5,1},{6,10},{7,3},{8,12},{9,5},{1... | collective-permute-start | bytes 909320 | tf_op jit(solution)/shard_map/ppermute | solution.py:50
  9.4 11.7 %collective-permute-start.1 = (bf16[336,128]{1,0:T(8,128)(2,1)S(1)}, bf16[336,128]{1,0:T(8,128)(2,1)S(1)}, u32[]{:S(2)}, u32[]{:S(2)}) collective-permute-start(bf16[336,128]{1,0:T(8,128)(2,1)S(1)} %get-tuple-element.48), channel_id=1, source_target_pairs={{0,8},{4,12},{8,0},{12,4},{16,24},{20,28},{24,16},{28,20},{32,40},... | collective-permute-start | bytes 258056 | tf_op jit(solution)/shard_map/ppermute | solution.py:39
  12.1 9.0 %collective-permute-start.2 = (bf16[336,128]{1,0:T(8,128)(2,1)S(1)}, bf16[336,128]{1,0:T(8,128)(2,1)S(1)}, u32[]{:S(2)}, u32[]{:S(2)}) collective-permute-start(bf16[336,128]{1,0:T(8,128)(2,1)S(1)} %get-tuple-element.49), channel_id=1, source_target_pairs={{0,12},{4,0},{8,4},{12,8},{16,28},{20,16},{24,20},{28,24},{32,44},... | collective-permute-start | bytes 258056 | tf_op jit(solution)/shard_map/ppermute | solution.py:39
  13.5 11.8 %collective-permute-start = (bf16[336,128]{1,0:T(8,128)(2,1)S(1)}, bf16[336,128]{1,0:T(8,128)(2,1)S(1)}, u32[]{:S(2)}, u32[]{:S(2)}) collective-permute-start(bf16[336,128]{1,0:T(8,128)(2,1)S(1)} %get-tuple-element.47), channel_id=1, source_target_pairs={{0,4},{4,8},{8,12},{12,0},{16,20},{20,24},{24,28},{28,16},{32,36},... | collective-permute-start | bytes 258056 | tf_op jit(solution)/shard_map/ppermute | solution.py:39
  14.1 21.8 %copy-start = (bf16[512,512]{1,0:T(8,128)(2,1)S(1)}, bf16[512,512]{1,0:T(8,128)(2,1)}, u32[]{:S(2)}) copy-start(bf16[512,512]{1,0:T(8,128)(2,1)} %vu.1) | copy-start | bytes 1572868
  14.1 21.8 %copy-start.1 = (bf16[512,512]{1,0:T(8,128)(2,1)S(1)}, bf16[512,512]{1,0:T(8,128)(2,1)}, u32[]{:S(2)}) copy-start(bf16[512,512]{1,0:T(8,128)(2,1)} %ku.1) | copy-start | bytes 1572868
  14.2 11.2 %collective-permute-start.6 = (bf16[592,128]{1,0:T(8,128)(2,1)S(1)}, bf16[592,128]{1,0:T(8,128)(2,1)S(1)}, u32[]{:S(2)}, u32[]{:S(2)}) collective-permute-start(bf16[592,128]{1,0:T(8,128)(2,1)S(1)} %fusion.1), channel_id=1, source_target_pairs={{0,8},{1,9},{2,10},{3,11},{4,12},{5,13},{6,14},{7,15},{8,0},{9,1},... | collective-permute-start | bytes 454664 | tf_op jit(solution)/shard_map/ppermute | solution.py:50
  21.1 7.1 %collective-permute-start.11 = (bf16[2,336,128]{2,1,0:T(8,128)(2,1)S(1)}, bf16[2,336,128]{2,1,0:T(8,128)(2,1)S(1)}, u32[]{:S(2)}, u32[]{:S(2)}) collective-permute-start(bf16[2,336,128]{2,1,0:T(8,128)(2,1)S(1)} %pad_maximum_fusion.2.q1), channel_id=1, source_target_pairs={{0,48},{4,52},{8,56},{12,60},{16,0},{20,4},{24,8},{28,12},{32,16},... | collective-permute-start | bytes 516104 | tf_op jit(solution)/shard_map/ppermute | solution.py:39
  25.3 10.6 %collective-permute-start.5 = (bf16[2,592,128]{2,1,0:T(8,128)(2,1)S(1)}, bf16[2,592,128]{2,1,0:T(8,128)(2,1)S(1)}, u32[]{:S(2)}, u32[]{:S(2)}) collective-permute-start(bf16[2,592,128]{2,1,0:T(8,128)(2,1)S(1)} %collective-permute-done.4.lp), channel_id=1, source_target_pairs={{0,1},{1,0},{2,3},{3,2},{4,5},{5,4},{6,7},{7,6},{8,9},{9,8},{10,11... | collective-permute-start | bytes 909320 | tf_op jit(solution)/shard_map/ppermute | solution.py:54
  25.3 8.5 %collective-permute-start.8 = (bf16[2,336,128]{2,1,0:T(8,128)(2,1)S(1)}, bf16[2,336,128]{2,1,0:T(8,128)(2,1)S(1)}, u32[]{:S(2)}, u32[]{:S(2)}) collective-permute-start(bf16[2,336,128]{2,1,0:T(8,128)(2,1)S(1)} %pad_maximum_fusion.1.q0), channel_id=1, source_target_pairs={{0,16},{4,20},{8,24},{12,28},{16,32},{20,36},{24,40},{28,44},{32,4... | collective-permute-start | bytes 516104 | tf_op jit(solution)/shard_map/ppermute | solution.py:39
  25.4 8.4 %collective-permute-start.7 = (bf16[592,128]{1,0:T(8,128)(2,1)S(1)}, bf16[592,128]{1,0:T(8,128)(2,1)S(1)}, u32[]{:S(2)}, u32[]{:S(2)}) collective-permute-start(bf16[592,128]{1,0:T(8,128)(2,1)S(1)} %collective-permute-done.6.lh), channel_id=1, source_target_pairs={{0,1},{1,0},{2,3},{3,2},{4,5},{5,4},{6,7},{7,6},{8,9},{9,8},{10,11... | collective-permute-start | bytes 454664 | tf_op jit(solution)/shard_map/ppermute | solution.py:54
  26.0 12.3 %collective-permute-start.9 = (bf16[2,336,128]{2,1,0:T(8,128)(2,1)S(1)}, bf16[2,336,128]{2,1,0:T(8,128)(2,1)S(1)}, u32[]{:S(2)}, u32[]{:S(2)}) collective-permute-start(bf16[2,336,128]{2,1,0:T(8,128)(2,1)S(1)} %pad_maximum_fusion.2.q1), channel_id=1, source_target_pairs={{0,16},{4,20},{8,24},{12,28},{16,32},{20,36},{24,40},{28,44},{32,4... | collective-permute-start | bytes 516104 | tf_op jit(solution)/shard_map/ppermute | solution.py:39
  28.2 10.1 %collective-permute-start.10 = (bf16[2,336,128]{2,1,0:T(8,128)(2,1)S(1)}, bf16[2,336,128]{2,1,0:T(8,128)(2,1)S(1)}, u32[]{:S(2)}, u32[]{:S(2)}) collective-permute-start(bf16[2,336,128]{2,1,0:T(8,128)(2,1)S(1)} %pad_maximum_fusion.1.q0), channel_id=1, source_target_pairs={{0,48},{4,52},{8,56},{12,60},{16,0},{20,4},{24,8},{28,12},{32,16},... | collective-permute-start | bytes 516104 | tf_op jit(solution)/shard_map/ppermute | solution.py:39
  33.9 7.5 %collective-permute-start.13 = (bf16[2,336,128]{2,1,0:T(8,128)(2,1)S(1)}, bf16[2,336,128]{2,1,0:T(8,128)(2,1)S(1)}, u32[]{:S(2)}, u32[]{:S(2)}) collective-permute-start(bf16[2,336,128]{2,1,0:T(8,128)(2,1)S(1)} %collective-permute-done.11.b1), channel_id=1, source_target_pairs={{0,48},{4,52},{8,56},{12,60},{16,0},{20,4},{24,8},{28,12},{32,16},... | collective-permute-start | bytes 516104 | tf_op jit(solution)/shard_map/ppermute | solution.py:39
  33.9 7.5 %collective-permute-start.12 = (bf16[2,336,128]{2,1,0:T(8,128)(2,1)S(1)}, bf16[2,336,128]{2,1,0:T(8,128)(2,1)S(1)}, u32[]{:S(2)}, u32[]{:S(2)}) collective-permute-start(bf16[2,336,128]{2,1,0:T(8,128)(2,1)S(1)} %collective-permute-done.8.a0), channel_id=1, source_target_pairs={{0,16},{4,20},{8,24},{12,28},{16,32},{20,36},{24,40},{28,44},{32,4... | collective-permute-start | bytes 516104 | tf_op jit(solution)/shard_map/ppermute | solution.py:39
  42.9 4.0 %collective-permute-start.14 = (f32[16,512]{1,0:T(8,128)S(1)}, f32[16,512]{1,0:T(8,128)S(1)}, u32[]{:S(2)}, u32[]{:S(2)}) collective-permute-start(f32[16,512]{1,0:T(8,128)S(1)} %get-tuple-element.70.refs_14_), channel_id=1, source_target_pairs={{0,48},{4,52},{8,56},{12,60},{16,0},{20,4},{24,8},{28,12},{32,16},... | collective-permute-start | bytes 98312 | tf_op jit(solution)/shard_map/ppermute | solution.py:39
  44.6 5.4 %collective-permute-start.15 = (f32[16,512]{1,0:T(8,128)S(1)}, f32[16,512]{1,0:T(8,128)S(1)}, u32[]{:S(2)}, u32[]{:S(2)}) collective-permute-start(f32[16,512]{1,0:T(8,128)S(1)} %get-tuple-element.70.refs_14_), channel_id=1, source_target_pairs={{0,32},{4,36},{8,40},{12,44},{16,48},{20,52},{24,56},{28,60},{32,0... | collective-permute-start | bytes 98312 | tf_op jit(solution)/shard_map/ppermute | solution.py:39
  45.1 5.3 %collective-permute-start.16 = (f32[16,512]{1,0:T(8,128)S(1)}, f32[16,512]{1,0:T(8,128)S(1)}, u32[]{:S(2)}, u32[]{:S(2)}) collective-permute-start(f32[16,512]{1,0:T(8,128)S(1)} %get-tuple-element.70.refs_14_), channel_id=1, source_target_pairs={{0,16},{4,20},{8,24},{12,28},{16,32},{20,36},{24,40},{28,44},{32,4... | collective-permute-start | bytes 98312 | tf_op jit(solution)/shard_map/ppermute | solution.py:39
  60.2 8.4 %collective-permute-start.23 = (bf16[640,128]{1,0:T(8,128)(2,1)S(1)}, bf16[640,128]{1,0:T(8,128)(2,1)S(1)}, u32[]{:S(2)}, u32[]{:S(2)}) collective-permute-start(bf16[640,128]{1,0:T(8,128)(2,1)S(1)} %get-tuple-element.80), channel_id=1, source_target_pairs={{0,4},{4,8},{8,12},{12,0},{16,20},{20,24},{24,28},{28,16},{32,36},... | collective-permute-start | bytes 491528 | tf_op jit(solution)/shard_map/ppermute | solution.py:39
  60.3 8.3 %collective-permute-start.24 = (bf16[640,128]{1,0:T(8,128)(2,1)S(1)}, bf16[640,128]{1,0:T(8,128)(2,1)S(1)}, u32[]{:S(2)}, u32[]{:S(2)}) collective-permute-start(bf16[640,128]{1,0:T(8,128)(2,1)S(1)} %get-tuple-element.81), channel_id=1, source_target_pairs={{0,8},{4,12},{8,0},{12,4},{16,24},{20,28},{24,16},{28,20},{32,40},... | collective-permute-start | bytes 491528 | tf_op jit(solution)/shard_map/ppermute | solution.py:39
  63.4 6.1 %collective-permute-start.25 = (bf16[640,128]{1,0:T(8,128)(2,1)S(1)}, bf16[640,128]{1,0:T(8,128)(2,1)S(1)}, u32[]{:S(2)}, u32[]{:S(2)}) collective-permute-start(bf16[640,128]{1,0:T(8,128)(2,1)S(1)} %get-tuple-element.82), channel_id=1, source_target_pairs={{0,12},{4,0},{8,4},{12,8},{16,28},{20,16},{24,20},{28,24},{32,44},... | collective-permute-start | bytes 491528 | tf_op jit(solution)/shard_map/ppermute | solution.py:39
  63.7 11.2 %all-to-all-start = ((bf16[8,128,128]{2,1,0:T(8,128)(2,1)}), bf16[8,128,128]{2,1,0:T(8,128)(2,1)S(1)}, u32[]{:S(2)}, u32[]{:S(2)}) async-start(bf16[8,128,128]{2,1,0:T(8,128)(2,1)} %get-tuple-element.85), calls=%async_computation | async-start | bytes 524288 | tf_op jit(solution)/shard_map/all_to_all | solution.py:426
  70.2 11.2 %collective-permute-start.26 = (bf16[576,128]{1,0:T(8,128)(2,1)S(1)}, bf16[576,128]{1,0:T(8,128)(2,1)S(1)}, u32[]{:S(2)}, u32[]{:S(2)}) collective-permute-start(bf16[576,128]{1,0:T(8,128)(2,1)S(1)} %get-tuple-element.84), channel_id=1, source_target_pairs={{0,64},{4,68},{8,72},{12,76},{16,80},{20,84},{24,88},{28,92},{32,9... | collective-permute-start | bytes 442376 | tf_op jit(solution)/shard_map/ppermute | solution.py:39
  76.0 35.3 %all-to-all-start.1 = ((bf16[32,128,128]{2,1,0:T(8,128)(2,1)}), bf16[32,128,128]{2,1,0:T(8,128)(2,1)S(1)}, u32[]{:S(2)}, u32[]{:S(2)}) async-start(bf16[32,128,128]{2,1,0:T(8,128)(2,1)} %shard_map.101), calls=%async_computation.1 | async-start | bytes 2097152 | tf_op jit(solution)/shard_map/all_to_all | solution.py:437
  81.4 6.1 %collective-permute-start.27 = (bf16[576,128]{1,0:T(8,128)(2,1)S(1)}, bf16[576,128]{1,0:T(8,128)(2,1)S(1)}, u32[]{:S(2)}, u32[]{:S(2)}) collective-permute-start(bf16[576,128]{1,0:T(8,128)(2,1)S(1)} %reduce-precision_convert_fusion.1), channel_id=1, source_target_pairs={{0,1},{1,0},{2,3},{3,2},{4,5},{5,4},{6,7},{7,6},{8,9},{9,8},{10,11... | collective-permute-start | bytes 442376 | tf_op jit(solution)/shard_map/ppermute | solution.py:54
  81.5 20.1 %collective-permute-start.17 = (bf16[768,128]{1,0:T(8,128)(2,1)S(1)}, bf16[768,128]{1,0:T(8,128)(2,1)S(1)}, u32[]{:S(2)}, u32[]{:S(2)}) collective-permute-start(bf16[768,128]{1,0:T(8,128)(2,1)S(1)} %get-tuple-element.72), channel_id=1, source_target_pairs={{0,16},{4,20},{8,24},{12,28},{16,32},{20,36},{24,40},{28,44},{32,4... | collective-permute-start | bytes 589832 | tf_op jit(solution)/shard_map/ppermute | solution.py:39
  83.4 18.3 %collective-permute-start.18 = (bf16[768,128]{1,0:T(8,128)(2,1)S(1)}, bf16[768,128]{1,0:T(8,128)(2,1)S(1)}, u32[]{:S(2)}, u32[]{:S(2)}) collective-permute-start(bf16[768,128]{1,0:T(8,128)(2,1)S(1)} %get-tuple-element.73), channel_id=1, source_target_pairs={{0,32},{4,36},{8,40},{12,44},{16,48},{20,52},{24,56},{28,60},{32,0... | collective-permute-start | bytes 589832 | tf_op jit(solution)/shard_map/ppermute | solution.py:39
  86.1 15.6 %collective-permute-start.19 = (bf16[768,128]{1,0:T(8,128)(2,1)S(1)}, bf16[768,128]{1,0:T(8,128)(2,1)S(1)}, u32[]{:S(2)}, u32[]{:S(2)}) collective-permute-start(bf16[768,128]{1,0:T(8,128)(2,1)S(1)} %get-tuple-element.74), channel_id=1, source_target_pairs={{0,48},{4,52},{8,56},{12,60},{16,0},{20,4},{24,8},{28,12},{32,16},... | collective-permute-start | bytes 589832 | tf_op jit(solution)/shard_map/ppermute | solution.py:39
  87.6 23.0 %collective-permute-start.28 = (bf16[576,128]{1,0:T(8,128)(2,1)S(1)}, bf16[576,128]{1,0:T(8,128)(2,1)S(1)}, u32[]{:S(2)}, u32[]{:S(2)}) collective-permute-start(bf16[576,128]{1,0:T(8,128)(2,1)S(1)} %reduce-precision_convert_fusion), channel_id=1, source_target_pairs={{0,2},{1,3},{2,0},{3,1},{4,6},{5,7},{6,4},{7,5},{8,10},{9,11},{10,... | collective-permute-start | bytes 442376 | tf_op jit(solution)/shard_map/ppermute | solution.py:445
  101.8 4.4 %collective-permute-start.20 = (bf16[192,128]{1,0:T(8,128)(2,1)S(1)}, bf16[192,128]{1,0:T(8,128)(2,1)S(1)}, u32[]{:S(2)}, u32[]{:S(2)}) collective-permute-start(bf16[192,128]{1,0:T(8,128)(2,1)S(1)} %get-tuple-element.76), channel_id=1, source_target_pairs={{0,12},{4,0},{8,4},{12,8},{16,28},{20,16},{24,20},{28,24},{32,44},... | collective-permute-start | bytes 147464 | tf_op jit(solution)/shard_map/ppermute | solution.py:39
  103.4 5.6 %collective-permute-start.21 = (bf16[192,128]{1,0:T(8,128)(2,1)S(1)}, bf16[192,128]{1,0:T(8,128)(2,1)S(1)}, u32[]{:S(2)}, u32[]{:S(2)}) collective-permute-start(bf16[192,128]{1,0:T(8,128)(2,1)S(1)} %get-tuple-element.77), channel_id=1, source_target_pairs={{0,8},{4,12},{8,0},{12,4},{16,24},{20,28},{24,16},{28,20},{32,40},... | collective-permute-start | bytes 147464 | tf_op jit(solution)/shard_map/ppermute | solution.py:39
  104.4 5.3 %collective-permute-start.22 = (bf16[192,128]{1,0:T(8,128)(2,1)S(1)}, bf16[192,128]{1,0:T(8,128)(2,1)S(1)}, u32[]{:S(2)}, u32[]{:S(2)}) collective-permute-start(bf16[192,128]{1,0:T(8,128)(2,1)S(1)} %get-tuple-element.78), channel_id=1, source_target_pairs={{0,4},{4,8},{8,12},{12,0},{16,20},{20,24},{24,28},{28,16},{32,36},... | collective-permute-start | bytes 147464 | tf_op jit(solution)/shard_map/ppermute | solution.py:39

commit v3 on v2

--- a/solution.py
+++ b/solution.py
@@ -11,7 +11,6 @@
 
 BF = jnp.bfloat16
 F32 = jnp.float32
-D_LAT = 512
 D_ROPE = 64
 D_NOPE = 128
 ROWS = 128
@@ -168,12 +167,13 @@
 
 
 def forward_own(
-    core, q0, q1, pair, lp, lpe, lh, lhe, ku, vu,
+    core, x, q0, q1, pair, lp, lpe, lh, lhe, ku, vu,
     qp_hbm, do_hbm, qtag_hbm, compt_hbm, kpt_hbm, kp_hbm, v_hbm, ktag_hbm, kp, v, ktag, stats,
     qp, do, qtag, compt, kpt, sems, late_sems,
 ):
     take_queries([ref[i] for ref in (q0, q1) for i in range(2)], qp, do, qtag)
     first = core[0] == 0
+    head = pl.ds(pl.multiple_of((x[0] & 3) * 128, 128), 128)
     for n in range(8):
         if n < 2:
             block = pair[n]
@@ -188,10 +188,10 @@
         kpt[128:192, at : at + 128] = block[512:576]
         ktag[8 * n : 8 * n + 8] = block[576:592].astype(F32)[0:8]
     kpt[192:256] = jnp.zeros((64, NK), BF)
-    kpt[0:128] = mm(ku[...].T, compt[...], NN).astype(BF)
+    kpt[0:128] = mm(ku[:, head].T, compt[...], NN).astype(BF)
     pairs = [(qp, qp_hbm), (do, do_hbm), (qtag, qtag_hbm), (compt, compt_hbm), (kpt, kpt_hbm), (ktag, ktag_hbm)]
     copies = copied(pairs, sems)
-    v[...] = mm(vu[...].T, compt[...], NN).astype(BF).T
+    v[...] = mm(vu[:, head].T, compt[...], NN).astype(BF).T
     kp[...] = kpt[...].T
     copies += copied([(kp, kp_hbm), (v, v_hbm)], late_sems)
     statistics(512, qp, do, qtag, kp, v, ktag, stats, 0)
@@ -367,8 +367,6 @@
     qd = along(qb1, dz=-1)
     lpe = to_core(lp)
     lhe = to_core(lh)
-    ku = lax.dynamic_slice(key_up, (0, x * 128), (D_LAT, 128))
-    vu = lax.dynamic_slice(value_up, (0, x * 128), (D_LAT, 128))
 
     flops = 2 * NQ * NK * 512
 
@@ -386,7 +384,7 @@
     qp0, do0, qtag0, compt, kpt, kp, v, ktag, *here, own_stats = call(
         forward_own,
         at_hbm(rows(512) + wide + keyed) + keyed + [((8, 512), F32)],
-        [(core[None], SM), q0, q1, pair, lp, lpe, lh, lhe, ku, vu],
+        [(core[None], SM), (x[None], SM), q0, q1, pair, lp, lpe, lh, lhe, key_up, value_up],
         scratch=at_vmem(rows(512) + wide) + [pltpu.SemaphoreType.DMA((6,)), pltpu.SemaphoreType.DMA((2,))],
         flops=flops // 4, grant=20,
     )

time: 113 us -> 113 us (level)
  no operation moved by 1% of the time
where the time goes in v3:
time: 113 us
  starting transfers between devices  49.3 us (44%)
  waiting for transfers between devices  39.3 us (35%)
  Pallas kernels  22.4 us (20%)
    ppermute x23, waiting for transfers between devices, along(): return lax.ppermute(value, 'seq', pairs)  36.3 us
    ppermute x23, starting transfers between devices, along(): return lax.ppermute(value, 'seq', pairs)  33.7 us
    pallas_call x10, Pallas kernels, call(): pl.pallas_call(kernel, out_shape=[HB(o[0], o[1]) if o[2:] == (HB,) else j...  22.4 us
    all_to_all x1, starting transfers between devices, shards(): whole = lax.all_to_all(every, 'seq', 0, 0, tiled=True)  5.35 us
    all_to_all x1, starting transfers between devices, shards(): lax.all_to_all(up, 'seq', 0, 0, tiled=True, axis_index_groups=YZ_GROUPS)  3.96 us
    all_to_all x1, waiting for transfers between devices, shards(): lax.all_to_all(up, 'seq', 0, 0, tiled=True, axis_index_groups=YZ_GROUPS)  3.06 us
    ppermute x1, starting transfers between devices, shards(): far16 = lax.ppermute(two, 'head', [(0, 2), (1, 3), (2, 0), (3, 1)])  2.99 us
    ppermute x2, starting transfers between devices, by_core(): return lax.ppermute(value, ('seq', 'head'), pairs)  2.67 us
  transfers between devices with their start and end apart: 31, of which 14 were waited for; matrix products, arithmetic and copies ran while one was open for 1% of the time, Pallas kernels for 7%

profile of v3, /device:TPU:0, one launch (start us, length us, event | category | flops | bytes accessed | tf_op | source)
XLA Modules:
  0.0 112.9 jit_solution(17173333882626801477)
XLA Ops:
  0.6 1.3 %shard_map.93 = (bf16[336,128]{1,0:T(8,128)(2,1)S(1)}, bf16[336,128]{1,0:T(8,128)(2,1)S(1)}, bf16[336,128]{1,0:T(8,128)(2,1)S(1)}, bf16[336,128]{1,0:T(8,128)(2,1)S(1)}, bf16[592,128]{1,0:T(8,128)(2,1)S(1)}) custom-call(s32[128]{0:T(128)} %pos_hbm.1, s32[1]{0:T(128)} %bitcast.x, bf16[128,768]{1,0:T(8,128)(2,1)} %q_hbm.1, bf16[128,512]{1,0:T(8,128)(2,1)} %g_hbm.1, ...), custom_call_target="tpu_custom_call" | custom-call | flops 1 | bytes 1048576 | tf_op jit(solution)/shard_map/pallas_call | solution.py:63
  1.9 1.8 %collective-permute-start.3 = (bf16[592,128]{1,0:T(8,128)(2,1)S(1)}, bf16[592,128]{1,0:T(8,128)(2,1)S(1)}, u32[]{:S(2)}, u32[]{:S(2)}) collective-permute-start(bf16[592,128]{1,0:T(8,128)(2,1)S(1)} %get-tuple-element.50), channel_id=1, source_target_pairs={{0,64},{4,68},{8,72},{12,76},{16,80},{20,84},{24,88},{28,92},{32,9... | collective-permute-start | bytes 454664 | tf_op jit(solution)/shard_map/ppermute | solution.py:38
  3.7 3.9 %collective-permute-done.3 = bf16[592,128]{1,0:T(8,128)(2,1)S(1)} collective-permute-done((bf16[592,128]{1,0:T(8,128)(2,1)S(1)}, bf16[592,128]{1,0:T(8,128)(2,1)S(1)}, u32[]{:S(2)}, u32[]{:S(2)}) %collective-permute-start.3) | collective-permute-done | bytes 151584 | tf_op jit(solution)/shard_map/ppermute | solution.py:38
  7.6 1.7 %collective-permute-start.4 = (bf16[2,592,128]{2,1,0:T(8,128)(2,1)S(1)}, bf16[2,592,128]{2,1,0:T(8,128)(2,1)S(1)}, u32[]{:S(2)}, u32[]{:S(2)}) collective-permute-start(bf16[2,592,128]{2,1,0:T(8,128)(2,1)S(1)} %pad_maximum_fusion.pair), channel_id=1, source_target_pairs={{0,4},{1,13},{2,6},{3,15},{4,8},{5,1},{6,10},{7,3},{8,12},{9,5},{1... | collective-permute-start | bytes 909320 | tf_op jit(solution)/shard_map/ppermute | solution.py:49
  9.4 2.7 %collective-permute-start.1 = (bf16[336,128]{1,0:T(8,128)(2,1)S(1)}, bf16[336,128]{1,0:T(8,128)(2,1)S(1)}, u32[]{:S(2)}, u32[]{:S(2)}) collective-permute-start(bf16[336,128]{1,0:T(8,128)(2,1)S(1)} %get-tuple-element.48), channel_id=1, source_target_pairs={{0,8},{4,12},{8,0},{12,4},{16,24},{20,28},{24,16},{28,20},{32,40},... | collective-permute-start | bytes 258056 | tf_op jit(solution)/shard_map/ppermute | solution.py:38
  12.1 1.4 %collective-permute-start.2 = (bf16[336,128]{1,0:T(8,128)(2,1)S(1)}, bf16[336,128]{1,0:T(8,128)(2,1)S(1)}, u32[]{:S(2)}, u32[]{:S(2)}) collective-permute-start(bf16[336,128]{1,0:T(8,128)(2,1)S(1)} %get-tuple-element.49), channel_id=1, source_target_pairs={{0,12},{4,0},{8,4},{12,8},{16,28},{20,16},{24,20},{28,24},{32,44},... | collective-permute-start | bytes 258056 | tf_op jit(solution)/shard_map/ppermute | solution.py:38
  13.5 0.6 collective-permute-start
  14.2 0.9 collective-permute-start.6
  15.1 5.9 %collective-permute-done.1 = bf16[336,128]{1,0:T(8,128)(2,1)S(1)} collective-permute-done((bf16[336,128]{1,0:T(8,128)(2,1)S(1)}, bf16[336,128]{1,0:T(8,128)(2,1)S(1)}, u32[]{:S(2)}, u32[]{:S(2)}) %collective-permute-start.1) | collective-permute-done | bytes 86048 | tf_op jit(solution)/shard_map/ppermute | solution.py:38
  21.1 4.2 %collective-permute-start.11 = (bf16[2,336,128]{2,1,0:T(8,128)(2,1)S(1)}, bf16[2,336,128]{2,1,0:T(8,128)(2,1)S(1)}, u32[]{:S(2)}, u32[]{:S(2)}) collective-permute-start(bf16[2,336,128]{2,1,0:T(8,128)(2,1)S(1)} %pad_maximum_fusion.2.q1), channel_id=1, source_target_pairs={{0,48},{4,52},{8,56},{12,60},{16,0},{20,4},{24,8},{28,12},{32,16},... | collective-permute-start | bytes 516104 | tf_op jit(solution)/shard_map/ppermute | solution.py:38
  25.4 0.6 collective-permute-start.7
  26.0 2.2 %collective-permute-done.11.b1 = bf16[2,336,128]{2,1,0:T(8,128)(2,1)S(1)} collective-permute-done((bf16[2,336,128]{2,1,0:T(8,128)(2,1)S(1)}, bf16[2,336,128]{2,1,0:T(8,128)(2,1)S(1)}, u32[]{:S(2)}, u32[]{:S(2)}) %collective-permute-start.11) | collective-permute-done | bytes 172064 | tf_op jit(solution)/shard_map/ppermute | solution.py:38
  28.2 3.7 %collective-permute-start.10 = (bf16[2,336,128]{2,1,0:T(8,128)(2,1)S(1)}, bf16[2,336,128]{2,1,0:T(8,128)(2,1)S(1)}, u32[]{:S(2)}, u32[]{:S(2)}) collective-permute-start(bf16[2,336,128]{2,1,0:T(8,128)(2,1)S(1)} %pad_maximum_fusion.1.q0), channel_id=1, source_target_pairs={{0,48},{4,52},{8,56},{12,60},{16,0},{20,4},{24,8},{28,12},{32,16},... | collective-permute-start | bytes 516104 | tf_op jit(solution)/shard_map/ppermute | solution.py:38
  31.9 1.9 %collective-permute-done.8.a0 = bf16[2,336,128]{2,1,0:T(8,128)(2,1)S(1)} collective-permute-done((bf16[2,336,128]{2,1,0:T(8,128)(2,1)S(1)}, bf16[2,336,128]{2,1,0:T(8,128)(2,1)S(1)}, u32[]{:S(2)}, u32[]{:S(2)}) %collective-permute-start.8) | collective-permute-done | bytes 172064 | tf_op jit(solution)/shard_map/ppermute | solution.py:38
  33.9 2.0 %collective-permute-start.12 = (bf16[2,336,128]{2,1,0:T(8,128)(2,1)S(1)}, bf16[2,336,128]{2,1,0:T(8,128)(2,1)S(1)}, u32[]{:S(2)}, u32[]{:S(2)}) collective-permute-start(bf16[2,336,128]{2,1,0:T(8,128)(2,1)S(1)} %collective-permute-done.8.a0), channel_id=1, source_target_pairs={{0,16},{4,20},{8,24},{12,28},{16,32},{20,36},{24,40},{28,44},{32,4... | collective-permute-start | bytes 516104 | tf_op jit(solution)/shard_map/ppermute | solution.py:38
  35.9 2.4 %shard_map.94 = (bf16[512,256]{1,0:T(8,128)(2,1)}, bf16[512,128]{1,0:T(8,128)(2,1)}, f32[8,512]{1,0:T(8,128)}, bf16[512,1024]{1,0:T(8,128)(2,1)}, bf16[256,1024]...) custom-call(s32[1]{0:T(128)} %bitcast.1.core, ...), custom_call_target="tpu_custom_call" | custom-call | flops 536870912 | bytes 1048576 | tf_op jit(solution)/shard_map/pallas_call | solution.py:63
  38.3 3.0 %shard_map.95 = (bf16[1024,256]{1,0:T(8,128)(2,1)}, bf16[1024,128]{1,0:T(8,128)(2,1)}, f32[8,1024]{1,0:T(8,128)}, f32[8,1024]{1,0:T(8,128)S(1)}) custom-call(bf16[2,336,128]{2,1,0:T(8,128)(2,1)S(1)} %collective-permute-done.8.a0, bf16[2,336,128]{2,1,0:T(8,128)(2,1)S(1)} %collective-permute-done.9.a1, bf16[2,336,128]{2,1,0:T(8,128)(2,1)S(1)} %collective-permute-done.10.b0, ...), custom_call_target="tpu_custom_call" | custom-call | flops 1073741824 | bytes 1048576 | tf_op jit(solution)/shard_map/pallas_call | solution.py:63
  41.3 1.5 %shard_map.96 = (bf16[512,256]{1,0:T(8,128)(2,1)}, bf16[512,128]{1,0:T(8,128)(2,1)}, f32[8,512]{1,0:T(8,128)}, f32[16,512]{1,0:T(8,128)S(1)}) custom-call(bf16[2,336,128]{2,1,0:T(8,128)(2,1)S(1)} %collective-permute-done.12.qc, bf16[2,336,128]{2,1,0:T(8,128)(2,1)S(1)} %collective-permute-done.13.qd, bf16[1024,256]{1,0:T(8,128)(2,1)S(1)} %get-tuple-element.58.kp, ...), custom_call_target="tpu_custom_call" | custom-call | flops 536870912 | bytes 1048576 | tf_op jit(solution)/shard_map/pallas_call | solution.py:63
  42.9 1.7 %collective-permute-start.14 = (f32[16,512]{1,0:T(8,128)S(1)}, f32[16,512]{1,0:T(8,128)S(1)}, u32[]{:S(2)}, u32[]{:S(2)}) collective-permute-start(f32[16,512]{1,0:T(8,128)S(1)} %get-tuple-element.70.refs_14_), channel_id=1, source_target_pairs={{0,48},{4,52},{8,56},{12,60},{16,0},{20,4},{24,8},{28,12},{32,16},... | collective-permute-start | bytes 98312 | tf_op jit(solution)/shard_map/ppermute | solution.py:38
  44.6 0.5 collective-permute-start.15
  45.0 0.5 collective-permute-start.16
  45.5 1.4 %collective-permute-done.14.refs_15_ = f32[16,512]{1,0:T(8,128)S(1)} collective-permute-done((f32[16,512]{1,0:T(8,128)S(1)}, f32[16,512]{1,0:T(8,128)S(1)}, u32[]{:S(2)}, u32[]{:S(2)}) %collective-permute-start.14) | collective-permute-done | bytes 32800 | tf_op jit(solution)/shard_map/ppermute | solution.py:38
  46.9 3.1 %collective-permute-done.15.refs_16_ = f32[16,512]{1,0:T(8,128)S(1)} collective-permute-done((f32[16,512]{1,0:T(8,128)S(1)}, f32[16,512]{1,0:T(8,128)S(1)}, u32[]{:S(2)}, u32[]{:S(2)}) %collective-permute-start.15) | collective-permute-done | bytes 32800 | tf_op jit(solution)/shard_map/ppermute | solution.py:38
  50.0 0.3 collective-permute-done.16.refs_17_
  50.3 9.9 %shard_map.97 = (bf16[768,128]{1,0:T(8,128)(2,1)S(1)}, bf16[768,128]{1,0:T(8,128)(2,1)S(1)}, bf16[768,128]{1,0:T(8,128)(2,1)S(1)}, bf16[768,128]{1,0:T(8,128)(2,...) custom-call(bf16[1024,256]{1,0:T(8,128)(2,1)} %get-tuple-element.51., ...), custom_call_target="tpu_custom_call" | custom-call | flops 6442450944 | bytes 1048576 | tf_op jit(solution)/shard_map/pallas_call | solution.py:63
  60.3 3.1 %collective-permute-start.24 = (bf16[640,128]{1,0:T(8,128)(2,1)S(1)}, bf16[640,128]{1,0:T(8,128)(2,1)S(1)}, u32[]{:S(2)}, u32[]{:S(2)}) collective-permute-start(bf16[640,128]{1,0:T(8,128)(2,1)S(1)} %get-tuple-element.81), channel_id=1, source_target_pairs={{0,8},{4,12},{8,0},{12,4},{16,24},{20,28},{24,16},{28,20},{32,40},... | collective-permute-start | bytes 491528 | tf_op jit(solution)/shard_map/ppermute | solution.py:38
  63.8 4.0 %all-to-all-start = ((bf16[8,128,128]{2,1,0:T(8,128)(2,1)}), bf16[8,128,128]{2,1,0:T(8,128)(2,1)S(1)}, u32[]{:S(2)}, u32[]{:S(2)}) async-start(bf16[8,128,128]{2,1,0:T(8,128)(2,1)} %get-tuple-element.85), calls=%async_computation | async-start | bytes 524288 | tf_op jit(solution)/shard_map/all_to_all | solution.py:424
  67.7 0.9 collective-permute-done.23.x1
  68.6 0.9 collective-permute-done.25.x3
  69.5 0.7 shard_map.100
  70.2 1.7 %collective-permute-start.26 = (bf16[576,128]{1,0:T(8,128)(2,1)S(1)}, bf16[576,128]{1,0:T(8,128)(2,1)S(1)}, u32[]{:S(2)}, u32[]{:S(2)}) collective-permute-start(bf16[576,128]{1,0:T(8,128)(2,1)S(1)} %get-tuple-element.84), channel_id=1, source_target_pairs={{0,64},{4,68},{8,72},{12,76},{16,80},{20,84},{24,88},{28,92},{32,9... | collective-permute-start | bytes 442376 | tf_op jit(solution)/shard_map/ppermute | solution.py:38
  71.9 3.1 %all-to-all-done.parts = bf16[8,128,128]{2,1,0:T(8,128)(2,1)S(1)} async-done(((bf16[8,128,128]{2,1,0:T(8,128)(2,1)}), bf16[8,128,128]{2,1,0:T(8,128)(2,1)S(1)}, u32[]{:S(2)}, u32[]{:S(2)}) %all-to-all-start) | async-done | bytes 262176 | tf_op jit(solution)/shard_map/all_to_all | solution.py:424
  74.9 1.1 shard_map.101
  76.0 5.4 %all-to-all-start.1 = ((bf16[32,128,128]{2,1,0:T(8,128)(2,1)}), bf16[32,128,128]{2,1,0:T(8,128)(2,1)S(1)}, u32[]{:S(2)}, u32[]{:S(2)}) async-start(bf16[32,128,128]{2,1,0:T(8,128)(2,1)} %shard_map.101), calls=%async_computation.1 | async-start | bytes 2097152 | tf_op jit(solution)/shard_map/all_to_all | solution.py:435
  81.6 1.9 %collective-permute-start.17 = (bf16[768,128]{1,0:T(8,128)(2,1)S(1)}, bf16[768,128]{1,0:T(8,128)(2,1)S(1)}, u32[]{:S(2)}, u32[]{:S(2)}) collective-permute-start(bf16[768,128]{1,0:T(8,128)(2,1)S(1)} %get-tuple-element.72), channel_id=1, source_target_pairs={{0,16},{4,20},{8,24},{12,28},{16,32},{20,36},{24,40},{28,44},{32,4... | collective-permute-start | bytes 589832 | tf_op jit(solution)/shard_map/ppermute | solution.py:38
  83.4 2.7 %collective-permute-start.18 = (bf16[768,128]{1,0:T(8,128)(2,1)S(1)}, bf16[768,128]{1,0:T(8,128)(2,1)S(1)}, u32[]{:S(2)}, u32[]{:S(2)}) collective-permute-start(bf16[768,128]{1,0:T(8,128)(2,1)S(1)} %get-tuple-element.73), channel_id=1, source_target_pairs={{0,32},{4,36},{8,40},{12,44},{16,48},{20,52},{24,56},{28,60},{32,0... | collective-permute-start | bytes 589832 | tf_op jit(solution)/shard_map/ppermute | solution.py:38
  86.1 1.5 %collective-permute-start.19 = (bf16[768,128]{1,0:T(8,128)(2,1)S(1)}, bf16[768,128]{1,0:T(8,128)(2,1)S(1)}, u32[]{:S(2)}, u32[]{:S(2)}) collective-permute-start(bf16[768,128]{1,0:T(8,128)(2,1)S(1)} %get-tuple-element.74), channel_id=1, source_target_pairs={{0,48},{4,52},{8,56},{12,60},{16,0},{20,4},{24,8},{28,12},{32,16},... | collective-permute-start | bytes 589832 | tf_op jit(solution)/shard_map/ppermute | solution.py:38
  87.6 3.0 %collective-permute-start.28 = (bf16[576,128]{1,0:T(8,128)(2,1)S(1)}, bf16[576,128]{1,0:T(8,128)(2,1)S(1)}, u32[]{:S(2)}, u32[]{:S(2)}) collective-permute-start(bf16[576,128]{1,0:T(8,128)(2,1)S(1)} %reduce-precision_convert_fusion), channel_id=1, source_target_pairs={{0,2},{1,3},{2,0},{3,1},{4,6},{5,7},{6,4},{7,5},{8,10},{9,11},{10,... | collective-permute-start | bytes 442376 | tf_op jit(solution)/shard_map/ppermute | solution.py:443
  90.6 11.1 %collective-permute-done.17.z1 = bf16[768,128]{1,0:T(8,128)(2,1)S(1)} collective-permute-done((bf16[768,128]{1,0:T(8,128)(2,1)S(1)}, bf16[768,128]{1,0:T(8,128)(2,1)S(1)}, u32[]{:S(2)}, u32[]{:S(2)}) %collective-permute-start.17) | collective-permute-done | bytes 196640 | tf_op jit(solution)/shard_map/ppermute | solution.py:38
  101.8 1.6 %collective-permute-start.20 = (bf16[192,128]{1,0:T(8,128)(2,1)S(1)}, bf16[192,128]{1,0:T(8,128)(2,1)S(1)}, u32[]{:S(2)}, u32[]{:S(2)}) collective-permute-start(bf16[192,128]{1,0:T(8,128)(2,1)S(1)} %get-tuple-element.76), channel_id=1, source_target_pairs={{0,12},{4,0},{8,4},{12,8},{16,28},{20,16},{24,20},{28,24},{32,44},... | collective-permute-start | bytes 147464 | tf_op jit(solution)/shard_map/ppermute | solution.py:38
  103.4 1.0 collective-permute-start.21
  104.4 0.8 collective-permute-start.22
  105.2 1.0 collective-permute-done.20.q1
  106.2 2.8 %collective-permute-done.21.q2 = bf16[192,128]{1,0:T(8,128)(2,1)S(1)} collective-permute-done((bf16[192,128]{1,0:T(8,128)(2,1)S(1)}, bf16[192,128]{1,0:T(8,128)(2,1)S(1)}, u32[]{:S(2)}, u32[]{:S(2)}) %collective-permute-start.21) | collective-permute-done | bytes 49184 | tf_op jit(solution)/shard_map/ppermute | solution.py:38
  109.0 0.7 collective-permute-done.22.q3
  109.7 0.9 shard_map.99
  110.6 0.7 add_bitcast_fusion
  111.3 1.5 %shard_map.102 = (f32[512,512]{1,0:T(8,128)}, f32[512,512]{1,0:T(8,128)}) custom-call(bf16[32,128,128]{2,1,0:T(8,128)(2,1)S(1)} %all-to-all-done.1.a), custom_call_target="tpu_custom_call" | custom-call | flops 1 | bytes 1048576 | tf_op jit(solution)/shard_map/pallas_call | solution.py:63
  (35 shorter events, 0.9 us)
Async XLA Ops:
  1.9 5.7 %collective-permute-start.3 = (bf16[592,128]{1,0:T(8,128)(2,1)S(1)}, bf16[592,128]{1,0:T(8,128)(2,1)S(1)}, u32[]{:S(2)}, u32[]{:S(2)}) collective-permute-start(bf16[592,128]{1,0:T(8,128)(2,1)S(1)} %get-tuple-element.50), channel_id=1, source_target_pairs={{0,64},{4,68},{8,72},{12,76},{16,80},{20,84},{24,88},{28,92},{32,9... | collective-permute-start | bytes 454664 | tf_op jit(solution)/shard_map/ppermute | solution.py:38
  7.6 17.7 %collective-permute-start.4 = (bf16[2,592,128]{2,1,0:T(8,128)(2,1)S(1)}, bf16[2,592,128]{2,1,0:T(8,128)(2,1)S(1)}, u32[]{:S(2)}, u32[]{:S(2)}) collective-permute-start(bf16[2,592,128]{2,1,0:T(8,128)(2,1)S(1)} %pad_maximum_fusion.pair), channel_id=1, source_target_pairs={{0,4},{1,13},{2,6},{3,15},{4,8},{5,1},{6,10},{7,3},{8,12},{9,5},{1... | collective-permute-start | bytes 909320 | tf_op jit(solution)/shard_map/ppermute | solution.py:49
  9.4 11.7 %collective-permute-start.1 = (bf16[336,128]{1,0:T(8,128)(2,1)S(1)}, bf16[336,128]{1,0:T(8,128)(2,1)S(1)}, u32[]{:S(2)}, u32[]{:S(2)}) collective-permute-start(bf16[336,128]{1,0:T(8,128)(2,1)S(1)} %get-tuple-element.48), channel_id=1, source_target_pairs={{0,8},{4,12},{8,0},{12,4},{16,24},{20,28},{24,16},{28,20},{32,40},... | collective-permute-start | bytes 258056 | tf_op jit(solution)/shard_map/ppermute | solution.py:38
  12.1 9.0 %collective-permute-start.2 = (bf16[336,128]{1,0:T(8,128)(2,1)S(1)}, bf16[336,128]{1,0:T(8,128)(2,1)S(1)}, u32[]{:S(2)}, u32[]{:S(2)}) collective-permute-start(bf16[336,128]{1,0:T(8,128)(2,1)S(1)} %get-tuple-element.49), channel_id=1, source_target_pairs={{0,12},{4,0},{8,4},{12,8},{16,28},{20,16},{24,20},{28,24},{32,44},... | collective-permute-start | bytes 258056 | tf_op jit(solution)/shard_map/ppermute | solution.py:38
  13.5 11.8 %collective-permute-start = (bf16[336,128]{1,0:T(8,128)(2,1)S(1)}, bf16[336,128]{1,0:T(8,128)(2,1)S(1)}, u32[]{:S(2)}, u32[]{:S(2)}) collective-permute-start(bf16[336,128]{1,0:T(8,128)(2,1)S(1)} %get-tuple-element.47), channel_id=1, source_target_pairs={{0,4},{4,8},{8,12},{12,0},{16,20},{20,24},{24,28},{28,16},{32,36},... | collective-permute-start | bytes 258056 | tf_op jit(solution)/shard_map/ppermute | solution.py:38
  14.1 21.8 %copy-start = (bf16[512,512]{1,0:T(8,128)(2,1)S(1)}, bf16[512,512]{1,0:T(8,128)(2,1)}, u32[]{:S(2)}) copy-start(bf16[512,512]{1,0:T(8,128)(2,1)} %ku.3) | copy-start | bytes 1572868
  14.1 21.8 %copy-start.1 = (bf16[512,512]{1,0:T(8,128)(2,1)S(1)}, bf16[512,512]{1,0:T(8,128)(2,1)}, u32[]{:S(2)}) copy-start(bf16[512,512]{1,0:T(8,128)(2,1)} %vu.3) | copy-start | bytes 1572868
  14.2 11.2 %collective-permute-start.6 = (bf16[592,128]{1,0:T(8,128)(2,1)S(1)}, bf16[592,128]{1,0:T(8,128)(2,1)S(1)}, u32[]{:S(2)}, u32[]{:S(2)}) collective-permute-start(bf16[592,128]{1,0:T(8,128)(2,1)S(1)} %fusion.1), channel_id=1, source_target_pairs={{0,8},{1,9},{2,10},{3,11},{4,12},{5,13},{6,14},{7,15},{8,0},{9,1},... | collective-permute-start | bytes 454664 | tf_op jit(solution)/shard_map/ppermute | solution.py:49
  21.1 7.1 %collective-permute-start.11 = (bf16[2,336,128]{2,1,0:T(8,128)(2,1)S(1)}, bf16[2,336,128]{2,1,0:T(8,128)(2,1)S(1)}, u32[]{:S(2)}, u32[]{:S(2)}) collective-permute-start(bf16[2,336,128]{2,1,0:T(8,128)(2,1)S(1)} %pad_maximum_fusion.2.q1), channel_id=1, source_target_pairs={{0,48},{4,52},{8,56},{12,60},{16,0},{20,4},{24,8},{28,12},{32,16},... | collective-permute-start | bytes 516104 | tf_op jit(solution)/shard_map/ppermute | solution.py:38
  25.3 10.6 %collective-permute-start.5 = (bf16[2,592,128]{2,1,0:T(8,128)(2,1)S(1)}, bf16[2,592,128]{2,1,0:T(8,128)(2,1)S(1)}, u32[]{:S(2)}, u32[]{:S(2)}) collective-permute-start(bf16[2,592,128]{2,1,0:T(8,128)(2,1)S(1)} %collective-permute-done.4.lp), channel_id=1, source_target_pairs={{0,1},{1,0},{2,3},{3,2},{4,5},{5,4},{6,7},{7,6},{8,9},{9,8},{10,11... | collective-permute-start | bytes 909320 | tf_op jit(solution)/shard_map/ppermute | solution.py:53
  25.3 8.5 %collective-permute-start.8 = (bf16[2,336,128]{2,1,0:T(8,128)(2,1)S(1)}, bf16[2,336,128]{2,1,0:T(8,128)(2,1)S(1)}, u32[]{:S(2)}, u32[]{:S(2)}) collective-permute-start(bf16[2,336,128]{2,1,0:T(8,128)(2,1)S(1)} %pad_maximum_fusion.1.q0), channel_id=1, source_target_pairs={{0,16},{4,20},{8,24},{12,28},{16,32},{20,36},{24,40},{28,44},{32,4... | collective-permute-start | bytes 516104 | tf_op jit(solution)/shard_map/ppermute | solution.py:38
  25.4 8.4 %collective-permute-start.7 = (bf16[592,128]{1,0:T(8,128)(2,1)S(1)}, bf16[592,128]{1,0:T(8,128)(2,1)S(1)}, u32[]{:S(2)}, u32[]{:S(2)}) collective-permute-start(bf16[592,128]{1,0:T(8,128)(2,1)S(1)} %collective-permute-done.6.lh), channel_id=1, source_target_pairs={{0,1},{1,0},{2,3},{3,2},{4,5},{5,4},{6,7},{7,6},{8,9},{9,8},{10,11... | collective-permute-start | bytes 454664 | tf_op jit(solution)/shard_map/ppermute | solution.py:53
  26.0 12.3 %collective-permute-start.9 = (bf16[2,336,128]{2,1,0:T(8,128)(2,1)S(1)}, bf16[2,336,128]{2,1,0:T(8,128)(2,1)S(1)}, u32[]{:S(2)}, u32[]{:S(2)}) collective-permute-start(bf16[2,336,128]{2,1,0:T(8,128)(2,1)S(1)} %pad_maximum_fusion.2.q1), channel_id=1, source_target_pairs={{0,16},{4,20},{8,24},{12,28},{16,32},{20,36},{24,40},{28,44},{32,4... | collective-permute-start | bytes 516104 | tf_op jit(solution)/shard_map/ppermute | solution.py:38
  28.2 10.1 %collective-permute-start.10 = (bf16[2,336,128]{2,1,0:T(8,128)(2,1)S(1)}, bf16[2,336,128]{2,1,0:T(8,128)(2,1)S(1)}, u32[]{:S(2)}, u32[]{:S(2)}) collective-permute-start(bf16[2,336,128]{2,1,0:T(8,128)(2,1)S(1)} %pad_maximum_fusion.1.q0), channel_id=1, source_target_pairs={{0,48},{4,52},{8,56},{12,60},{16,0},{20,4},{24,8},{28,12},{32,16},... | collective-permute-start | bytes 516104 | tf_op jit(solution)/shard_map/ppermute | solution.py:38
  33.9 7.4 %collective-permute-start.13 = (bf16[2,336,128]{2,1,0:T(8,128)(2,1)S(1)}, bf16[2,336,128]{2,1,0:T(8,128)(2,1)S(1)}, u32[]{:S(2)}, u32[]{:S(2)}) collective-permute-start(bf16[2,336,128]{2,1,0:T(8,128)(2,1)S(1)} %collective-permute-done.11.b1), channel_id=1, source_target_pairs={{0,48},{4,52},{8,56},{12,60},{16,0},{20,4},{24,8},{28,12},{32,16},... | collective-permute-start | bytes 516104 | tf_op jit(solution)/shard_map/ppermute | solution.py:38
  33.9 7.4 %collective-permute-start.12 = (bf16[2,336,128]{2,1,0:T(8,128)(2,1)S(1)}, bf16[2,336,128]{2,1,0:T(8,128)(2,1)S(1)}, u32[]{:S(2)}, u32[]{:S(2)}) collective-permute-start(bf16[2,336,128]{2,1,0:T(8,128)(2,1)S(1)} %collective-permute-done.8.a0), channel_id=1, source_target_pairs={{0,16},{4,20},{8,24},{12,28},{16,32},{20,36},{24,40},{28,44},{32,4... | collective-permute-start | bytes 516104 | tf_op jit(solution)/shard_map/ppermute | solution.py:38
  42.9 4.0 %collective-permute-start.14 = (f32[16,512]{1,0:T(8,128)S(1)}, f32[16,512]{1,0:T(8,128)S(1)}, u32[]{:S(2)}, u32[]{:S(2)}) collective-permute-start(f32[16,512]{1,0:T(8,128)S(1)} %get-tuple-element.70.refs_14_), channel_id=1, source_target_pairs={{0,48},{4,52},{8,56},{12,60},{16,0},{20,4},{24,8},{28,12},{32,16},... | collective-permute-start | bytes 98312 | tf_op jit(solution)/shard_map/ppermute | solution.py:38
  44.6 5.4 %collective-permute-start.15 = (f32[16,512]{1,0:T(8,128)S(1)}, f32[16,512]{1,0:T(8,128)S(1)}, u32[]{:S(2)}, u32[]{:S(2)}) collective-permute-start(f32[16,512]{1,0:T(8,128)S(1)} %get-tuple-element.70.refs_14_), channel_id=1, source_target_pairs={{0,32},{4,36},{8,40},{12,44},{16,48},{20,52},{24,56},{28,60},{32,0... | collective-permute-start | bytes 98312 | tf_op jit(solution)/shard_map/ppermute | solution.py:38
  45.0 5.3 %collective-permute-start.16 = (f32[16,512]{1,0:T(8,128)S(1)}, f32[16,512]{1,0:T(8,128)S(1)}, u32[]{:S(2)}, u32[]{:S(2)}) collective-permute-start(f32[16,512]{1,0:T(8,128)S(1)} %get-tuple-element.70.refs_14_), channel_id=1, source_target_pairs={{0,16},{4,20},{8,24},{12,28},{16,32},{20,36},{24,40},{28,44},{32,4... | collective-permute-start | bytes 98312 | tf_op jit(solution)/shard_map/ppermute | solution.py:38
  60.3 8.4 %collective-permute-start.23 = (bf16[640,128]{1,0:T(8,128)(2,1)S(1)}, bf16[640,128]{1,0:T(8,128)(2,1)S(1)}, u32[]{:S(2)}, u32[]{:S(2)}) collective-permute-start(bf16[640,128]{1,0:T(8,128)(2,1)S(1)} %get-tuple-element.80), channel_id=1, source_target_pairs={{0,4},{4,8},{8,12},{12,0},{16,20},{20,24},{24,28},{28,16},{32,36},... | collective-permute-start | bytes 491528 | tf_op jit(solution)/shard_map/ppermute | solution.py:38
  60.3 8.3 %collective-permute-start.24 = (bf16[640,128]{1,0:T(8,128)(2,1)S(1)}, bf16[640,128]{1,0:T(8,128)(2,1)S(1)}, u32[]{:S(2)}, u32[]{:S(2)}) collective-permute-start(bf16[640,128]{1,0:T(8,128)(2,1)S(1)} %get-tuple-element.81), channel_id=1, source_target_pairs={{0,8},{4,12},{8,0},{12,4},{16,24},{20,28},{24,16},{28,20},{32,40},... | collective-permute-start | bytes 491528 | tf_op jit(solution)/shard_map/ppermute | solution.py:38
  63.4 6.1 %collective-permute-start.25 = (bf16[640,128]{1,0:T(8,128)(2,1)S(1)}, bf16[640,128]{1,0:T(8,128)(2,1)S(1)}, u32[]{:S(2)}, u32[]{:S(2)}) collective-permute-start(bf16[640,128]{1,0:T(8,128)(2,1)S(1)} %get-tuple-element.82), channel_id=1, source_target_pairs={{0,12},{4,0},{8,4},{12,8},{16,28},{20,16},{24,20},{28,24},{32,44},... | collective-permute-start | bytes 491528 | tf_op jit(solution)/shard_map/ppermute | solution.py:38
  63.8 11.2 %all-to-all-start = ((bf16[8,128,128]{2,1,0:T(8,128)(2,1)}), bf16[8,128,128]{2,1,0:T(8,128)(2,1)S(1)}, u32[]{:S(2)}, u32[]{:S(2)}) async-start(bf16[8,128,128]{2,1,0:T(8,128)(2,1)} %get-tuple-element.85), calls=%async_computation | async-start | bytes 524288 | tf_op jit(solution)/shard_map/all_to_all | solution.py:424
  70.2 11.2 %collective-permute-start.26 = (bf16[576,128]{1,0:T(8,128)(2,1)S(1)}, bf16[576,128]{1,0:T(8,128)(2,1)S(1)}, u32[]{:S(2)}, u32[]{:S(2)}) collective-permute-start(bf16[576,128]{1,0:T(8,128)(2,1)S(1)} %get-tuple-element.84), channel_id=1, source_target_pairs={{0,64},{4,68},{8,72},{12,76},{16,80},{20,84},{24,88},{28,92},{32,9... | collective-permute-start | bytes 442376 | tf_op jit(solution)/shard_map/ppermute | solution.py:38
  76.0 35.3 %all-to-all-start.1 = ((bf16[32,128,128]{2,1,0:T(8,128)(2,1)}), bf16[32,128,128]{2,1,0:T(8,128)(2,1)S(1)}, u32[]{:S(2)}, u32[]{:S(2)}) async-start(bf16[32,128,128]{2,1,0:T(8,128)(2,1)} %shard_map.101), calls=%async_computation.1 | async-start | bytes 2097152 | tf_op jit(solution)/shard_map/all_to_all | solution.py:435
  81.5 6.1 %collective-permute-start.27 = (bf16[576,128]{1,0:T(8,128)(2,1)S(1)}, bf16[576,128]{1,0:T(8,128)(2,1)S(1)}, u32[]{:S(2)}, u32[]{:S(2)}) collective-permute-start(bf16[576,128]{1,0:T(8,128)(2,1)S(1)} %reduce-precision_convert_fusion.1), channel_id=1, source_target_pairs={{0,1},{1,0},{2,3},{3,2},{4,5},{5,4},{6,7},{7,6},{8,9},{9,8},{10,11... | collective-permute-start | bytes 442376 | tf_op jit(solution)/shard_map/ppermute | solution.py:53
  81.6 20.1 %collective-permute-start.17 = (bf16[768,128]{1,0:T(8,128)(2,1)S(1)}, bf16[768,128]{1,0:T(8,128)(2,1)S(1)}, u32[]{:S(2)}, u32[]{:S(2)}) collective-permute-start(bf16[768,128]{1,0:T(8,128)(2,1)S(1)} %get-tuple-element.72), channel_id=1, source_target_pairs={{0,16},{4,20},{8,24},{12,28},{16,32},{20,36},{24,40},{28,44},{32,4... | collective-permute-start | bytes 589832 | tf_op jit(solution)/shard_map/ppermute | solution.py:38
  83.4 18.2 %collective-permute-start.18 = (bf16[768,128]{1,0:T(8,128)(2,1)S(1)}, bf16[768,128]{1,0:T(8,128)(2,1)S(1)}, u32[]{:S(2)}, u32[]{:S(2)}) collective-permute-start(bf16[768,128]{1,0:T(8,128)(2,1)S(1)} %get-tuple-element.73), channel_id=1, source_target_pairs={{0,32},{4,36},{8,40},{12,44},{16,48},{20,52},{24,56},{28,60},{32,0... | collective-permute-start | bytes 589832 | tf_op jit(solution)/shard_map/ppermute | solution.py:38
  86.1 15.6 %collective-permute-start.19 = (bf16[768,128]{1,0:T(8,128)(2,1)S(1)}, bf16[768,128]{1,0:T(8,128)(2,1)S(1)}, u32[]{:S(2)}, u32[]{:S(2)}) collective-permute-start(bf16[768,128]{1,0:T(8,128)(2,1)S(1)} %get-tuple-element.74), channel_id=1, source_target_pairs={{0,48},{4,52},{8,56},{12,60},{16,0},{20,4},{24,8},{28,12},{32,16},... | collective-permute-start | bytes 589832 | tf_op jit(solution)/shard_map/ppermute | solution.py:38
  87.6 23.0 %collective-permute-start.28 = (bf16[576,128]{1,0:T(8,128)(2,1)S(1)}, bf16[576,128]{1,0:T(8,128)(2,1)S(1)}, u32[]{:S(2)}, u32[]{:S(2)}) collective-permute-start(bf16[576,128]{1,0:T(8,128)(2,1)S(1)} %reduce-precision_convert_fusion), channel_id=1, source_target_pairs={{0,2},{1,3},{2,0},{3,1},{4,6},{5,7},{6,4},{7,5},{8,10},{9,11},{10,... | collective-permute-start | bytes 442376 | tf_op jit(solution)/shard_map/ppermute | solution.py:443
  101.8 4.4 %collective-permute-start.20 = (bf16[192,128]{1,0:T(8,128)(2,1)S(1)}, bf16[192,128]{1,0:T(8,128)(2,1)S(1)}, u32[]{:S(2)}, u32[]{:S(2)}) collective-permute-start(bf16[192,128]{1,0:T(8,128)(2,1)S(1)} %get-tuple-element.76), channel_id=1, source_target_pairs={{0,12},{4,0},{8,4},{12,8},{16,28},{20,16},{24,20},{28,24},{32,44},... | collective-permute-start | bytes 147464 | tf_op jit(solution)/shard_map/ppermute | solution.py:38
  103.4 5.6 %collective-permute-start.21 = (bf16[192,128]{1,0:T(8,128)(2,1)S(1)}, bf16[192,128]{1,0:T(8,128)(2,1)S(1)}, u32[]{:S(2)}, u32[]{:S(2)}) collective-permute-start(bf16[192,128]{1,0:T(8,128)(2,1)S(1)} %get-tuple-element.77), channel_id=1, source_target_pairs={{0,8},{4,12},{8,0},{12,4},{16,24},{20,28},{24,16},{28,20},{32,40},... | collective-permute-start | bytes 147464 | tf_op jit(solution)/shard_map/ppermute | solution.py:38
  104.4 5.3 %collective-permute-start.22 = (bf16[192,128]{1,0:T(8,128)(2,1)S(1)}, bf16[192,128]{1,0:T(8,128)(2,1)S(1)}, u32[]{:S(2)}, u32[]{:S(2)}) collective-permute-start(bf16[192,128]{1,0:T(8,128)(2,1)S(1)} %get-tuple-element.78), channel_id=1, source_target_pairs={{0,4},{4,8},{8,12},{12,0},{16,20},{20,24},{24,28},{28,16},{32,36},... | collective-permute-start | bytes 147464 | tf_op jit(solution)/shard_map/ppermute | solution.py:38
